TPU v7x, 32 devices: a whole 2x2x4 slice. The times are simulated.
32 devices in a mesh: lat: 8 (over z, x), lon: 4 (over y, core).
Axes of the slice: x: 2, y: 2, z: 4, core: 2. Of those that a mesh axis runs over, the one named last changes fastest.
Arguments:
- state: bfloat16 [2, 48, 96, 192], P(None, 'lat', 'lon'), may hold values from -6 to 6
- out_cot: bfloat16 [2, 48, 96, 192], P(None, 'lat', 'lon'), may hold values from -6 to 6
- qkv_weight: bfloat16 [2, 192, 576], replicated, may hold values from -0.4375 to 0.4375
- proj_weight: bfloat16 [2, 192, 192], replicated, may hold values from -0.4375 to 0.4375
- fc1_weight: bfloat16 [2, 192, 768], replicated, may hold values from -0.4375 to 0.4375
- fc2_weight: bfloat16 [2, 768, 192], replicated, may hold values from -0.21875 to 0.21875
- norm_gain: float32 [2, 2, 192], replicated, may hold values from 0.5 to 1.5
- bias_table: float32 [2, 8, 1, 6, 3312], P(None, 'lat'), may hold values from -3 to 303
Outputs:
- state_grad: float32 [2, 48, 96, 192], P(None, 'lat', 'lon')
- qkv_grad: float32 [2, 192, 576], P(None, 'lat', 'lon')
- proj_grad: float32 [2, 192, 192], P(None, 'lat', 'lon')
- fc1_grad: float32 [2, 192, 768], P(None, 'lat', 'lon')
- fc2_grad: float32 [2, 768, 192], P(None, 'lat', 'lon')
- norm_gain_grad: float32 [2, 2, 192], replicated
- bias_table_grad: float32 [2, 8, 1, 6, 3312], P(None, 'lat', None, None, 'lon')
All inputs are finite; a program needn't handle non-finite values.
Results may differ from a plain program's by a relative error of at most 0.028.
Values may be sent and summed in bfloat16 or wider, within the bound.
No kernel may reach another device: no remote copies, remote signals or barrier semaphores. Data moves between devices by JAX's collectives and lax.ppermute only.
A program may use at most 128 MiB of HBM per device.

v0:
```python
import jax
import jax.numpy as jnp
from jax import lax
from jax.sharding import PartitionSpec as P

WZ = 2
WH = 6
WW = 12


def from_behind(value, axis, steps):
    count = lax.axis_size(axis)
    pairs = [(source, (source + steps) % count) for source in range(count)]
    return lax.ppermute(value, axis, pairs)


def as_sent(array):

    def short(part):
        return part.astype(jnp.bfloat16) if part.dtype == jnp.float32 else part

    return jax.tree.map(short, array)


def position_index():
    tokens = jnp.arange(WZ * WH * WW, dtype=jnp.int32)
    level_in = tokens // (WH * WW)
    row_in = tokens // WW % WH
    column_in = tokens % WW
    level_part = (level_in[:, None] * WZ + level_in[None, :]) * (WH * WH * (2 * WW - 1))
    row_part = (row_in[:, None] * WH + row_in[None, :]) * (2 * WW - 1)
    return level_part + row_part + column_in[:, None] - column_in[None, :] + WW - 1


def shifted_labels(lat_windows, level_windows, lat_start, lat_total):
    tokens = jnp.arange(WZ * WH * WW, dtype=jnp.int32)
    level_in = tokens // (WH * WW)
    row_in = tokens // WW % WH
    global_level = (
        jnp.arange(level_windows, dtype=jnp.int32)[None, :, None] * WZ + level_in[None, None, :]
    )
    global_row = (
        lat_start
        + jnp.arange(lat_windows, dtype=jnp.int32)[:, None, None] * WH
        + row_in[None, None, :]
    )
    level_mark = (global_level >= level_windows * WZ - 1).astype(jnp.int32)
    row_mark = (global_row >= lat_total - WH // 2).astype(jnp.int32)
    return 2 * level_mark + row_mark


def to_windows(brick):
    levels, rows, columns, model_width = brick.shape
    shaped = brick.reshape(levels // WZ, WZ, rows // WH, WH, columns // WW, WW, model_width)
    shaped = shaped.transpose(2, 0, 4, 1, 3, 5, 6)
    return shaped.reshape(rows // WH, levels // WZ, columns // WW, WZ * WH * WW, model_width)


def from_windows(windows):
    lat_windows, level_windows, lon_windows, window_size, model_width = windows.shape
    shaped = windows.reshape(lat_windows, level_windows, lon_windows, WZ, WH, WW, model_width)
    shaped = shaped.transpose(1, 3, 0, 4, 2, 5, 6)
    return shaped.reshape(level_windows * WZ, lat_windows * WH, lon_windows * WW, model_width)


def layer_norm(values, gain):
    average = jnp.mean(values, -1, keepdims=True)
    centred = values - average
    variance = jnp.mean(centred * centred, -1, keepdims=True)
    return centred * lax.rsqrt(variance + 1e-05) * gain


def rounded(values):
    return lax.optimization_barrier(values.astype(jnp.bfloat16)).astype(jnp.float32)


def run_block(values, gain_pair, table_part, offsets, labels, weights):
    w_qkv, w_proj, w_fc1, w_fc2 = weights
    head_count = table_part.shape[2]
    model_width = values.shape[-1]
    head_size = model_width // head_count
    normed = layer_norm(values, gain_pair[0]).astype(jnp.bfloat16)
    qkv_out = jnp.dot(normed, w_qkv, preferred_element_type=jnp.float32) + offsets[0]
    projected = rounded(qkv_out).reshape(values.shape[:-1] + (3, head_count, head_size))
    queries = projected[..., 0, :, :]
    key_vectors = projected[..., 1, :, :]
    value_vectors = projected[..., 2, :, :]
    scores = jnp.einsum("abcqhd,abckhd->abchqk", queries, key_vectors) * head_size ** (-0.5)
    bias_full = jnp.take(table_part, position_index(), axis=3)
    allowed = (labels[:, :, :, None] == labels[:, :, None, :])[:, :, None, None]
    scores = jnp.where(allowed, scores + bias_full[:, :, None], -1e30)
    attention = rounded(jax.nn.softmax(scores, axis=-1))
    attended = jnp.einsum("abchqk,abckhd->abcqhd", attention, value_vectors).reshape(values.shape)
    joined = attended.astype(jnp.bfloat16)
    middle = values + jnp.dot(joined, w_proj, preferred_element_type=jnp.float32) + offsets[1]
    normed_two = layer_norm(middle, gain_pair[1]).astype(jnp.bfloat16)
    expanded = jnp.dot(normed_two, w_fc1, preferred_element_type=jnp.float32) + offsets[2]
    hidden = jax.nn.gelu(expanded, approximate=False).astype(jnp.bfloat16)
    result = middle + jnp.dot(hidden, w_fc2, preferred_element_type=jnp.float32) + offsets[3]
    return (result, (normed, joined, normed_two, hidden))


def open_block(values, gain_pair, table_part, labels, weights):
    lead = values.shape[:-1]
    model_width = values.shape[-1]
    offsets = (
        jnp.zeros(lead + (3 * model_width,), jnp.float32),
        jnp.zeros(lead + (model_width,), jnp.float32),
        jnp.zeros(lead + (weights[2].shape[1],), jnp.float32),
        jnp.zeros(lead + (model_width,), jnp.float32),
    )

    def forward(inputs, gains_in, table_in, offsets_in):
        return run_block(inputs, gains_in, table_in, offsets_in, labels, weights)

    return jax.vjp(forward, values, gain_pair, table_part, offsets, has_aux=True)


def close_block(pullback, stored, cotangent):
    value_grad, gain_grad, table_grad, output_grads = pullback(cotangent)
    weight_grads = tuple(
        (
            lax.dot_general(
                inputs_act.reshape(-1, inputs_act.shape[-1]),
                grad_out.reshape(-1, grad_out.shape[-1]).astype(jnp.bfloat16),
                (((0,), (0,)), ((), ())),
                preferred_element_type=jnp.float32,
            )
            for inputs_act, grad_out in zip(stored, output_grads)
        )
    )
    return (value_grad, weight_grads, gain_grad, table_grad)


def body(state, out_cot, qkv_weight, proj_weight, fc1_weight, fc2_weight, norm_gain, bias_table):
    matrices = (qkv_weight, proj_weight, fc1_weight, fc2_weight)
    first_weights = tuple((w[0] for w in matrices))
    second_weights = tuple((w[1] for w in matrices))
    half_lat = WH // 2
    half_lon = WW // 2
    lat_rows = state.shape[1]
    lat_windows = lat_rows // WH
    level_windows = state.shape[0] // WZ
    windows_in = to_windows(state.astype(jnp.float32))
    unmasked = jnp.zeros((lat_windows, level_windows, WZ * WH * WW), jnp.int32)
    first_out, first_pull, first_inputs = open_block(
        windows_in, norm_gain[0], bias_table[0], unmasked, first_weights
    )
    state_one = from_windows(first_out).astype(jnp.bfloat16)
    paired = jnp.stack((state_one, out_cot))
    arrived = from_behind(paired[:, :, :half_lat], "lat", -1)
    paired = jnp.concatenate((paired[:, :, half_lat:], arrived), 2)
    arrived = from_behind(paired[:, :, :, :half_lon], "lon", -1)
    paired = jnp.roll(jnp.concatenate((paired[:, :, :, half_lon:], arrived), 3), -(WZ // 2), 1)
    rolled = paired[0]
    cot_rolled = paired[1]
    lat_start = lax.axis_index("lat") * lat_rows
    lat_total = lat_rows * lax.axis_size("lat")
    shifted = shifted_labels(lat_windows, level_windows, lat_start, lat_total)
    both_windows = to_windows(jnp.concatenate((rolled, cot_rolled), 3).astype(jnp.float32))
    model_width = state.shape[-1]
    second_out, second_pull, second_inputs = open_block(
        both_windows[..., :model_width], norm_gain[1], bias_table[1], shifted, second_weights
    )
    rolled_grad, second_grads, second_gains, second_table = close_block(
        second_pull, second_inputs, both_windows[..., model_width:]
    )
    returned = jnp.roll(from_windows(rolled_grad), WZ // 2, 0)
    arrived = from_behind(as_sent(returned[:, :, -half_lon:]), "lon", 1)
    returned = jnp.concatenate((arrived, returned[:, :, :-half_lon]), 2)
    arrived = from_behind(as_sent(returned[:, -half_lat:]), "lat", 1)
    returned = jnp.concatenate((arrived, returned[:, :-half_lat]), 1)
    state_grad, first_grads, first_gains, first_table = close_block(
        first_pull, first_inputs, to_windows(returned)
    )
    stacked = tuple((jnp.stack((left, right)) for left, right in zip(first_grads, second_grads)))
    partial_sums = (
        lax.psum_scatter(
            stacked[0].astype(jnp.bfloat16), "lat", scatter_dimension=1, tiled=True
        ).astype(jnp.float32),
        lax.psum_scatter(
            stacked[1].astype(jnp.bfloat16), "lat", scatter_dimension=1, tiled=True
        ).astype(jnp.float32),
        lax.psum_scatter(
            stacked[2].astype(jnp.bfloat16), "lat", scatter_dimension=1, tiled=True
        ).astype(jnp.float32),
        lax.psum_scatter(
            stacked[3].astype(jnp.bfloat16), "lat", scatter_dimension=1, tiled=True
        ).astype(jnp.float32),
    )
    summed = (
        lax.psum_scatter(
            partial_sums[0].astype(jnp.bfloat16), "lon", scatter_dimension=2, tiled=True
        ).astype(jnp.float32),
        lax.psum_scatter(
            partial_sums[1].astype(jnp.bfloat16), "lon", scatter_dimension=2, tiled=True
        ).astype(jnp.float32),
        lax.psum_scatter(
            partial_sums[2].astype(jnp.bfloat16), "lon", scatter_dimension=2, tiled=True
        ).astype(jnp.float32),
        lax.psum_scatter(
            partial_sums[3].astype(jnp.bfloat16), "lon", scatter_dimension=2, tiled=True
        ).astype(jnp.float32),
    )
    table_grad = lax.psum_scatter(
        jnp.stack((first_table, second_table)).astype(jnp.bfloat16),
        "lon",
        scatter_dimension=4,
        tiled=True,
    ).astype(jnp.float32)
    gain_grad = lax.psum(jnp.stack((first_gains, second_gains)), ("lat", "lon"))
    return (
        from_windows(state_grad),
        summed[0],
        summed[1],
        summed[2],
        summed[3],
        gain_grad,
        table_grad,
    )


def solution(mesh):
    in_specs = (
        P(None, "lat", "lon", None),
        P(None, "lat", "lon", None),
        P(),
        P(),
        P(),
        P(),
        P(),
        P(None, "lat", None, None, None),
    )
    out_specs = (
        P(None, "lat", "lon", None),
        P(None, "lat", "lon"),
        P(None, "lat", "lon"),
        P(None, "lat", "lon"),
        P(None, "lat", "lon"),
        P(),
        P(None, "lat", None, None, "lon"),
    )
    return jax.shard_map(body, mesh=mesh, in_specs=in_specs, out_specs=out_specs, check_vma=False)
```

profile of v0, /device:TPU:0, one launch (start us, length us, event | category | flops | bytes accessed | tf_op | source)
XLA Modules:
  0.0 669.4 jit_solution(4049416523696214050)
XLA Ops:
  20.8 39.1 %gather_fusion = f32[20736,6]{1,0:T(8,128)} fusion(f32[6,3312]{0,1:T(8,128)S(1)} %bitcast.488, s32[21504]{0:T(1024)S(1)} %pad_clamp_fusion), kind=kCustom, calls=%fused_computation.clone | custom fusion | bytes 1078272 | tf_op jit(solution)/shard_map/jvp(jit(_take))/gather | solution.py:89
  59.9 11.6 %copy.312 = f32[144,144,6]{0,1,2:T(8,128)S(1)} copy(f32[144,144,6]{2,1,0:T(8,128)} %bitcast.490) | data formatting | bytes 995328 | tf_op jit(solution)/shard_map/jvp(jit(_take))/gather | solution.py:89
  71.5 38.8 %gather_fusion.1 = f32[20736,6]{1,0:T(8,128)} fusion(f32[6,3312]{0,1:T(8,128)S(1)} %bitcast.487, s32[21504]{0:T(1024)S(1)} %pad_clamp_fusion), kind=kCustom, calls=%fused_computation.1.clone | custom fusion | bytes 1078272 | tf_op jit(solution)/shard_map/jvp(jit(_take))/gather | solution.py:89
  110.3 11.6 %copy.327 = f32[144,144,6]{0,1,2:T(8,128)S(1)} copy(f32[144,144,6]{2,1,0:T(8,128)} %bitcast.489) | data formatting | bytes 995328 | tf_op jit(solution)/shard_map/jvp(jit(_take))/gather | solution.py:89
  123.3 1.9 fusion.191
  128.1 2.9 multiply_convert_fusion.1
  132.9 6.1 collective-permute-start
  154.3 3.4 fusion.193
  161.4 1.9 fusion.61
  183.0 6.2 collective-permute-done.3
  207.5 1.8 pad_maximum_fusion.3
  209.4 3.7 fusion.177
  217.8 10.4 %copy.385 = f32[144,144,6]{2,1,0:T(8,128)} copy(f32[144,144,6]{0,1,2:T(8,128)S(1)} %bitcast.507) | data formatting | bytes 995328 | tf_op jit(solution)/shard_map/transpose(jvp())/broadcast_in_dim | solution.py:91
  228.3 10.5 %copy.384 = f32[144,144,6]{2,1,0:T(8,128)} copy(f32[144,144,6]{0,1,2:T(8,128)S(1)} %bitcast.506) | data formatting | bytes 995328 | tf_op jit(solution)/shard_map/transpose(jvp())/broadcast_in_dim | solution.py:91
  238.7 112.8 %scatter_custom_fusion.1 = f32[6,3312]{0,1:T(8,128)S(1)} fusion(s32[20736]{0:T(1024)} %reshape.1221, f32[20736,6]{1,0:T(8,128)} %bitcast.492, f32[]{:T(128)} %constant.77.clone.1), kind=kCustom, calls=%fused_computation.153 | custom fusion | flops 124416 | bytes 80000 | tf_op jit(solution)/shard_map/transpose(jvp(jit(_take)))/scatter-add | solution.py:89
  351.6 112.8 %scatter_custom_fusion = f32[6,3312]{0,1:T(8,128)S(1)} fusion(s32[20736]{0:T(1024)} %reshape.1221, f32[20736,6]{1,0:T(8,128)} %bitcast.491, f32[]{:T(128)} %constant.77.clone.1), kind=kCustom, calls=%fused_computation.155 | custom fusion | flops 124416 | bytes 80000 | tf_op jit(solution)/shard_map/transpose(jvp(jit(_take)))/scatter-add | solution.py:89
  467.0 13.0 %copy.366 = bf16[2,1,1,6,3312]{3,0,2,1,4:T(2,128)(2,1)} copy(bf16[2,1,1,6,3312]{3,4,2,1,0:T(8,128)(2,1)S(1)} %pad_maximum_fusion) | data formatting | bytes 158976 | tf_op jit(solution)/shard_map/stack | solution.py:206
  487.3 37.5 %reduce-scatter.29.cloned.1.call-done = bf16[96,384]{1,0:T(8,128)(2,1)} async-done(((bf16[768,384]{1,0:T(8,128)(2,1)}), bf16[96,384]{1,0:T(8,128)(2,1)}) %reduce-scatter.29.cloned.1.call-update) | async-done | bytes 73744
  527.9 40.9 %psum.7 = f32[2,2,192]{2,1,0:T(2,128)} all-reduce(f32[2,2,192]{2,1,0:T(2,128)S(1)} %pad_maximum_fusion.10), channel_id=1, replica_groups=mesh['lat'=8,'lon'=4] {'lat','lon'}, use_global_device_ids=true, to_apply=%region_34.36 | all-reduce | flops 768 | bytes 6144 | tf_op jit(solution)/shard_map/psum | solution.py:211
  568.8 3.4 all-reduce.17.cloned.1.call-done
  575.2 19.4 %reduce-scatter.23.cloned.1.call-done = bf16[48,48]{1,0:T(8,128)(2,1)} async-done(((bf16[192,48]{1,0:T(8,128)(2,1)}), bf16[48,48]{1,0:T(8,128)(2,1)}) %reduce-scatter.23.cloned.1.call-update) | async-done | bytes 4624
  596.1 20.5 %reduce-scatter.21.cloned.1.call-done = bf16[144,48]{1,0:T(8,128)(2,1)} async-done(((bf16[576,48]{1,0:T(8,128)(2,1)}), bf16[144,48]{1,0:T(8,128)(2,1)}) %reduce-scatter.21.cloned.1.call-update) | async-done | bytes 13840
  618.2 20.7 %reduce-scatter.27.cloned.1.call-done = bf16[192,48]{1,0:T(8,128)(2,1)} async-done(((bf16[768,48]{1,0:T(8,128)(2,1)}), bf16[192,48]{1,0:T(8,128)(2,1)}) %reduce-scatter.27.cloned.1.call-update) | async-done | bytes 18448
  640.5 20.4 %reduce-scatter.19.cloned.1.call-done = bf16[2,96,48]{1,2,0:T(8,128)(2,1)} async-done(((bf16[2,96,192]{1,2,0:T(8,128)(2,1)}), bf16[2,96,48]{1,2,0:T(8,128)(2,1)}) %reduce-scatter.19.cloned.1.call-update) | async-done | bytes 18448 | tf_op jit(solution)/shard_map/reduce_scatter | solution.py:201
  (361 shorter events, 100.7 us)
Async XLA Ops:
  7.2 473.9 %all-reduce.19.cloned.1.call-start = ((), (), s32[]{:S(2)}) async-start(), calls=%async_computation.13 | async-start | bytes 1376256
  131.0 9.5 %copy-start.78 = (u32[32]{0:T(128)S(1)}, u32[32]{0:T(128)}, u32[]{:S(2)}) copy-start(u32[32]{0:T(128)} %constant.217) | copy-start | bytes 388
  131.0 10.0 %copy-start.77 = (u32[32]{0:T(128)S(1)}, u32[32]{0:T(128)}, u32[]{:S(2)}) copy-start(u32[32]{0:T(128)} %constant.209) | copy-start | bytes 388
  131.1 10.6 %copy-start.40 = (s32[144,144,1]{1,0,2:T(8,128)S(1)}, s32[144,144,1]{1,0,2:T(8,128)}, u32[]{:S(2)}) copy-start(s32[144,144,1]{1,0,2:T(8,128)} %get-tuple-element.91) | copy-start | bytes 248836
  131.1 12.1 %copy-start.46 = (f32[2,2,6,12]{1,3,0,2:T(8,128)S(1)}, f32[2,2,6,12]{1,3,0,2:T(8,128)}, u32[]{:S(2)}) copy-start(f32[2,2,6,12]{1,3,0,2:T(8,128)} %get-tuple-element.87) | copy-start | bytes 3460
  132.9 14.2 %collective-permute-start = (bf16[2,2,3,24,192]{4,1,3,2,0:T(2,128)(2,1)S(1)}, bf16[2,2,3,24,192]{4,1,3,2,0:T(2,128)(2,1)S(1)}, u32[]{:S(2)}, u32[]{:S(2)}) collective-permute-start(bf16[2,2,3,24,192]{4,1,3,2,0:T(2,128)(2,1)S(1)} %get-tuple-element.82), channel_id=1, source_target_pairs={{0,28},{4,0},{8,4},{12,8},{16,12},{20,16},{24,20},{28,24},{1,29},{... | collective-permute-start | bytes 331784 | tf_op jit(solution)/shard_map/ppermute | solution.py:14
  147.1 3.2 collective-permute-start.1
  157.7 15.5 %copy-start.48 = (f32[2,6,144]{2,1,0:T(8,128)}, f32[2,6,144]{2,1,0:T(8,128)S(1)}, u32[]{:S(2)}) copy-start(f32[2,6,144]{2,1,0:T(8,128)S(1)} %get-tuple-element.104) | copy-start | bytes 20740
  178.3 3.5 collective-permute-start.2
  182.1 7.1 %collective-permute-start.3 = (bf16[2,3,24,192]{3,0,2,1:T(2,128)(2,1)S(1)}, bf16[2,3,24,192]{3,0,2,1:T(2,128)(2,1)S(1)}, u32[]{:S(2)}, u32[]{:S(2)}) collective-permute-start(bf16[2,3,24,192]{3,0,2,1:T(2,128)(2,1)S(1)} %slice.349), channel_id=1, source_target_pairs={{0,4},{4,8},{8,12},{12,16},{16,20},{20,24},{24,28},{28,0},{1,5},{5... | collective-permute-start | bytes 165896 | tf_op jit(solution)/shard_map/ppermute | solution.py:14
  209.4 275.3 %reduce-scatter.25.cloned.1.call-start = ((), (), s32[]{:S(2)}) async-start(), calls=%async_computation.9 | async-start | bytes 663552
  213.2 311.7 %reduce-scatter.29.cloned.1.call-start = ((), (), s32[]{:S(2)}) async-start(), calls=%async_computation.11 | async-start | bytes 663552
  217.8 10.4 %copy-start.12 = (f32[6,144,144]{1,2,0:T(8,128)S(1)}, f32[6,144,144]{1,2,0:T(8,128)}, u32[]{:S(2)}) copy-start(f32[6,144,144]{1,2,0:T(8,128)} %get-tuple-element.117) | copy-start | bytes 1492996
  465.4 106.8 %all-reduce.17.cloned.1.call-start = ((), (), s32[]{:S(2)}) async-start(), calls=%async_computation.12 | async-start | bytes 3391488
  466.9 13.1 %copy-start.8 = (f32[1,1,2,2,6,12,192]{6,2,5,4,3,1,0:T(2,128)S(1)}, f32[1,1,2,2,6,12,192]{6,2,5,4,3,1,0:T(2,128)}, u32[]{:S(2)}) copy-start(f32[1,1,2,2,6,12,192]{6,2,5,4,3,1,0:T(2,128)} %copy.303) | copy-start | bytes 663556
  466.9 13.1 %copy-start.10 = (bf16[1,1,2,144,3,6,32]{3,6,5,4,2,1,0:T(8,128)(2,1)S(1)}, bf16[1,1,2,144,3,6,32]{3,6,5,4,2,1,0:T(8,128)(2,1)}, u32[]{:S(2)}) copy-start(bf16[1,1,2,144,3,6,32]{3,6,5,4,2,1,0:T(8,128)(2,1)} %copy-done.9) | copy-start | bytes 995332
  466.9 13.1 %copy-start.20 = (bf16[2,192,576]{2,1,0:T(8,128)(2,1)S(1)}, bf16[2,192,576]{2,1,0:T(8,128)(2,1)}, u32[]{:S(2)}) copy-start(bf16[2,192,576]{2,1,0:T(8,128)(2,1)} %param.12) | copy-start | bytes 1327108
  467.0 13.1 %copy-start.60 = (f32[2,144]{1,0:T(2,128)S(1)}, f32[2,144]{1,0:T(2,128)}, u32[]{:S(2)}) copy-start(f32[2,144]{1,0:T(2,128)} %div.217) | copy-start | bytes 3460
  467.0 13.1 %copy-start.68 = (f32[1,1,192]{2,1,0:T(1,128)S(1)}, f32[1,1,192]{2,1,0:T(1,128)}, u32[]{:S(2)}) copy-start(f32[1,1,192]{2,1,0:T(1,128)} %copy-done.67) | copy-start | bytes 2308
  467.0 13.6 %copy-start.73 = (f32[2,144]{1,0:T(2,128)S(1)}, f32[2,144]{1,0:T(2,128)}, u32[]{:S(2)}) copy-start(f32[2,144]{1,0:T(2,128)} %add.351) | copy-start | bytes 3460
  480.7 114.0 %reduce-scatter.23.cloned.1.call-start = ((), (), s32[]{:S(2)}) async-start(), calls=%async_computation.8 | async-start | bytes 61440
  482.7 133.9 %reduce-scatter.21.cloned.1.call-start = ((), (), s32[]{:S(2)}) async-start(), calls=%async_computation.7 | async-start | bytes 184320
  484.7 154.2 %reduce-scatter.27.cloned.1.call-start = ((), (), s32[]{:S(2)}) async-start(), calls=%async_computation.10 | async-start | bytes 245760
  487.0 173.9 %reduce-scatter.19.cloned.1.call-start = ((), (), s32[]{:S(2)}) async-start(), calls=%async_computation.6 | async-start | bytes 122880 | tf_op jit(solution)/shard_map/reduce_scatter | solution.py:201
  (67 other events, 190.4 us)
Sparse Core Ops, SparseCore 0:
  209.5 70.8 all-reduce.18
  283.6 61.5 reduce-scatter.24
  465.5 59.3 reduce-scatter.28
  527.1 45.0 all-reduce.16
  575.1 19.5 reduce-scatter.22
  596.9 19.6 reduce-scatter.20
  619.1 19.7 reduce-scatter.26
  641.3 19.5 reduce-scatter.18
where the time goes:
time: 674 us; the launch traced here: 669 us
  other arithmetic  263 us (39%)
  local copies, waits for them, and re-layouts  178 us (26%)
  waiting for transfers between devices  131 us (19%)
  blocking collectives  40.9 us (6%)
  matrix products  30.3 us (4%)
  between operations  17.2 us (3%)
  starting transfers between devices  9.24 us (1%)
    scatter-add x2, other arithmetic, run_block(): bias_full = jnp.take(table_part, position_index(), axis=3)  226 us
    unnamed x15, waiting for transfers between devices  102 us
    gather x4, local copies, waits for them, and re-layouts, run_block(): bias_full = jnp.take(table_part, position_index(), axis=3)  101 us
    psum x1, blocking collectives, body(): gain_grad = lax.psum(jnp.stack((first_gains, second_gains)), ('lat', 'lon'))  40.9 us
    unnamed x186, local copies, waits for them, and re-layouts  27 us
    broadcast_in_dim x2, local copies, waits for them, and re-layouts, run_block(): scores = jnp.where(allowed, scores + bias_full[:, :, None], -1e+30)  20.9 us
    reduce_scatter x1, waiting for transfers between devices, body(): lax.psum_scatter(partial_sums[3].astype(jnp.bfloat16), 'lon', scatter_dim...  20.4 us
  transfers between devices with their start and end apart: 12, of which 9 were waited for; matrix products, arithmetic and copies ran while one was open for 44% of the time, Pallas kernels for 0%

commit v1 on v0

v1 whole, which is shorter than its diff:
```python
import functools

import jax
import jax.numpy as jnp
import numpy as np
from jax import lax
from jax.experimental import pallas as pl
from jax.experimental.pallas import tpu as pltpu
from jax.sharding import PartitionSpec as P

WZ = 2
WH = 6
WW = 12
ZH = WZ * WH
SPAN = 2 * WW - 1
WT = ZH * WW
EPS = 1e-05
NEG = -1e30

f32 = jnp.float32
bf16 = jnp.bfloat16


def one_hot(sources, width):
    table = np.zeros((len(sources), width), np.float32)
    for row, source in enumerate(sources):
        if source >= 0:
            table[row, source] = 1.0
    return jnp.asarray(table, bf16)


class Plan:
    def __init__(self, lon, heads, channels):
        half_h, half_w = WH // 2, WW // 2
        self.lon, self.heads, self.channels = lon, heads, channels
        self.tokens = lon * ZH
        self.windows = lon // WW
        order = [(l, z, h) for l in range(lon) for z in range(WZ) for h in range(WH)]
        self.index = {t: i for i, t in enumerate(order)}
        natural = {(l, z, h): (z * WH + h) * lon + l for l, z, h in order}
        self.to_order = one_hot([natural[t] for t in order], self.tokens)
        place = {natural[t]: i for i, t in enumerate(order)}
        self.to_natural = one_hot([place[i] for i in range(self.tokens)], self.tokens)
        lat_msg = [t for t in order if t[2] < half_h and t[0] >= half_w]
        lon_msg = [t for t in order if t[2] >= half_h and t[0] < half_w]
        cor_msg = [t for t in order if t[2] < half_h and t[0] < half_w]
        self.sizes = (len(lat_msg), len(lon_msg), len(cor_msg))
        self.send_down = [one_hot([self.index[t] for t in m], self.tokens) for m in (lat_msg, lon_msg, cor_msg)]
        picks = ([], [], [], [])
        for l, z, h in order:
            t = (l + half_w, (z + WZ // 2) % WZ, h + half_h)
            over_l, over_h = t[0] >= lon, t[2] >= WH
            t = (t[0] % lon, t[1], t[2] % WH)
            which = {(False, False): 0, (False, True): 1, (True, False): 2, (True, True): 3}[(over_l, over_h)]
            source = self.index[t] if which == 0 else (lat_msg, lon_msg, cor_msg)[which - 1].index(t)
            for i, pick in enumerate(picks):
                pick.append(source if i == which else -1)
        self.roll = [one_hot(picks[0], self.tokens)] + [one_hot(p, n) for p, n in zip(picks[1:], self.sizes)]
        back = {}
        for l, z, h in order:
            t = (l + half_w, (z + WZ // 2) % WZ, h + half_h)
            which = {(False, False): 0, (False, True): 1, (True, False): 2, (True, True): 3}[(t[0] >= lon, t[2] >= WH)]
            back[(t[0] % lon, t[1], t[2] % WH)] = (which, self.index[(l, z, h)])
        msgs = ([], [], [])
        picks = ([], [], [], [])
        for t in order:
            which, source = back[t]
            if which:
                msgs[which - 1].append(source)
            for i, pick in enumerate(picks):
                pick.append((source if which == 0 else len(msgs[which - 1]) - 1) if i == which else -1)
        self.send_up = [one_hot(m, self.tokens) for m in msgs]
        self.unroll = [one_hot(picks[0], self.tokens)] + [one_hot(p, n) for p, n in zip(picks[1:], self.sizes)]
        row = -np.ones(16 * heads, np.int64)
        for h in range(heads):
            for i in range(ZH):
                row[16 * h + i] = 8 * i + h
        self.row_pick = one_hot(row, 8 * ZH)
        lane = -np.ones(384, np.int64)
        for d in range(SPAN):
            for zk in range(WZ):
                for hk in range(WH):
                    lane[(SPAN - 1 - d) * ZH + zk * WH + hk] = zk * 256 + hk * SPAN + d
        self.lane_pick = one_hot(lane, 512).T
        level = np.array([(r % ZH) // WH for r in range(WT)])
        late = np.array([int(r % WH >= WH // 2) for r in range(WT)])
        self.level_mask = jnp.asarray(np.where(level[:, None] == level[None, :], 0.0, NEG), f32)
        self.late_mask = jnp.asarray(np.where(late[:, None] == late[None, :], 0.0, NEG), f32)


def mm(a, b):
    return lax.dot_general(a, b, (((1,), (0,)), ((), ())), preferred_element_type=f32)


def mm_nt(a, b):
    return lax.dot_general(a, b, (((1,), (1,)), ((), ())), preferred_element_type=f32)


def mm_tn(a, b):
    return lax.dot_general(a, b, (((0,), (0,)), ((), ())), preferred_element_type=f32)


def split3(v):
    hi = v.astype(bf16)
    rest = v - hi.astype(f32)
    mid = rest.astype(bf16)
    low = (rest - mid.astype(f32)).astype(bf16)
    return hi, mid, low


def norm(u, gain):
    average = jnp.mean(u, -1, keepdims=True)
    centred = u - average
    scale = lax.rsqrt(jnp.mean(centred * centred, -1, keepdims=True) + EPS)
    hat = centred * scale
    return (hat * gain).astype(bf16), hat, scale


def norm_back(grad, hat, scale, gain):
    inner = grad * gain
    gain_grad = jnp.sum(grad * hat, 0, keepdims=True)
    value = scale * (inner - jnp.mean(inner, -1, keepdims=True) - hat * jnp.mean(inner * hat, -1, keepdims=True))
    return value, gain_grad


def expand_bias(block, table_ref, row_pick, lane_pick, x_ref, bias_ref, heads, mask):
    x_ref[...] = jnp.zeros_like(x_ref)
    table = table_ref[block]
    piece = WH * SPAN
    for i in range(ZH):
        for zk in range(WZ):
            zq, hq = i // WH, i % WH
            start = ((zq * WZ + zk) * WH + hq) * piece
            x_ref[8 * i : 8 * i + heads, 256 * zk : 256 * zk + piece] = table[:, start : start + piece]
    wide = None
    for part in split3(x_ref[...]):
        moved = mm(mm(row_pick[...], part).astype(bf16), lane_pick[...])
        wide = moved if wide is None else wide + moved
    for w in range(WW):
        start = (WW - 1 - w) * ZH
        turned = pltpu.roll(wide, (384 - start) % 384, 1) if start else wide
        for h in range(heads):
            rows = turned[16 * h : 16 * h + ZH, 0:WT]
            if mask is not None:
                rows = rows + mask[ZH * w : ZH * w + ZH, :]
            bias_ref[h, ZH * w : ZH * w + ZH, :] = rows


def fold_bias(bias_grad_ref, row_pick, lane_pick, fold_ref, out_ref, heads):
    fold_ref[...] = jnp.zeros_like(fold_ref)
    total = None
    for w in range(WW):
        for h in range(heads):
            fold_ref[16 * h : 16 * h + ZH, 0:WT] = bias_grad_ref[h, ZH * w : ZH * w + ZH, :]
        start = (WW - 1 - w) * ZH
        turned = fold_ref[...]
        if start:
            turned = pltpu.roll(turned, start, 1)
        total = turned if total is None else total + turned
    back = mm_nt(mm_tn(row_pick[...], total.astype(bf16)).astype(bf16), lane_pick[...])
    piece = WH * SPAN
    for i in range(ZH):
        for zk in range(WZ):
            zq, hq = i // WH, i % WH
            slot = (zq * WZ + zk) * WH + hq
            out_ref[slot] = back[8 * i : 8 * i + heads, 256 * zk : 256 * zk + piece].astype(out_ref.dtype)


def head_masks(heads, channels):
    lanes = lax.broadcasted_iota(jnp.int32, (1, channels), 1)
    size = channels // heads
    return [(lanes >= size * h) & (lanes < size * (h + 1)) for h in range(heads)]


def pick(mask, value):
    return jnp.where(mask, value, jnp.zeros_like(value))


def forward(u, block, gains, w, bias_ref, p_ref, plan):
    channels, heads = plan.channels, plan.heads
    w_qkv, w_proj, w_fc1, w_fc2 = w
    gain_one = gains[block, 0:1, :]
    gain_two = gains[block, 1:2, :]
    n1, hat1, scale1 = norm(u, gain_one)
    qkv_w = w_qkv[block]
    q, k, v = (mm(n1, qkv_w[:, i * channels : (i + 1) * channels]).astype(bf16) for i in range(3))
    masks = head_masks(heads, channels)
    factor = (channels // heads) ** (-0.5)
    outs = []
    for n in range(plan.windows):
        rows = slice(n * WT, (n + 1) * WT)
        qw, kw, vw = q[rows], k[rows], v[rows]
        total = None
        for h in range(heads):
            s = mm_nt(pick(masks[h], qw), kw) * factor + bias_ref[h]
            e = jnp.exp(s - jnp.max(s, -1, keepdims=True))
            p = (e / jnp.sum(e, -1, keepdims=True))
            if p_ref is not None:
                p_ref[n * heads + h] = p
            o = mm(p.astype(bf16), pick(masks[h], vw))
            total = o if total is None else total + o
        outs.append(total.astype(bf16))
    o = jnp.concatenate(outs, 0)
    middle = u + mm(o, w_proj[block])
    n2, hat2, scale2 = norm(middle, gain_two)
    wide = mm(n2, w_fc1[block])
    cdf = 0.5 * (1.0 + lax.erf(wide * (0.5**0.5)))
    g = (wide * cdf).astype(bf16)
    out = middle + mm(g, w_fc2[block])
    return out, (n1, hat1, scale1, q, k, v, o, n2, hat2, scale2, wide, cdf, g)


def backward(grad, kept, block, gains, w, bias_grad_ref, p_ref, plan):
    channels, heads = plan.channels, plan.heads
    w_qkv, w_proj, w_fc1, w_fc2 = w
    n1, hat1, scale1, q, k, v, o, n2, hat2, scale2, wide, cdf, g = kept
    gain_one = gains[block, 0:1, :]
    gain_two = gains[block, 1:2, :]
    dz = grad.astype(bf16)
    dg = mm_nt(dz, w_fc2[block]).astype(bf16).astype(f32)
    density = jnp.exp(-0.5 * wide * wide) * (1.0 / np.sqrt(2.0 * np.pi))
    dh = (dg * (cdf + wide * density)).astype(bf16)
    dn2 = mm_nt(dh, w_fc1[block]).astype(bf16).astype(f32)
    dmid, gain_grad_two = norm_back(dn2, hat2, scale2, gain_two)
    dmid = grad + dmid
    dp_out = dmid.astype(bf16)
    do = mm_nt(dp_out, w_proj[block]).astype(bf16)
    masks = head_masks(heads, channels)
    factor = (channels // heads) ** (-0.5)
    dqs, dks, dvs = [], [], []
    for n in range(plan.windows):
        rows = slice(n * WT, (n + 1) * WT)
        qw, kw, vw, dow = q[rows], k[rows], v[rows], do[rows]
        dq = dk = dv = None
        for h in range(heads):
            dom = pick(masks[h], dow)
            p = p_ref[n * heads + h]
            dp = mm_nt(dom, vw).astype(bf16).astype(f32)
            ds = p * (dp - jnp.sum(dp * p, -1, keepdims=True))
            if n == 0:
                bias_grad_ref[h] = ds
            else:
                bias_grad_ref[h] += ds
            dsb = (ds * factor).astype(bf16)
            a = mm(dsb, pick(masks[h], kw))
            b = mm_tn(dsb, pick(masks[h], qw))
            c = mm_tn(p.astype(bf16), dom)
            dq, dk, dv = (a, b, c) if dq is None else (dq + a, dk + b, dv + c)
        dqs.append(dq.astype(bf16))
        dks.append(dk.astype(bf16))
        dvs.append(dv.astype(bf16))
    dq, dk, dv = (jnp.concatenate(parts, 0) for parts in (dqs, dks, dvs))
    qkv_w = w_qkv[block]
    dn1 = None
    for i, part in enumerate((dq, dk, dv)):
        term = mm_nt(part, qkv_w[:, i * channels : (i + 1) * channels])
        dn1 = term if dn1 is None else dn1 + term
    dn1 = dn1.astype(bf16).astype(f32)
    du, gain_grad_one = norm_back(dn1, hat1, scale1, gain_one)
    du = dmid + du
    return du, (gain_grad_one, gain_grad_two), (dq, dk, dv, dp_out, dh, dz)


def weight_grads(kept, cots, out_ref):
    n1, o, n2, g = kept[0], kept[6], kept[7], kept[12]
    dq, dk, dv, dp_out, dh, dz = cots
    lat, lon = out_ref.shape[0], out_ref.shape[1]
    channels = n1.shape[1]
    rows = channels // lat
    g_qkv = jnp.concatenate([mm_tn(n1, part) for part in (dq, dk, dv)], 1)
    g_proj = mm_tn(o, dp_out)
    g_fc1 = mm_tn(n2, dh)
    g_fc2 = mm_tn(g, dz)
    groups = g.shape[1] // channels
    g_fc2 = g_fc2.reshape(lat, groups, rows, channels)
    parts = [g_qkv, g_proj, g_fc1] + [g_fc2[:, a].reshape(channels, channels) for a in range(groups)]
    for j in range(lon):
        pieces = []
        for part in parts:
            width = part.shape[1] // lon
            pieces.append(part[:, j * width : (j + 1) * width])
        mine = jnp.concatenate(pieces, 1).astype(out_ref.dtype)
        for i in range(lat):
            out_ref[i, j] = mine[i * rows : (i + 1) * rows]


def first_kernel(plan, x, cot, to_order, sel_lat, sel_lon, sel_cor, table, row_pick, lane_pick, w_qkv, w_proj, w_fc1, w_fc2, gains,
                 s1, m_lat, m_lon, m_cor, x_ref, bias_ref):
    w = (w_qkv, w_proj, w_fc1, w_fc2)
    expand_bias(0, table, row_pick, lane_pick, x_ref, bias_ref, plan.heads, None)
    u = mm(to_order[...], x[...])
    out, _ = forward(u, 0, gains, w, bias_ref, None, plan)
    both = jnp.concatenate([out, mm(to_order[...], cot[...])], 1).astype(bf16)
    s1[...] = both
    for message, chosen in ((m_lat, sel_lat), (m_lon, sel_lon), (m_cor, sel_cor)):
        message[...] = mm(chosen[...], both).astype(bf16)


def second_kernel(plan, last, s1, r_lat, r_lon, r_cor, roll0, roll1, roll2, roll3, sel_lat, sel_lon, sel_cor,
                  level_mask, late_mask, table, row_pick, lane_pick, w_qkv, w_proj, w_fc1, w_fc2, gains,
                  rolled, m_lat, m_lon, m_cor, grads, gain_out, table_out,
                  x_ref, bias_ref, p_ref, bias_grad_ref, fold_ref):
    w = (w_qkv, w_proj, w_fc1, w_fc2)
    channels = plan.channels
    mask = level_mask[...] + late_mask[...] * last[0].astype(f32)
    expand_bias(1, table, row_pick, lane_pick, x_ref, bias_ref, plan.heads, mask)
    both = mm(roll0[...], s1[...]) + mm(roll1[...], r_lat[...]) + mm(roll2[...], r_lon[...]) + mm(roll3[...], r_cor[...])
    u, cot = both[:, :channels], both[:, channels:]
    _, kept = forward(u, 1, gains, w, bias_ref, p_ref, plan)
    du, gain_grads, cots = backward(cot, kept, 1, gains, w, bias_grad_ref, p_ref, plan)
    du = du.astype(bf16)
    rolled[...] = du
    for message, chosen in ((m_lat, sel_lat), (m_lon, sel_lon), (m_cor, sel_cor)):
        message[...] = mm(chosen[...], du).astype(bf16)
    gain_out[0:1, :] = gain_grads[0]
    gain_out[1:2, :] = gain_grads[1]
    weight_grads(kept, cots, grads)
    fold_bias(bias_grad_ref, row_pick, lane_pick, fold_ref, table_out, plan.heads)


def third_kernel(plan, x, rolled, r_lat, r_lon, r_cor, unroll0, unroll1, unroll2, unroll3, to_order, to_natural,
                 table, row_pick, lane_pick, w_qkv, w_proj, w_fc1, w_fc2, gains,
                 state_grad, grads, gain_out, table_out,
                 x_ref, bias_ref, p_ref, bias_grad_ref, fold_ref):
    w = (w_qkv, w_proj, w_fc1, w_fc2)
    expand_bias(0, table, row_pick, lane_pick, x_ref, bias_ref, plan.heads, None)
    u = mm(to_order[...], x[...])
    _, kept = forward(u, 0, gains, w, bias_ref, p_ref, plan)
    grad = mm(unroll0[...], rolled[...]) + mm(unroll1[...], r_lat[...]) + mm(unroll2[...], r_lon[...]) + mm(unroll3[...], r_cor[...])
    du, gain_grads, cots = backward(grad, kept, 0, gains, w, bias_grad_ref, p_ref, plan)
    state_grad[...] = sum(mm(to_natural[...], part) for part in split3(du))
    gain_out[0:1, :] = gain_grads[0]
    gain_out[1:2, :] = gain_grads[1]
    weight_grads(kept, cots, grads)
    fold_bias(bias_grad_ref, row_pick, lane_pick, fold_ref, table_out, plan.heads)


VMEM_LIMIT = 60 * 1024 * 1024


def call(body, outs, scratch, args, name, flops, scalar=False):
    specs = [pl.BlockSpec(memory_space=pltpu.VMEM) for _ in args]
    if scalar:
        specs[0] = pl.BlockSpec(memory_space=pltpu.SMEM)
    moved = sum(a.size * a.dtype.itemsize for a in args)
    return pl.pallas_call(
        body,
        out_shape=outs,
        in_specs=specs,
        out_specs=[pl.BlockSpec(memory_space=pltpu.VMEM) for _ in outs],
        scratch_shapes=scratch,
        name=name,
        compiler_params=pltpu.CompilerParams(vmem_limit_bytes=VMEM_LIMIT),
        cost_estimate=pl.CostEstimate(flops=flops, bytes_accessed=moved, transcendentals=0),
    )(*args)


def rounded(v):
    return lax.reduce_precision(v, 8, 7)


def body(state, out_cot, qkv_weight, proj_weight, fc1_weight, fc2_weight, norm_gain, bias_table):
    levels, rows, lon, channels = state.shape
    heads = bias_table.shape[3]
    assert levels == WZ and rows == WH and lon % WW == 0
    plan = Plan(lon, heads, channels)
    tokens = plan.tokens
    lats, lons = lax.axis_size("lat"), lax.axis_size("lon")
    count = lats * lons
    axes = ("lat", "lon")
    lat, lon_at = lax.axis_index("lat"), lax.axis_index("lon")
    me = lat * lons + lon_at

    def shift(value, by_lat, by_lon):
        pairs = []
        for a in range(lats):
            for b in range(lons):
                pairs.append((a * lons + b, ((a + by_lat) % lats) * lons + (b + by_lon) % lons))
        return lax.ppermute(value, axes, pairs)

    x = state.reshape(tokens, channels)
    cot = out_cot.reshape(tokens, channels)
    table = bias_table.reshape(2, heads, bias_table.shape[-1])
    weights = (qkv_weight, proj_weight, fc1_weight, fc2_weight)
    n_lat, n_lon, n_cor = plan.sizes
    piece = WH * SPAN
    hidden = fc1_weight.shape[-1]
    columns = sum(a.shape[-1] for a in (qkv_weight, proj_weight, fc1_weight)) // lons + (hidden // channels) * (channels // lons)
    grad_shape = jax.ShapeDtypeStruct((lats, lons, channels // lats, columns), bf16)
    gain_shape = jax.ShapeDtypeStruct((2, channels), f32)
    table_shape = jax.ShapeDtypeStruct((WZ * WZ * WH, heads, piece), f32)
    bias_scratch = [pltpu.VMEM((8 * ZH, 512), f32), pltpu.VMEM((heads, WT, WT), f32)]
    back_scratch = bias_scratch + [
        pltpu.VMEM((plan.windows * heads, WT, WT), f32),
        pltpu.VMEM((heads, WT, WT), f32),
        pltpu.VMEM((16 * heads, 384), f32),
    ]

    def messages(width):
        return [jax.ShapeDtypeStruct((n, width), bf16) for n in plan.sizes]

    flops = 2 * tokens * sum(w.size // 2 for w in weights)
    s1, *out = call(
        functools.partial(first_kernel, plan),
        [jax.ShapeDtypeStruct((tokens, 2 * channels), bf16)] + messages(2 * channels),
        bias_scratch,
        [x, cot, plan.to_order, *plan.send_down, table, plan.row_pick, plan.lane_pick, *weights, norm_gain],
        "first", flops,
    )
    r_lat = shift(out[0], -1, 0)
    r_lon = shift(out[1], 0, -1)
    r_cor = shift(out[2], -1, -1)
    last = (lat == lats - 1).astype(jnp.int32).reshape(1)
    rolled, *out = call(
        functools.partial(second_kernel, plan),
        [jax.ShapeDtypeStruct((tokens, channels), bf16)] + messages(channels) + [grad_shape, gain_shape, table_shape],
        back_scratch,
        [last, s1, r_lat, r_lon, r_cor, *plan.roll, *plan.send_up, plan.level_mask, plan.late_mask,
         table, plan.row_pick, plan.lane_pick, *weights, norm_gain],
        "second", 3 * flops, True,
    )
    r_lat = shift(out[0], 1, 0)
    r_lon = shift(out[1], 0, 1)
    r_cor = shift(out[2], 1, 1)
    grads_two, gain_two, table_two = out[3:]
    state_grad, grads_one, gain_one, table_one = call(
        functools.partial(third_kernel, plan),
        [jax.ShapeDtypeStruct((tokens, channels), f32), grad_shape, gain_shape, table_shape],
        back_scratch,
        [x, rolled, r_lat, r_lon, r_cor, *plan.unroll, plan.to_order, plan.to_natural,
         table, plan.row_pick, plan.lane_pick, *weights, norm_gain],
        "third", 3 * flops,
    )

    bits = count.bit_length() - 1
    lon_bits = lons.bit_length() - 1
    size = grad_shape.shape[2:]
    held = jnp.concatenate((grads_one, grads_two), -1).reshape((2,) * bits + (size[0], 2 * size[1]))
    gain = jnp.concatenate((gain_one, gain_two), 0)
    tables = jnp.stack((table_one, table_two)).transpose(0, 2, 1, 3).reshape(2 * heads, lons, -1)
    tables = tables.transpose(1, 0, 2).reshape((2,) * lon_bits + (2 * heads, -1))
    for bit in range(bits):
        mine = (me >> bit) & 1
        pairs = [(i, i ^ (1 << bit)) for i in range(count)]
        axis = held.ndim - 3
        keep = lax.dynamic_index_in_dim(held, mine, axis, keepdims=False)
        send = lax.dynamic_index_in_dim(held, 1 - mine, axis, keepdims=False)
        high = rounded(gain)
        low = rounded(gain - high)
        extra = jnp.concatenate((high, low), 0).astype(bf16)
        extra = jnp.pad(extra, ((0, 0), (0, 2 * size[1] - channels)))
        message = jnp.concatenate((send.astype(bf16).reshape(-1, 2 * size[1]), extra), 0)
        got = lax.ppermute(message, axes, pairs)
        other = got[-8:, :channels].astype(f32)
        gain = (high + low) + (other[:4] + other[4:])
        held = keep.astype(f32) + got[:-8].reshape(keep.shape).astype(f32)
        if bit < bits - 1:
            held = held.astype(bf16)
        if bit < lon_bits:
            axis = tables.ndim - 3
            keep = lax.dynamic_index_in_dim(tables, mine, axis, keepdims=False)
            send = lax.dynamic_index_in_dim(tables, 1 - mine, axis, keepdims=False)
            tables = keep + lax.ppermute(send.astype(bf16), axes, pairs).astype(f32)

    cuts, start = [], 0
    widths = [w.shape[-1] // lons for w in (qkv_weight, proj_weight, fc1_weight)] + [channels // lons] * (hidden // channels)
    for width in widths:
        cuts.append(jnp.stack((held[:, start : start + width], held[:, size[1] + start : size[1] + start + width])))
        start += width
    fc2 = jnp.concatenate(cuts[3:], 1)
    return (
        state_grad.reshape(state.shape),
        cuts[0],
        cuts[1],
        cuts[2],
        fc2,
        gain.reshape(2, 2, channels),
        tables.reshape(2, 1, 1, heads, -1),
    )


def solution(mesh):
    in_specs = (
        P(None, "lat", "lon", None),
        P(None, "lat", "lon", None),
        P(),
        P(),
        P(),
        P(),
        P(),
        P(None, "lat", None, None, None),
    )
    out_specs = (
        P(None, "lat", "lon", None),
        P(None, "lat", "lon"),
        P(None, "lat", "lon"),
        P(None, "lat", "lon"),
        P(None, "lat", "lon"),
        P(),
        P(None, "lat", None, None, "lon"),
    )
    return jax.shard_map(body, mesh=mesh, in_specs=in_specs, out_specs=out_specs, check_vma=False)
```

time: 674 us -> 99.2 us (0.15)
  other arithmetic: 263 us -> 5.27 us
  local copies, waits for them, and re-layouts: 178 us -> 9.88 us
  waiting for transfers between devices: 131 us -> 37.8 us
  blocking collectives: 40.9 us -> 0 us
  Pallas kernels: 0 us -> 32.9 us
  matrix products: 30.3 us -> 0 us
  between operations: 17.2 us -> 1.07 us
    scatter-add x2 -> x0, other arithmetic: 226 us -> none  [run_block(): bias_full = jnp.take(table_part, position_index(), axis=3)]
    unnamed x15 -> x0, waiting for transfers between devices: 102 us -> none
    gather x4 -> x0, local copies, waits for them, and re-layouts: 101 us -> none  [run_block(): bias_full = jnp.take(table_part, position_index(), axis=3)]
    psum x1 -> x0, blocking collectives: 40.9 us -> none  [body(): gain_grad = lax.psum(jnp.stack((first_gains, second_gains)), ('lat', 'lon'))]
    pallas_call x0 -> x3, Pallas kernels: none -> 32.9 us  [call(): pl.pallas_call(body, out_shape=outs, in_specs=specs, out_specs=[pl.BlockS...]
    ppermute x4 -> x13, waiting for transfers between devices: 8.61 us -> 37.8 us  [the longest x5 27.9 us: body(): got = lax.ppermute(message, axes, pairs)]
    dot_general x33 -> x0, matrix products: 24.9 us -> none  [the longest x8 9.84 us: close_block(): lax.dot_general(inputs_act.reshape(-1, inputs_act.shape[-1]), grad_out.re...]
    unnamed x186 -> x27, local copies, waits for them, and re-layouts: 27 us -> 5.26 us
  transfers between devices with their start and end apart: 12 -> 13, of which waited for: 9 -> 9; matrix products, arithmetic and copies ran while one was open for 44% -> 2% of each run, Pallas kernels for 0% -> 0%
where the time goes in v1:
time: 99.2 us; the launch traced here: 98.9 us
  waiting for transfers between devices  37.8 us (38%)
  Pallas kernels  32.9 us (33%)
  starting transfers between devices  12 us (12%)
  local copies, waits for them, and re-layouts  9.88 us (10%)
  other arithmetic  5.27 us (5%)
  between operations  1.07 us (1%)
    pallas_call x3, Pallas kernels, call(): pl.pallas_call(body, out_shape=outs, in_specs=specs, out_specs=[pl.BlockS...  32.9 us
    ppermute x5, waiting for transfers between devices, body(): got = lax.ppermute(message, axes, pairs)  27.9 us
    ppermute x6, waiting for transfers between devices, shift(): return lax.ppermute(value, axes, pairs)  9.84 us
    ppermute x6, starting transfers between devices, shift(): return lax.ppermute(value, axes, pairs)  8.63 us
    unnamed x27, local copies, waits for them, and re-layouts  5.26 us
    ppermute x5, starting transfers between devices, body(): got = lax.ppermute(message, axes, pairs)  2.06 us
  transfers between devices with their start and end apart: 13, of which 9 were waited for; matrix products, arithmetic and copies ran while one was open for 2% of the time, Pallas kernels for 0%

profile of v1, /device:TPU:0, one launch (start us, length us, event | category | flops | bytes accessed | tf_op | source)
XLA Modules:
  0.0 98.9 jit_solution(1033708299114041017)
XLA Ops:
  0.6 2.2 %copy.57.w_fc2 = bf16[2,768,192]{2,1,0:T(8,128)(2,1)} copy(bf16[2,768,192]{1,2,0:T(8,128)(2,1)} %param.33) | data formatting | bytes 1179648 | tf_op args[5]
  2.9 1.0 %copy.87 = f32[2,1,1,6,3312]{4,0,3,2,1:T(2,128)S(1)} copy(f32[2,1,1,6,3312]{4,2,3,1,0:T(1,128)} %param.35) | data formatting | bytes 317952 | tf_op args[7]
  3.9 0.7 copy.56.table
  4.6 7.2 %first.1 = (bf16[288,384]{1,0:T(8,128)(2,1)}, bf16[108,384]{1,0:T(8,128)(2,1)}, bf16[36,384]{1,0:T(8,128)(2,1)}, bf16[36,384]{1,0:T(8,128)(2,1)}) custom-call(bf16[288,192]{1,0:T(8,128)(2,1)} %bitcast.95, bf16[288,192]{1,0:T(8,128)(2,1)} %bitcast.101, bf16[288,288]{1,0:T(8,128)(2,1)} %constant.110.clone.to_order, bf16[108,288]{1,0:T(8,128)(2,1)} %constant.112.clone.sel_lat, ...), custom_call_target="tpu_custom_call" | custom-call | flops 254803968 | bytes 2833920 | tf_op jit(solution)/shard_map/first/pallas_call | solution.py:346
  11.8 6.0 %collective-permute-start = (bf16[108,384]{1,0:T(8,128)(2,1)}, bf16[108,384]{1,0:T(8,128)(2,1)S(1)}, u32[]{:S(2)}, u32[]{:S(2)}) collective-permute-start(bf16[108,384]{1,0:T(8,128)(2,1)} %get-tuple-element.23), channel_id=1, source_target_pairs={{0,28},{1,29},{2,30},{3,31},{4,0},{5,1},{6,2},{7,3},{8,4},{9,5},{1... | collective-permute-start | bytes 248840 | tf_op jit(solution)/shard_map/ppermute | solution.py:379
  18.4 0.9 collective-permute-start.2
  19.4 0.9 collective-permute-done.1.r_lon
  20.2 1.7 %collective-permute-done.2.r_cor = bf16[36,384]{1,0:T(8,128)(2,1)S(1)} collective-permute-done((bf16[36,384]{1,0:T(8,128)(2,1)}, bf16[36,384]{1,0:T(8,128)(2,1)S(1)}, u32[]{:S(2)}, u32[]{:S(2)}) %collective-permute-start.2) | collective-permute-done | bytes 27680 | tf_op jit(solution)/shard_map/ppermute | solution.py:379
  22.6 12.0 %second.1 = (bf16[288,192]{1,0:T(8,128)(2,1)}, bf16[108,192]{1,0:T(8,128)(2,1)}, bf16[36,192]{1,0:T(8,128)(2,1)}, bf16[36,192]{1,0:T(8,128)(2,1)}, bf16[8,4,24,5...) custom-call(s32[1]{0:T(128)} %bitcast.1.last, bf16[288,384]{1,0:T(8,128)(2,1)} %get-tuple-element.22.s1, ...), custom_call_target="tpu_custom_call" | custom-call | flops 764411904 | bytes 3241732 | tf_op jit(solution)/shard_map/second/pallas_call | solution.py:346
  34.6 0.7 collective-permute-start.3
  35.6 3.1 %collective-permute-done.4.r_lon = bf16[36,192]{1,0:T(8,128)(2,1)S(1)} collective-permute-done((bf16[36,192]{1,0:T(8,128)(2,1)}, bf16[36,192]{1,0:T(8,128)(2,1)S(1)}, u32[]{:S(2)}, u32[]{:S(2)}) %collective-permute-start.4) | collective-permute-done | bytes 13856 | tf_op jit(solution)/shard_map/ppermute | solution.py:379
  38.8 4.1 %collective-permute-done.5.r_cor = bf16[36,192]{1,0:T(8,128)(2,1)S(1)} collective-permute-done((bf16[36,192]{1,0:T(8,128)(2,1)}, bf16[36,192]{1,0:T(8,128)(2,1)S(1)}, u32[]{:S(2)}, u32[]{:S(2)}) %collective-permute-start.5) | collective-permute-done | bytes 13856 | tf_op jit(solution)/shard_map/ppermute | solution.py:379
  43.5 13.7 %third.1 = (f32[288,192]{1,0:T(8,128)}, bf16[8,4,24,576]{3,2,1,0:T(8,128)(2,1)}, f32[2,192]{1,0:T(2,128)}, f32[24,6,138]{2,1,0:T(8,128)}) custom-call(bf16[288,192]{1,0:T(8,128)(2,1)} %bitcast.96, bf16[288,192]{1,0:T(8,128)(2,1)} %get-tuple-element.26.rolled, bf16[108,192]{1,0:T(8,128)(2,1)} %copy-done.4, bf16[36,192]{1,0:T(8,128)(2,1)} %copy-done.7, ...), custom_call_target="tpu_custom_call" | custom-call | flops 764411904 | bytes 3234816 | tf_op jit(solution)/shard_map/third/pallas_call | solution.py:346
  57.2 1.7 %pad_maximum_fusion = bf16[8,4,24,1152]{3,2,1,0:T(8,128)(2,1)S(1)} fusion(bf16[8,4,24,576]{3,2,1,0:T(8,128)(2,1)S(1)} %copy-done, bf16[8,4,24,576]{3,2,1,0:T(8,128)(2,1)} %get-tuple-element.31), kind=kLoop, calls=%fused_computation | loop fusion | flops 3538944 | bytes 3538944 | tf_op jit(solution)/shard_map/concatenate | solution.py:438
  59.4 2.6 %collective-permute-done.6 = bf16[392,1152]{1,0:T(8,128)(2,1)} collective-permute-done((bf16[392,1152]{1,0:T(8,128)(2,1)S(1)}, bf16[392,1152]{1,0:T(8,128)(2,1)}, u32[]{:S(2)}, u32[]{:S(2)}) %collective-permute-start.6) | collective-permute-done | bytes 903200 | tf_op jit(solution)/shard_map/ppermute | solution.py:453
  62.0 1.2 %slice.136 = bf16[384,1152]{1,0:T(8,128)(2,1)S(1)} slice(bf16[392,1152]{1,0:T(8,128)(2,1)} %collective-permute-done.6), slice={[0:384], [0:1152]} | slice | bytes 1769472 | tf_op jit(solution)/shard_map/slice | solution.py:456
  63.6 0.8 slice_convert_fusion.4
  64.4 1.2 %collective-permute-start.7 = (bf16[200,1152]{1,0:T(8,128)(2,1)S(1)}, bf16[200,1152]{1,0:T(8,128)(2,1)S(1)}, u32[]{:S(2)}, u32[]{:S(2)}) collective-permute-start(bf16[200,1152]{1,0:T(8,128)(2,1)S(1)} %pad_maximum_fusion.2), channel_id=1, source_target_pairs={{0,2},{1,3},{2,0},{3,1},{4,6},{5,7},{6,4},{7,5},{8,10},{9,11},{10,... | collective-permute-start | bytes 1382408 | tf_op jit(solution)/shard_map/ppermute | solution.py:453
  66.4 10.7 %collective-permute-done.7 = bf16[200,1152]{1,0:T(8,128)(2,1)S(1)} collective-permute-done((bf16[200,1152]{1,0:T(8,128)(2,1)S(1)}, bf16[200,1152]{1,0:T(8,128)(2,1)S(1)}, u32[]{:S(2)}, u32[]{:S(2)}) %collective-permute-start.7) | collective-permute-done | bytes 460832 | tf_op jit(solution)/shard_map/ppermute | solution.py:453
  77.7 6.8 %collective-permute-done.8 = bf16[104,1152]{1,0:T(8,128)(2,1)S(1)} collective-permute-done((bf16[104,1152]{1,0:T(8,128)(2,1)S(1)}, bf16[104,1152]{1,0:T(8,128)(2,1)S(1)}, u32[]{:S(2)}, u32[]{:S(2)}) %collective-permute-start.8) | collective-permute-done | bytes 239648 | tf_op jit(solution)/shard_map/ppermute | solution.py:453
  84.8 1.2 %collective-permute-start.12 = (bf16[12,828]{1,0:T(8,128)(2,1)S(1)}, bf16[12,828]{1,0:T(8,128)(2,1)S(1)}, u32[]{:S(2)}, u32[]{:S(2)}) collective-permute-start(bf16[12,828]{1,0:T(8,128)(2,1)S(1)} %bitcast.103), channel_id=1, source_target_pairs={{0,2},{1,3},{2,0},{3,1},{4,6},{5,7},{6,4},{7,5},{8,10},{9,11},{10,... | collective-permute-start | bytes 59624 | tf_op jit(solution)/shard_map/ppermute | solution.py:463
  86.1 3.6 %collective-permute-done.9 = bf16[56,1152]{1,0:T(8,128)(2,1)S(1)} collective-permute-done((bf16[56,1152]{1,0:T(8,128)(2,1)S(1)}, bf16[56,1152]{1,0:T(8,128)(2,1)S(1)}, u32[]{:S(2)}, u32[]{:S(2)}) %collective-permute-start.9) | collective-permute-done | bytes 129056 | tf_op jit(solution)/shard_map/ppermute | solution.py:453
  91.1 4.2 %collective-permute-done.10 = bf16[32,1152]{1,0:T(8,128)(2,1)S(1)} collective-permute-done((bf16[32,1152]{1,0:T(8,128)(2,1)S(1)}, bf16[32,1152]{1,0:T(8,128)(2,1)S(1)}, u32[]{:S(2)}, u32[]{:S(2)}) %collective-permute-start.10) | collective-permute-done | bytes 73760 | tf_op jit(solution)/shard_map/ppermute | solution.py:453
  96.3 0.7 copy.69
  (94 shorter events, 8.7 us)
Async XLA Ops:
  11.8 10.2 %collective-permute-start = (bf16[108,384]{1,0:T(8,128)(2,1)}, bf16[108,384]{1,0:T(8,128)(2,1)S(1)}, u32[]{:S(2)}, u32[]{:S(2)}) collective-permute-start(bf16[108,384]{1,0:T(8,128)(2,1)} %get-tuple-element.23), channel_id=1, source_target_pairs={{0,28},{1,29},{2,30},{3,31},{4,0},{5,1},{6,2},{7,3},{8,4},{9,5},{1... | collective-permute-start | bytes 248840 | tf_op jit(solution)/shard_map/ppermute | solution.py:379
  17.8 2.5 %collective-permute-start.1 = (bf16[36,384]{1,0:T(8,128)(2,1)}, bf16[36,384]{1,0:T(8,128)(2,1)S(1)}, u32[]{:S(2)}, u32[]{:S(2)}) collective-permute-start(bf16[36,384]{1,0:T(8,128)(2,1)} %get-tuple-element.24), channel_id=1, source_target_pairs={{0,3},{1,0},{2,1},{3,2},{4,7},{5,4},{6,5},{7,6},{8,11},{9,8},{10,9... | collective-permute-start | bytes 82952 | tf_op jit(solution)/shard_map/ppermute | solution.py:379
  18.4 3.5 %collective-permute-start.2 = (bf16[36,384]{1,0:T(8,128)(2,1)}, bf16[36,384]{1,0:T(8,128)(2,1)S(1)}, u32[]{:S(2)}, u32[]{:S(2)}) collective-permute-start(bf16[36,384]{1,0:T(8,128)(2,1)} %get-tuple-element.25), channel_id=1, source_target_pairs={{0,31},{1,28},{2,29},{3,30},{4,3},{5,0},{6,1},{7,2},{8,7},{9,4},{1... | collective-permute-start | bytes 82952 | tf_op jit(solution)/shard_map/ppermute | solution.py:379
  20.2 1.7 %copy-start.5 = (bf16[36,384]{1,0:T(8,128)(2,1)}, bf16[36,384]{1,0:T(8,128)(2,1)S(1)}, u32[]{:S(2)}) copy-start(bf16[36,384]{1,0:T(8,128)(2,1)S(1)} %collective-permute-done.1.r_lon) | copy-start | bytes 82948
  22.0 0.6 copy-start.6
  22.0 0.6 copy-start.3
  34.6 8.3 %collective-permute-start.3 = (bf16[108,192]{1,0:T(8,128)(2,1)}, bf16[108,192]{1,0:T(8,128)(2,1)S(1)}, u32[]{:S(2)}, u32[]{:S(2)}) collective-permute-start(bf16[108,192]{1,0:T(8,128)(2,1)} %get-tuple-element.27), channel_id=1, source_target_pairs={{0,4},{1,5},{2,6},{3,7},{4,8},{5,9},{6,10},{7,11},{8,12},{9,13},{1... | collective-permute-start | bytes 124424 | tf_op jit(solution)/shard_map/ppermute | solution.py:379
  35.3 3.4 %collective-permute-start.4 = (bf16[36,192]{1,0:T(8,128)(2,1)}, bf16[36,192]{1,0:T(8,128)(2,1)S(1)}, u32[]{:S(2)}, u32[]{:S(2)}) collective-permute-start(bf16[36,192]{1,0:T(8,128)(2,1)} %get-tuple-element.28), channel_id=1, source_target_pairs={{0,1},{1,2},{2,3},{3,0},{4,5},{5,6},{6,7},{7,4},{8,9},{9,10},{10,1... | collective-permute-start | bytes 41480 | tf_op jit(solution)/shard_map/ppermute | solution.py:379
  35.5 7.4 %collective-permute-start.5 = (bf16[36,192]{1,0:T(8,128)(2,1)}, bf16[36,192]{1,0:T(8,128)(2,1)S(1)}, u32[]{:S(2)}, u32[]{:S(2)}) collective-permute-start(bf16[36,192]{1,0:T(8,128)(2,1)} %get-tuple-element.29), channel_id=1, source_target_pairs={{0,5},{1,6},{2,7},{3,4},{4,9},{5,10},{6,11},{7,8},{8,13},{9,14},{1... | collective-permute-start | bytes 41480 | tf_op jit(solution)/shard_map/ppermute | solution.py:379
  38.8 4.1 %copy-start.7 = (bf16[36,192]{1,0:T(8,128)(2,1)}, bf16[36,192]{1,0:T(8,128)(2,1)S(1)}, u32[]{:S(2)}) copy-start(bf16[36,192]{1,0:T(8,128)(2,1)S(1)} %collective-permute-done.4.r_lon) | copy-start | bytes 41476
  42.9 0.6 copy-start.8
  42.9 0.6 copy-start.4
  43.5 13.7 %copy-start = (bf16[8,4,24,576]{3,2,1,0:T(8,128)(2,1)S(1)}, bf16[8,4,24,576]{3,2,1,0:T(8,128)(2,1)}, u32[]{:S(2)}) copy-start(bf16[8,4,24,576]{3,2,1,0:T(8,128)(2,1)} %get-tuple-element.32) | copy-start | bytes 2654212
  57.2 1.8 %copy-start.9 = (f32[2,192]{1,0:T(2,128)S(1)}, f32[2,192]{1,0:T(2,128)}, u32[]{:S(2)}) copy-start(f32[2,192]{1,0:T(2,128)} %get-tuple-element.34) | copy-start | bytes 4612
  57.2 1.8 %copy-start.10 = (f32[2,192]{1,0:T(2,128)S(1)}, f32[2,192]{1,0:T(2,128)}, u32[]{:S(2)}) copy-start(f32[2,192]{1,0:T(2,128)} %get-tuple-element.33) | copy-start | bytes 4612
  59.3 2.6 %collective-permute-start.6 = (bf16[392,1152]{1,0:T(8,128)(2,1)S(1)}, bf16[392,1152]{1,0:T(8,128)(2,1)}, u32[]{:S(2)}, u32[]{:S(2)}) collective-permute-start(bf16[392,1152]{1,0:T(8,128)(2,1)S(1)} %pad_maximum_fusion.1), channel_id=1, source_target_pairs={{0,1},{1,0},{2,3},{3,2},{4,5},{5,4},{6,7},{7,6},{8,9},{9,8},{10,11... | collective-permute-start | bytes 2709512 | tf_op jit(solution)/shard_map/ppermute | solution.py:453
  63.5 2.2 %copy-start.1 = (f32[24,6,138]{2,1,0:T(8,128)S(1)}, f32[24,6,138]{2,1,0:T(8,128)}, u32[]{:S(2)}) copy-start(f32[24,6,138]{2,1,0:T(8,128)} %get-tuple-element.36) | copy-start | bytes 238468
  63.5 2.2 %copy-start.2 = (f32[24,6,138]{2,1,0:T(8,128)S(1)}, f32[24,6,138]{2,1,0:T(8,128)}, u32[]{:S(2)}) copy-start(f32[24,6,138]{2,1,0:T(8,128)} %get-tuple-element.35) | copy-start | bytes 238468
  64.4 12.7 %collective-permute-start.7 = (bf16[200,1152]{1,0:T(8,128)(2,1)S(1)}, bf16[200,1152]{1,0:T(8,128)(2,1)S(1)}, u32[]{:S(2)}, u32[]{:S(2)}) collective-permute-start(bf16[200,1152]{1,0:T(8,128)(2,1)S(1)} %pad_maximum_fusion.2), channel_id=1, source_target_pairs={{0,2},{1,3},{2,0},{3,1},{4,6},{5,7},{6,4},{7,5},{8,10},{9,11},{10,... | collective-permute-start | bytes 1382408 | tf_op jit(solution)/shard_map/ppermute | solution.py:453
  66.3 11.3 %collective-permute-start.11 = (bf16[2,12,828]{2,0,1:T(2,128)(2,1)S(1)}, bf16[2,12,828]{2,0,1:T(2,128)(2,1)S(1)}, u32[]{:S(2)}, u32[]{:S(2)}) collective-permute-start(bf16[2,12,828]{2,0,1:T(2,128)(2,1)S(1)} %bitcast.102), channel_id=1, source_target_pairs={{0,1},{1,0},{2,3},{3,2},{4,5},{5,4},{6,7},{7,6},{8,9},{9,8},{10,11... | collective-permute-start | bytes 119240 | tf_op jit(solution)/shard_map/ppermute | solution.py:463
  77.4 7.1 %collective-permute-start.8 = (bf16[104,1152]{1,0:T(8,128)(2,1)S(1)}, bf16[104,1152]{1,0:T(8,128)(2,1)S(1)}, u32[]{:S(2)}, u32[]{:S(2)}) collective-permute-start(bf16[104,1152]{1,0:T(8,128)(2,1)S(1)} %pad_maximum_fusion.3), channel_id=1, source_target_pairs={{0,4},{1,5},{2,6},{3,7},{4,0},{5,1},{6,2},{7,3},{8,12},{9,13},{10,... | collective-permute-start | bytes 718856 | tf_op jit(solution)/shard_map/ppermute | solution.py:453
  84.7 5.0 %collective-permute-start.9 = (bf16[56,1152]{1,0:T(8,128)(2,1)S(1)}, bf16[56,1152]{1,0:T(8,128)(2,1)S(1)}, u32[]{:S(2)}, u32[]{:S(2)}) collective-permute-start(bf16[56,1152]{1,0:T(8,128)(2,1)S(1)} %pad_maximum_fusion.4), channel_id=1, source_target_pairs={{0,8},{1,9},{2,10},{3,11},{4,12},{5,13},{6,14},{7,15},{8,0},{9,1},... | collective-permute-start | bytes 387080 | tf_op jit(solution)/shard_map/ppermute | solution.py:453
  84.8 5.6 %collective-permute-start.12 = (bf16[12,828]{1,0:T(8,128)(2,1)S(1)}, bf16[12,828]{1,0:T(8,128)(2,1)S(1)}, u32[]{:S(2)}, u32[]{:S(2)}) collective-permute-start(bf16[12,828]{1,0:T(8,128)(2,1)S(1)} %bitcast.103), channel_id=1, source_target_pairs={{0,2},{1,3},{2,0},{3,1},{4,6},{5,7},{6,4},{7,5},{8,10},{9,11},{10,... | collective-permute-start | bytes 59624 | tf_op jit(solution)/shard_map/ppermute | solution.py:463
  89.8 5.5 %collective-permute-start.10 = (bf16[32,1152]{1,0:T(8,128)(2,1)S(1)}, bf16[32,1152]{1,0:T(8,128)(2,1)S(1)}, u32[]{:S(2)}, u32[]{:S(2)}) collective-permute-start(bf16[32,1152]{1,0:T(8,128)(2,1)S(1)} %pad_maximum_fusion.5), channel_id=1, source_target_pairs={{0,16},{1,17},{2,18},{3,19},{4,20},{5,21},{6,22},{7,23},{8,24},{9,... | collective-permute-start | bytes 221192 | tf_op jit(solution)/shard_map/ppermute | solution.py:453

commit v2 on v1

--- a/solution.py
+++ b/solution.py
@@ -123,9 +123,11 @@
     return value, gain_grad
 
 
-def expand_bias(block, table_ref, row_pick, lane_pick, x_ref, bias_ref, heads, mask):
+def expand_bias(block, table_ref, row_pick, lane_pick, rows_ref, x_ref, bias_ref, heads, mask):
     x_ref[...] = jnp.zeros_like(x_ref)
-    table = table_ref[block]
+    for h in range(heads):
+        rows_ref[h : h + 1, :] = table_ref[block, h]
+    table = rows_ref[0:heads, :]
     piece = WH * SPAN
     for i in range(ZH):
         for zk in range(WZ):
@@ -159,11 +161,18 @@
         total = turned if total is None else total + turned
     back = mm_nt(mm_tn(row_pick[...], total.astype(bf16)).astype(bf16), lane_pick[...])
     piece = WH * SPAN
+    chunk = out_ref.shape[2]
     for i in range(ZH):
         for zk in range(WZ):
             zq, hq = i // WH, i % WH
-            slot = (zq * WZ + zk) * WH + hq
-            out_ref[slot] = back[8 * i : 8 * i + heads, 256 * zk : 256 * zk + piece].astype(out_ref.dtype)
+            start = ((zq * WZ + zk) * WH + hq) * piece
+            at = start
+            while at < start + piece:
+                j = at // chunk
+                end = min(start + piece, (j + 1) * chunk)
+                lane = 256 * zk + at - start
+                out_ref[j, :, at - j * chunk : end - j * chunk] = back[8 * i : 8 * i + heads, lane : lane + end - at]
+                at = end
 
 
 def head_masks(heads, channels):
@@ -176,17 +185,15 @@
     return jnp.where(mask, value, jnp.zeros_like(value))
 
 
-def forward(u, block, gains, w, bias_ref, p_ref, plan):
+def forward(u, block, gains, w, bias_ref, p_ref, plan, outs=None):
     channels, heads = plan.channels, plan.heads
     w_qkv, w_proj, w_fc1, w_fc2 = w
-    gain_one = gains[block, 0:1, :]
-    gain_two = gains[block, 1:2, :]
-    n1, hat1, scale1 = norm(u, gain_one)
+    n1, hat1, scale1 = norm(u, gains[block, 0:1, :])
     qkv_w = w_qkv[block]
     q, k, v = (mm(n1, qkv_w[:, i * channels : (i + 1) * channels]).astype(bf16) for i in range(3))
     masks = head_masks(heads, channels)
     factor = (channels // heads) ** (-0.5)
-    outs = []
+    joined = []
     for n in range(plan.windows):
         rows = slice(n * WT, (n + 1) * WT)
         qw, kw, vw = q[rows], k[rows], v[rows]
@@ -194,35 +201,37 @@
         for h in range(heads):
             s = mm_nt(pick(masks[h], qw), kw) * factor + bias_ref[h]
             e = jnp.exp(s - jnp.max(s, -1, keepdims=True))
-            p = (e / jnp.sum(e, -1, keepdims=True))
-            if p_ref is not None:
-                p_ref[n * heads + h] = p
+            p = e / jnp.sum(e, -1, keepdims=True)
+            p_ref[n * heads + h] = p
             o = mm(p.astype(bf16), pick(masks[h], vw))
             total = o if total is None else total + o
-        outs.append(total.astype(bf16))
-    o = jnp.concatenate(outs, 0)
+        joined.append(total.astype(bf16))
+    o = jnp.concatenate(joined, 0)
     middle = u + mm(o, w_proj[block])
-    n2, hat2, scale2 = norm(middle, gain_two)
+    n2, hat2, scale2 = norm(middle, gains[block, 1:2, :])
     wide = mm(n2, w_fc1[block])
     cdf = 0.5 * (1.0 + lax.erf(wide * (0.5**0.5)))
     g = (wide * cdf).astype(bf16)
-    out = middle + mm(g, w_fc2[block])
-    return out, (n1, hat1, scale1, q, k, v, o, n2, hat2, scale2, wide, cdf, g)
-
-
-def backward(grad, kept, block, gains, w, bias_grad_ref, p_ref, plan):
+    return (n1, hat1, scale1, q, k, v, o, middle, n2, hat2, scale2, wide, cdf, g)
+
+
+def slope(wide, cdf):
+    return cdf + wide * (jnp.exp(-0.5 * wide * wide) * (1.0 / np.sqrt(2.0 * np.pi)))
+
+
+def mlp_back(grad, block, gains, w, hat2, scale2, gelu_slope):
+    _, _, w_fc1, w_fc2 = w
+    dz = grad.astype(bf16)
+    dg = mm(dz, w_fc2[block]).astype(bf16).astype(f32)
+    dh = (dg * gelu_slope).astype(bf16)
+    dn2 = mm_nt(dh, w_fc1[block]).astype(bf16).astype(f32)
+    dmid, gain_grad = norm_back(dn2, hat2, scale2, gains[block, 1:2, :])
+    return grad + dmid, gain_grad, dz, dh
+
+
+def attention_back(dmid, block, gains, w, n1, hat1, scale1, q, k, v, p_ref, bias_grad_ref, plan):
     channels, heads = plan.channels, plan.heads
-    w_qkv, w_proj, w_fc1, w_fc2 = w
-    n1, hat1, scale1, q, k, v, o, n2, hat2, scale2, wide, cdf, g = kept
-    gain_one = gains[block, 0:1, :]
-    gain_two = gains[block, 1:2, :]
-    dz = grad.astype(bf16)
-    dg = mm_nt(dz, w_fc2[block]).astype(bf16).astype(f32)
-    density = jnp.exp(-0.5 * wide * wide) * (1.0 / np.sqrt(2.0 * np.pi))
-    dh = (dg * (cdf + wide * density)).astype(bf16)
-    dn2 = mm_nt(dh, w_fc1[block]).astype(bf16).astype(f32)
-    dmid, gain_grad_two = norm_back(dn2, hat2, scale2, gain_two)
-    dmid = grad + dmid
+    w_qkv, w_proj, _, _ = w
     dp_out = dmid.astype(bf16)
     do = mm_nt(dp_out, w_proj[block]).astype(bf16)
     masks = head_masks(heads, channels)
@@ -256,24 +265,12 @@
         term = mm_nt(part, qkv_w[:, i * channels : (i + 1) * channels])
         dn1 = term if dn1 is None else dn1 + term
     dn1 = dn1.astype(bf16).astype(f32)
-    du, gain_grad_one = norm_back(dn1, hat1, scale1, gain_one)
-    du = dmid + du
-    return du, (gain_grad_one, gain_grad_two), (dq, dk, dv, dp_out, dh, dz)
-
-
-def weight_grads(kept, cots, out_ref):
-    n1, o, n2, g = kept[0], kept[6], kept[7], kept[12]
-    dq, dk, dv, dp_out, dh, dz = cots
-    lat, lon = out_ref.shape[0], out_ref.shape[1]
-    channels = n1.shape[1]
-    rows = channels // lat
-    g_qkv = jnp.concatenate([mm_tn(n1, part) for part in (dq, dk, dv)], 1)
-    g_proj = mm_tn(o, dp_out)
-    g_fc1 = mm_tn(n2, dh)
-    g_fc2 = mm_tn(g, dz)
-    groups = g.shape[1] // channels
-    g_fc2 = g_fc2.reshape(lat, groups, rows, channels)
-    parts = [g_qkv, g_proj, g_fc1] + [g_fc2[:, a].reshape(channels, channels) for a in range(groups)]
+    du, gain_grad = norm_back(dn1, hat1, scale1, gains[block, 0:1, :])
+    return dmid + du, gain_grad, dq, dk, dv, dp_out
+
+
+def put_slices(parts, out_ref):
+    lat, lon, rows = out_ref.shape[:3]
     for j in range(lon):
         pieces = []
         for part in parts:
@@ -284,61 +281,105 @@
             out_ref[i, j] = mine[i * rows : (i + 1) * rows]
 
 
+def attention_weights(n1, o, dq, dk, dv, dp_out):
+    return [jnp.concatenate([mm_tn(n1, part) for part in (dq, dk, dv)], 1), mm_tn(o, dp_out)]
+
+
+def mlp_weights(n2, g, dh, dz, lat):
+    channels = n2.shape[1]
+    groups = g.shape[1] // channels
+    g_fc2 = mm_tn(g, dz).reshape(lat, groups, channels // lat, channels)
+    return [mm_tn(n2, dh)] + [g_fc2[:, a].reshape(channels, channels) for a in range(groups)]
+
+
+KEPT = ("n1", "hat1", "scale1", "q", "k", "v", "o", "n2", "hat2", "scale2", "wide", "cdf", "g")
+
+
 def first_kernel(plan, x, cot, to_order, sel_lat, sel_lon, sel_cor, table, row_pick, lane_pick, w_qkv, w_proj, w_fc1, w_fc2, gains,
-                 s1, m_lat, m_lon, m_cor, x_ref, bias_ref):
+                 s1, m_lat, m_lon, m_cor, p_out, *rest):
+    kept_refs, (rows_ref, x_ref, bias_ref) = rest[:-3], rest[-3:]
     w = (w_qkv, w_proj, w_fc1, w_fc2)
-    expand_bias(0, table, row_pick, lane_pick, x_ref, bias_ref, plan.heads, None)
+    expand_bias(0, table, row_pick, lane_pick, rows_ref, x_ref, bias_ref, plan.heads, None)
     u = mm(to_order[...], x[...])
-    out, _ = forward(u, 0, gains, w, bias_ref, None, plan)
+    kept = forward(u, 0, gains, w, bias_ref, p_out, plan)
+    middle, g = kept[7], kept[13]
+    out = middle + mm_nt(g, w_fc2[0])
     both = jnp.concatenate([out, mm(to_order[...], cot[...])], 1).astype(bf16)
     s1[...] = both
     for message, chosen in ((m_lat, sel_lat), (m_lon, sel_lon), (m_cor, sel_cor)):
         message[...] = mm(chosen[...], both).astype(bf16)
-
-
-def second_kernel(plan, last, s1, r_lat, r_lon, r_cor, roll0, roll1, roll2, roll3, sel_lat, sel_lon, sel_cor,
-                  level_mask, late_mask, table, row_pick, lane_pick, w_qkv, w_proj, w_fc1, w_fc2, gains,
-                  rolled, m_lat, m_lon, m_cor, grads, gain_out, table_out,
-                  x_ref, bias_ref, p_ref, bias_grad_ref, fold_ref):
+    for ref, value in zip(kept_refs, kept[:7] + kept[8:]):
+        ref[...] = value
+
+
+def between_kernel(plan, last, level_mask, late_mask, table, row_pick, lane_pick, wide, cdf, bias_out, slope_out, rows_ref, x_ref):
+    mask = level_mask[...] + late_mask[...] * last[0].astype(f32)
+    expand_bias(1, table, row_pick, lane_pick, rows_ref, x_ref, bias_out, plan.heads, mask)
+    slope_out[...] = slope(wide[...], cdf[...])
+
+
+def second_kernel(plan, s1, r_lat, r_lon, r_cor, roll0, roll1, roll2, roll3, sel_lat, sel_lon, sel_cor,
+                  bias_ref, w_qkv, w_proj, w_fc1, w_fc2, gains,
+                  rolled, m_lat, m_lon, m_cor, gain_out, bias_grad_ref,
+                  n1_out, o_out, n2_out, g_out, dq_out, dk_out, dv_out, dp_out_out, dh_out, dz_out, p_ref):
     w = (w_qkv, w_proj, w_fc1, w_fc2)
     channels = plan.channels
-    mask = level_mask[...] + late_mask[...] * last[0].astype(f32)
-    expand_bias(1, table, row_pick, lane_pick, x_ref, bias_ref, plan.heads, mask)
     both = mm(roll0[...], s1[...]) + mm(roll1[...], r_lat[...]) + mm(roll2[...], r_lon[...]) + mm(roll3[...], r_cor[...])
     u, cot = both[:, :channels], both[:, channels:]
-    _, kept = forward(u, 1, gains, w, bias_ref, p_ref, plan)
-    du, gain_grads, cots = backward(cot, kept, 1, gains, w, bias_grad_ref, p_ref, plan)
+    n1, hat1, scale1, q, k, v, o, middle, n2, hat2, scale2, wide, cdf, g = forward(u, 1, gains, w, bias_ref, p_ref, plan)
+    dmid, gain_two, dz, dh = mlp_back(cot, 1, gains, w, hat2, scale2, slope(wide, cdf))
+    du, gain_one, dq, dk, dv, dp_out = attention_back(dmid, 1, gains, w, n1, hat1, scale1, q, k, v, p_ref, bias_grad_ref, plan)
     du = du.astype(bf16)
     rolled[...] = du
     for message, chosen in ((m_lat, sel_lat), (m_lon, sel_lon), (m_cor, sel_cor)):
         message[...] = mm(chosen[...], du).astype(bf16)
-    gain_out[0:1, :] = gain_grads[0]
-    gain_out[1:2, :] = gain_grads[1]
-    weight_grads(kept, cots, grads)
+    gain_out[0:1, :] = gain_one
+    gain_out[1:2, :] = gain_two
+    for ref, value in ((n1_out, n1), (o_out, o), (n2_out, n2), (g_out, g), (dq_out, dq), (dk_out, dk), (dv_out, dv),
+                       (dp_out_out, dp_out), (dh_out, dh), (dz_out, dz)):
+        ref[...] = value
+
+
+def grads_kernel(plan, n1, o, n2, g, dq, dk, dv, dp_out, dh, dz, bias_grad_ref, row_pick, lane_pick, grads, table_out, fold_ref):
+    parts = attention_weights(n1[...], o[...], dq[...], dk[...], dv[...], dp_out[...])
+    parts += mlp_weights(n2[...], g[...], dh[...], dz[...], grads.shape[0])
+    put_slices(parts, grads)
     fold_bias(bias_grad_ref, row_pick, lane_pick, fold_ref, table_out, plan.heads)
 
 
-def third_kernel(plan, x, rolled, r_lat, r_lon, r_cor, unroll0, unroll1, unroll2, unroll3, to_order, to_natural,
-                 table, row_pick, lane_pick, w_qkv, w_proj, w_fc1, w_fc2, gains,
-                 state_grad, grads, gain_out, table_out,
-                 x_ref, bias_ref, p_ref, bias_grad_ref, fold_ref):
-    w = (w_qkv, w_proj, w_fc1, w_fc2)
-    expand_bias(0, table, row_pick, lane_pick, x_ref, bias_ref, plan.heads, None)
-    u = mm(to_order[...], x[...])
-    _, kept = forward(u, 0, gains, w, bias_ref, p_ref, plan)
+def third_kernel(plan, rolled, r_lat, r_lon, r_cor, unroll0, unroll1, unroll2, unroll3,
+                 n2, hat2, scale2, gelu_slope, g, w_fc1, w_fc2, gains,
+                 dmid_out, gain_out, grads):
     grad = mm(unroll0[...], rolled[...]) + mm(unroll1[...], r_lat[...]) + mm(unroll2[...], r_lon[...]) + mm(unroll3[...], r_cor[...])
-    du, gain_grads, cots = backward(grad, kept, 0, gains, w, bias_grad_ref, p_ref, plan)
+    dmid, gain_two, dz, dh = mlp_back(grad, 0, gains, (None, None, w_fc1, w_fc2), hat2[...], scale2[...], gelu_slope[...])
+    dmid_out[...] = dmid
+    gain_out[...] = gain_two
+    put_slices(mlp_weights(n2[...], g[...], dh, dz, grads.shape[0]), grads)
+
+
+def fourth_kernel(plan, dmid, n1, hat1, scale1, q, k, v, o, p_ref, w_qkv, w_proj, gains, to_natural, row_pick, lane_pick,
+                  state_grad, gain_out, grads, table_out, bias_grad_ref, fold_ref):
+    n1 = n1[...]
+    du, gain_one, dq, dk, dv, dp_out = attention_back(
+        dmid[...], 0, gains, (w_qkv, w_proj, None, None), n1, hat1[...], scale1[...], q[...], k[...], v[...], p_ref, bias_grad_ref, plan)
+    put_slices(attention_weights(n1, o[...], dq, dk, dv, dp_out), grads)
+    gain_out[...] = gain_one
+    fold_bias(bias_grad_ref, row_pick, lane_pick, fold_ref, table_out, plan.heads)
     state_grad[...] = sum(mm(to_natural[...], part) for part in split3(du))
-    gain_out[0:1, :] = gain_grads[0]
-    gain_out[1:2, :] = gain_grads[1]
-    weight_grads(kept, cots, grads)
-    fold_bias(bias_grad_ref, row_pick, lane_pick, fold_ref, table_out, plan.heads)
-
-
-VMEM_LIMIT = 60 * 1024 * 1024
-
-
-def call(body, outs, scratch, args, name, flops, scalar=False):
+
+
+def last_kernel(widths, one_a, one_b, two, qkv, proj, fc1, fc2):
+    w_qkv, w_proj, w_fc1, w_fc2 = widths
+    for b, (attention, mlp) in enumerate(((one_a[...], one_b[...]), (two[:, : w_qkv + w_proj], two[:, w_qkv + w_proj :]))):
+        qkv[b] = attention[:, :w_qkv]
+        proj[b] = attention[:, w_qkv:]
+        fc1[b] = mlp[:, :w_fc1]
+        groups = (mlp.shape[1] - w_fc1) // w_fc2
+        tall = jnp.concatenate([mlp[:, w_fc1 + w_fc2 * a : w_fc1 + w_fc2 * (a + 1)] for a in range(groups)], 0)
+        fc2[b] = tall.T
+
+
+def call(body, outs, scratch, args, name, flops, limit, scalar=False):
     specs = [pl.BlockSpec(memory_space=pltpu.VMEM) for _ in args]
     if scalar:
         specs[0] = pl.BlockSpec(memory_space=pltpu.SMEM)
@@ -350,7 +391,7 @@
         out_specs=[pl.BlockSpec(memory_space=pltpu.VMEM) for _ in outs],
         scratch_shapes=scratch,
         name=name,
-        compiler_params=pltpu.CompilerParams(vmem_limit_bytes=VMEM_LIMIT),
+        compiler_params=pltpu.CompilerParams(vmem_limit_bytes=limit * 1024 * 1024),
         cost_estimate=pl.CostEstimate(flops=flops, bytes_accessed=moved, transcendentals=0),
     )(*args)
 
@@ -364,7 +405,7 @@
     heads = bias_table.shape[3]
     assert levels == WZ and rows == WH and lon % WW == 0
     plan = Plan(lon, heads, channels)
-    tokens = plan.tokens
+    tokens, windows = plan.tokens, plan.windows
     lats, lons = lax.axis_size("lat"), lax.axis_size("lon")
     count = lats * lons
     axes = ("lat", "lon")
@@ -378,105 +419,150 @@
                 pairs.append((a * lons + b, ((a + by_lat) % lats) * lons + (b + by_lon) % lons))
         return lax.ppermute(value, axes, pairs)
 
+    def shape(*dims, kind=bf16):
+        return jax.ShapeDtypeStruct(dims, kind)
+
     x = state.reshape(tokens, channels)
     cot = out_cot.reshape(tokens, channels)
-    table = bias_table.reshape(2, heads, bias_table.shape[-1])
-    weights = (qkv_weight, proj_weight, fc1_weight, fc2_weight)
-    n_lat, n_lon, n_cor = plan.sizes
-    piece = WH * SPAN
+    entries = bias_table.shape[-1]
+    table = bias_table.reshape(2, heads, 1, entries)
+    w_qkv, w_proj, w_fc1 = qkv_weight, proj_weight, fc1_weight
+    w_fc2 = fc2_weight.transpose(0, 2, 1)
+    weights = (w_qkv, w_proj, w_fc1, w_fc2)
     hidden = fc1_weight.shape[-1]
-    columns = sum(a.shape[-1] for a in (qkv_weight, proj_weight, fc1_weight)) // lons + (hidden // channels) * (channels // lons)
-    grad_shape = jax.ShapeDtypeStruct((lats, lons, channels // lats, columns), bf16)
-    gain_shape = jax.ShapeDtypeStruct((2, channels), f32)
-    table_shape = jax.ShapeDtypeStruct((WZ * WZ * WH, heads, piece), f32)
-    bias_scratch = [pltpu.VMEM((8 * ZH, 512), f32), pltpu.VMEM((heads, WT, WT), f32)]
-    back_scratch = bias_scratch + [
-        pltpu.VMEM((plan.windows * heads, WT, WT), f32),
-        pltpu.VMEM((heads, WT, WT), f32),
-        pltpu.VMEM((16 * heads, 384), f32),
-    ]
+    groups = hidden // channels
+    widths = tuple(w.shape[-1] // lons for w in (w_qkv, w_proj, w_fc1)) + (channels // lons,)
+    part_a = widths[0] + widths[1]
+    part_b = widths[2] + groups * widths[3]
+    slice_rows = channels // lats
+    table_shape = shape(lons, heads, entries // lons, kind=f32)
+    bias_shape = shape(heads, WT, WT, kind=f32)
+    expand_scratch = [pltpu.VMEM((8, entries), f32), pltpu.VMEM((8 * ZH, 512), f32)]
+    bias_scratch = pltpu.VMEM((heads, WT, WT), f32)
+    fold_scratch = pltpu.VMEM((16 * heads, 384), f32)
+    wide_f32 = shape(tokens, channels, kind=f32)
+    narrow = shape(tokens, channels)
+    column = shape(tokens, 1, kind=f32)
 
     def messages(width):
-        return [jax.ShapeDtypeStruct((n, width), bf16) for n in plan.sizes]
+        return [shape(n, width) for n in plan.sizes]
 
     flops = 2 * tokens * sum(w.size // 2 for w in weights)
-    s1, *out = call(
+    kept_shapes = [narrow, wide_f32, column, narrow, narrow, narrow, narrow, narrow, wide_f32, column,
+                   shape(tokens, hidden, kind=f32), shape(tokens, hidden, kind=f32), shape(tokens, hidden)]
+    s1, m_lat, m_lon, m_cor, p_one, *kept = call(
         functools.partial(first_kernel, plan),
-        [jax.ShapeDtypeStruct((tokens, 2 * channels), bf16)] + messages(2 * channels),
-        bias_scratch,
+        [shape(tokens, 2 * channels)] + messages(2 * channels) + [shape(windows * heads, WT, WT, kind=f32)] + kept_shapes,
+        expand_scratch + [bias_scratch],
         [x, cot, plan.to_order, *plan.send_down, table, plan.row_pick, plan.lane_pick, *weights, norm_gain],
-        "first", flops,
-    )
-    r_lat = shift(out[0], -1, 0)
-    r_lon = shift(out[1], 0, -1)
-    r_cor = shift(out[2], -1, -1)
+        "first", flops, FIRST,
+    )
+    kept = dict(zip(KEPT, kept))
+    r_lat = shift(m_lat, -1, 0)
+    r_lon = shift(m_lon, 0, -1)
+    r_cor = shift(m_cor, -1, -1)
     last = (lat == lats - 1).astype(jnp.int32).reshape(1)
-    rolled, *out = call(
+    bias_two, gelu_slope = call(
+        functools.partial(between_kernel, plan),
+        [bias_shape, shape(tokens, hidden, kind=f32)],
+        expand_scratch,
+        [last, plan.level_mask, plan.late_mask, table, plan.row_pick, plan.lane_pick, kept["wide"], kept["cdf"]],
+        "between", flops, BETWEEN, True,
+    )
+    rolled, m_lat, m_lon, m_cor, gain_two, bias_grad, *saved = call(
         functools.partial(second_kernel, plan),
-        [jax.ShapeDtypeStruct((tokens, channels), bf16)] + messages(channels) + [grad_shape, gain_shape, table_shape],
-        back_scratch,
-        [last, s1, r_lat, r_lon, r_cor, *plan.roll, *plan.send_up, plan.level_mask, plan.late_mask,
-         table, plan.row_pick, plan.lane_pick, *weights, norm_gain],
-        "second", 3 * flops, True,
-    )
-    r_lat = shift(out[0], 1, 0)
-    r_lon = shift(out[1], 0, 1)
-    r_cor = shift(out[2], 1, 1)
-    grads_two, gain_two, table_two = out[3:]
-    state_grad, grads_one, gain_one, table_one = call(
+        [narrow] + messages(channels) + [shape(2, channels, kind=f32), bias_shape]
+        + [narrow, narrow, narrow, shape(tokens, hidden), narrow, narrow, narrow, narrow, shape(tokens, hidden), narrow],
+        [pltpu.VMEM((windows * heads, WT, WT), f32)],
+        [s1, r_lat, r_lon, r_cor, *plan.roll, *plan.send_up, bias_two, *weights, norm_gain],
+        "second", 2 * flops, SECOND,
+    )
+    r_lat = shift(m_lat, 1, 0)
+    r_lon = shift(m_lon, 0, 1)
+    r_cor = shift(m_cor, 1, 1)
+    grads_two, table_two = call(
+        functools.partial(grads_kernel, plan),
+        [shape(lats, lons, slice_rows, part_a + part_b), table_shape],
+        [fold_scratch],
+        [*saved, bias_grad, plan.row_pick, plan.lane_pick],
+        "grads", flops, GRADS,
+    )
+    dmid, gain_one_b, grads_one_b = call(
         functools.partial(third_kernel, plan),
-        [jax.ShapeDtypeStruct((tokens, channels), f32), grad_shape, gain_shape, table_shape],
-        back_scratch,
-        [x, rolled, r_lat, r_lon, r_cor, *plan.unroll, plan.to_order, plan.to_natural,
-         table, plan.row_pick, plan.lane_pick, *weights, norm_gain],
-        "third", 3 * flops,
+        [wide_f32, shape(1, channels, kind=f32), shape(lats, lons, slice_rows, part_b)],
+        [],
+        [rolled, r_lat, r_lon, r_cor, *plan.unroll, kept["n2"], kept["hat2"], kept["scale2"], gelu_slope, kept["g"],
+         w_fc1, w_fc2, norm_gain],
+        "third", flops, THIRD,
+    )
+    state_grad, gain_one_a, grads_one_a, table_one = call(
+        functools.partial(fourth_kernel, plan),
+        [wide_f32, shape(1, channels, kind=f32), shape(lats, lons, slice_rows, part_a), table_shape],
+        [bias_scratch, fold_scratch],
+        [dmid, kept["n1"], kept["hat1"], kept["scale1"], kept["q"], kept["k"], kept["v"], kept["o"], p_one,
+         w_qkv, w_proj, norm_gain, plan.to_natural, plan.row_pick, plan.lane_pick],
+        "fourth", flops, FOURTH,
     )
 
     bits = count.bit_length() - 1
     lon_bits = lons.bit_length() - 1
-    size = grad_shape.shape[2:]
-    held = jnp.concatenate((grads_one, grads_two), -1).reshape((2,) * bits + (size[0], 2 * size[1]))
-    gain = jnp.concatenate((gain_one, gain_two), 0)
-    tables = jnp.stack((table_one, table_two)).transpose(0, 2, 1, 3).reshape(2 * heads, lons, -1)
-    tables = tables.transpose(1, 0, 2).reshape((2,) * lon_bits + (2 * heads, -1))
-    for bit in range(bits):
+
+    def exchange(value, bit):
+        return lax.ppermute(value, axes, [(i, i ^ (1 << bit)) for i in range(count)])
+
+    def halves(held, bit):
         mine = (me >> bit) & 1
-        pairs = [(i, i ^ (1 << bit)) for i in range(count)]
         axis = held.ndim - 3
         keep = lax.dynamic_index_in_dim(held, mine, axis, keepdims=False)
         send = lax.dynamic_index_in_dim(held, 1 - mine, axis, keepdims=False)
+        return keep.astype(f32), send.astype(bf16)
+
+    def scatter(value, first, stop, whole):
+        for bit in range(first, stop):
+            keep, send = halves(value, bit)
+            value = keep + exchange(send, bit).astype(f32)
+            if bit < whole - 1:
+                value = value.astype(bf16)
+        return value
+
+    def split(value, how_many):
+        return value.reshape((2,) * how_many + value.shape[-2:])
+
+    gain = jnp.concatenate((gain_one_a, gain_one_b, gain_two), 0)
+    two = scatter(split(grads_two, bits), 0, bits, bits)
+    one_b = scatter(split(grads_one_b, bits), 0, 1, bits)
+    one_a = split(grads_one_a, bits)
+    tables = [scatter(split(t, lon_bits), 0, lon_bits, lon_bits) for t in (table_one, table_two)]
+    for bit in range(bits):
+        keep, send = halves(one_a, bit)
         high = rounded(gain)
         low = rounded(gain - high)
         extra = jnp.concatenate((high, low), 0).astype(bf16)
-        extra = jnp.pad(extra, ((0, 0), (0, 2 * size[1] - channels)))
-        message = jnp.concatenate((send.astype(bf16).reshape(-1, 2 * size[1]), extra), 0)
-        got = lax.ppermute(message, axes, pairs)
-        other = got[-8:, :channels].astype(f32)
+        flat = jnp.pad(extra.reshape(-1), (0, -extra.size % part_a)).reshape(-1, part_a)
+        got = exchange(jnp.concatenate((send.reshape(-1, part_a), flat), 0), bit)
+        other = got[-flat.shape[0] :].reshape(-1)[: extra.size].reshape(extra.shape).astype(f32)
         gain = (high + low) + (other[:4] + other[4:])
-        held = keep.astype(f32) + got[:-8].reshape(keep.shape).astype(f32)
+        one_a = keep + got[: -flat.shape[0]].reshape(keep.shape).astype(f32)
         if bit < bits - 1:
-            held = held.astype(bf16)
-        if bit < lon_bits:
-            axis = tables.ndim - 3
-            keep = lax.dynamic_index_in_dim(tables, mine, axis, keepdims=False)
-            send = lax.dynamic_index_in_dim(tables, 1 - mine, axis, keepdims=False)
-            tables = keep + lax.ppermute(send.astype(bf16), axes, pairs).astype(f32)
-
-    cuts, start = [], 0
-    widths = [w.shape[-1] // lons for w in (qkv_weight, proj_weight, fc1_weight)] + [channels // lons] * (hidden // channels)
-    for width in widths:
-        cuts.append(jnp.stack((held[:, start : start + width], held[:, size[1] + start : size[1] + start + width])))
-        start += width
-    fc2 = jnp.concatenate(cuts[3:], 1)
+            one_a = one_a.astype(bf16)
+    one_b = scatter(one_b, 1, bits, bits)
+    qkv, proj, fc1, fc2 = call(
+        functools.partial(last_kernel, widths),
+        [shape(2, slice_rows, n, kind=f32) for n in widths[:3]] + [shape(2, widths[3], groups * slice_rows, kind=f32)],
+        [], [one_a, one_b, two], "last", 1000, 4,
+    )
     return (
         state_grad.reshape(state.shape),
-        cuts[0],
-        cuts[1],
-        cuts[2],
-        fc2,
+        qkv,
+        proj,
+        fc1,
+        fc2.transpose(0, 2, 1),
         gain.reshape(2, 2, channels),
-        tables.reshape(2, 1, 1, heads, -1),
-    )
+        jnp.stack(tables).reshape(2, 1, 1, heads, -1),
+    )
+
+
+FIRST, BETWEEN, SECOND, GRADS, THIRD, FOURTH = 8, 8, 8, 8, 8, 8
 
 
 def solution(mesh):

time: 99.2 us -> 118 us (1.19)
  local copies, waits for them, and re-layouts: 9.88 us -> 30 us
  starting transfers between devices: 12 us -> 28 us
  waiting for transfers between devices: 37.8 us -> 29.9 us
  Pallas kernels: 32.9 us -> 25.5 us
  other arithmetic: 5.27 us -> 1.7 us
    unnamed x27 -> x143, local copies, waits for them, and re-layouts: 5.26 us -> 28.2 us
    ppermute x7 -> x19, starting transfers between devices: 3.35 us -> 18.4 us  [exchange(): return lax.ppermute(value, axes, [(i, i ^ 1 << bit) for i in range(count)])]
    ppermute x6, waiting for transfers between devices: 9.84 us -> 2.09 us  [shift(): return lax.ppermute(value, axes, pairs)]
    pallas_call x3 -> x7, Pallas kernels: 32.9 us -> 25.5 us  [call(): pl.pallas_call(body, out_shape=outs, in_specs=specs, out_specs=[pl.BlockS...]
    another operation x12 -> x9, other arithmetic: 1.95 us -> 0.09 us  [the longest x3 1.86 us: body(): jnp.stack((held[:, start:start + width], held[:, size[1] + start:size[1]...]
    concatenate x12 -> x5, other arithmetic: 1.96 us -> 0.1 us  [body(): got = exchange(jnp.concatenate((send.reshape(-1, part_a), flat), 0), bit)]
    reshape x4 -> x0, local copies, waits for them, and re-layouts: 1.73 us -> none  [the longest x1 0.72 us: body(): table = bias_table.reshape(2, heads, bias_table.shape[-1])]
    slice x4, local copies, waits for them, and re-layouts: 1.3 us -> 0.03 us  [body(): one_a = keep + got[:-flat.shape[0]].reshape(keep.shape).astype(f32)]
  transfers between devices with their start and end apart: 13 -> 25, of which waited for: 9 -> 15; matrix products, arithmetic and copies ran while one was open for 2% -> 2% of each run, Pallas kernels for 0% -> 8%
where the time goes in v2:
time: 118 us; the launch traced here: 117 us
  local copies, waits for them, and re-layouts  30 us (25%)
  waiting for transfers between devices  29.9 us (25%)
  starting transfers between devices  28 us (24%)
  Pallas kernels  25.5 us (22%)
  other arithmetic  1.7 us (1%)
  between operations  1.65 us (1%)
    unnamed x143, local copies, waits for them, and re-layouts  28.2 us
    ppermute x19, waiting for transfers between devices, exchange(): return lax.ppermute(value, axes, [(i, i ^ 1 << bit) for i in range(count)])  27.8 us
    pallas_call x7, Pallas kernels, call(): pl.pallas_call(body, out_shape=outs, in_specs=specs, out_specs=[pl.BlockS...  25.5 us
    ppermute x19, starting transfers between devices, exchange(): return lax.ppermute(value, axes, [(i, i ^ 1 << bit) for i in range(count)])  18.4 us
    ppermute x6, starting transfers between devices, shift(): return lax.ppermute(value, axes, pairs)  9.62 us
  transfers between devices with their start and end apart: 25, of which 15 were waited for; matrix products, arithmetic and copies ran while one was open for 2% of the time, Pallas kernels for 8%

profile of v2, /device:TPU:0, one launch (start us, length us, event | category | flops | bytes accessed | tf_op | source)
XLA Modules:
  0.0 116.8 jit_solution(4703961569796738286)
XLA Ops:
  13.2 5.2 %first.1 = (bf16[288,384]{1,0:T(8,128)(2,1)S(1)}, bf16[108,384]{1,0:T(8,128)(2,1)}, bf16[36,384]{1,0:T(8,128)(2,1)}, bf16[36,384]{1,0:T(8,128)(2,1)}, f32[12,144...) custom-call(bf16[288,192]{1,0:T(8,128)(2,1)S(1)} %bitcast.139, ...), custom_call_target="tpu_custom_call" | custom-call | flops 254803968 | bytes 2833920 | tf_op jit(solution)/shard_map/first/pallas_call | solution.py:387
  28.8 6.1 %collective-permute-start = (bf16[108,384]{1,0:T(8,128)(2,1)}, bf16[108,384]{1,0:T(8,128)(2,1)}, u32[]{:S(2)}, u32[]{:S(2)}) collective-permute-start(bf16[108,384]{1,0:T(8,128)(2,1)} %get-tuple-element.57), channel_id=1, source_target_pairs={{0,28},{1,29},{2,30},{3,31},{4,0},{5,1},{6,2},{7,3},{8,4},{9,5},{1... | collective-permute-start | bytes 248840 | tf_op jit(solution)/shard_map/ppermute | solution.py:420
  39.5 1.6 %between.1 = (f32[6,144,144]{2,1,0:T(8,128)S(1)}, f32[288,768]{1,0:T(8,128)S(1)}) custom-call(s32[1]{0:T(128)} %bitcast.4.last, f32[144,144]{1,0:T(8,128)S(1)} %copy-done.40, f32[144,144]{1,0:T(8,128)S(1)} %copy-done.41, f32[2,6,1,3312]{3,2,1,0:T(1,128)S(1)} %bitcast.136, bf16[96,96]{1,0:T(8,128)(2,1)S(1)} %copy-done.21, bf16[512,384]{1,0:T(8,128)(2,1)S(1)} %copy-done.1, ...), custom_call_target="tpu_custom_call" | custom-call | flops 254803968 | bytes 2505988 | tf_op jit(solution)/shard_map/between/pallas_call | solution.py:387
  42.2 8.1 %second.1 = (bf16[288,192]{1,0:T(8,128)(2,1)S(1)}, bf16[108,192]{1,0:T(8,128)(2,1)S(1)}, bf16[36,192]{1,0:T(8,128)(2,1)S(1)}, bf16[36,192]{1,0:T(8,128)(2,1)S(1)...) custom-call(bf16[288,384]{1,0:T(8,128)(2,1)S(1)} %copy-done.30, ...), custom_call_target="tpu_custom_call" | custom-call | flops 509607936 | bytes 3002880 | tf_op jit(solution)/shard_map/second/pallas_call | solution.py:387
  50.4 1.7 %grads.1 = (bf16[8,4,24,576]{3,2,1,0:T(8,128)(2,1)S(1)}, f32[4,6,828]{2,1,0:T(8,128)S(1)}) custom-call(bf16[288,192]{1,0:T(8,128)(2,1)S(1)} %get-tuple-element.87.n1, bf16[288,192]{1,0:T(8,128)(2,1)S(1)} %get-tuple-element.88.o, bf16[288,192]{1,0:T(8,128)(2,1)S(1)} %get-tuple-element.89.n2, bf16[288,768]{1,0:T(8,128)(2,1)S(1)} %get-tuple-element.90.g, ...), custom_call_target="tpu_custom_call" | custom-call | flops 254803968 | bytes 2678784 | tf_op jit(solution)/shard_map/grads/pallas_call | solution.py:387
  53.5 1.5 %collective-permute-start.3 = (bf16[108,192]{1,0:T(8,128)(2,1)S(1)}, bf16[108,192]{1,0:T(8,128)(2,1)S(1)}, u32[]{:S(2)}, u32[]{:S(2)}) collective-permute-start(bf16[108,192]{1,0:T(8,128)(2,1)S(1)} %get-tuple-element.64), channel_id=1, source_target_pairs={{0,4},{1,5},{2,6},{3,7},{4,8},{5,9},{6,10},{7,11},{8,12},{9,13},{1... | collective-permute-start | bytes 124424 | tf_op jit(solution)/shard_map/ppermute | solution.py:420
  56.3 1.5 %collective-permute-start.24 = (bf16[6,828]{1,0:T(8,128)(2,1)S(1)}, bf16[6,828]{1,0:T(8,128)(2,1)S(1)}, u32[]{:S(2)}, u32[]{:S(2)}) collective-permute-start(bf16[6,828]{1,0:T(8,128)(2,1)S(1)} %dynamic-slice_bitcast_fusion.8), channel_id=1, source_target_pairs={{0,2},{1,3},{2,0},{3,1},{4,6},{5,7},{6,4},{7,5},{8,10},{9,11},{10,... | collective-permute-start | bytes 29816 | tf_op jit(solution)/shard_map/ppermute | solution.py:511
  58.0 2.1 %collective-permute-done.24 = bf16[6,828]{1,0:T(8,128)(2,1)S(1)} collective-permute-done((bf16[6,828]{1,0:T(8,128)(2,1)S(1)}, bf16[6,828]{1,0:T(8,128)(2,1)S(1)}, u32[]{:S(2)}, u32[]{:S(2)}) %collective-permute-start.24) | collective-permute-done | bytes 9968 | tf_op jit(solution)/shard_map/ppermute | solution.py:511
  60.1 2.1 %collective-permute-done.5.r_cor = bf16[36,192]{1,0:T(8,128)(2,1)S(1)} collective-permute-done((bf16[36,192]{1,0:T(8,128)(2,1)}, bf16[36,192]{1,0:T(8,128)(2,1)S(1)}, u32[]{:S(2)}, u32[]{:S(2)}) %collective-permute-start.5) | collective-permute-done | bytes 13856 | tf_op jit(solution)/shard_map/ppermute | solution.py:420
  62.4 2.0 %third.1 = (f32[288,192]{1,0:T(8,128)S(1)}, f32[1,192]{1,0:T(1,128)S(1)}, bf16[8,4,24,384]{3,2,1,0:T(8,128)(2,1)S(1)}) custom-call(bf16[288,192]{1,0:T(8,128)(2,1)S(1)} %copy-done.39, bf16[108,192]{1,0:T(8,128)(2,1)S(1)} %collective-permute-done.3.r_lat, bf16[36,192]{1,0:T(8,128)(2,1)S(1)} %collective-permute-done.4.r_lon, ...), custom_call_target="tpu_custom_call" | custom-call | flops 254803968 | bytes 3292032 | tf_op jit(solution)/shard_map/third/pallas_call | solution.py:387
  64.5 6.0 %fourth.1 = (f32[288,192]{1,0:T(8,128)}, f32[1,192]{1,0:T(1,128)S(1)}, bf16[8,4,24,192]{3,2,1,0:T(8,128)(2,1)S(1)}, f32[4,6,828]{2,1,0:T(8,128)S(1)}) custom-call(f32[288,192]{1,0:T(8,128)S(1)} %get-tuple-element.72.dmid, bf16[288,192]{1,0:T(8,128)(2,1)S(1)} %copy-done.43, f32[288,192]{1,0:T(8,128)S(1)} %copy-done.25, f32[288,1]{1,0:T(8,128)S(1)} %copy-done.45, ...), custom_call_target="tpu_custom_call" | custom-call | flops 254803968 | bytes 3162240 | tf_op jit(solution)/shard_map/fourth/pallas_call | solution.py:387
  74.5 3.3 %collective-permute-done.7 = bf16[200,192]{1,0:T(8,128)(2,1)S(1)} collective-permute-done((bf16[200,192]{1,0:T(8,128)(2,1)S(1)}, bf16[200,192]{1,0:T(8,128)(2,1)S(1)}, u32[]{:S(2)}, u32[]{:S(2)}) %collective-permute-start.7) | collective-permute-done | bytes 76832 | tf_op jit(solution)/shard_map/ppermute | solution.py:511
  78.1 4.1 %collective-permute-done.8 = bf16[104,192]{1,0:T(8,128)(2,1)S(1)} collective-permute-done((bf16[104,192]{1,0:T(8,128)(2,1)S(1)}, bf16[104,192]{1,0:T(8,128)(2,1)S(1)}, u32[]{:S(2)}, u32[]{:S(2)}) %collective-permute-start.8) | collective-permute-done | bytes 39968 | tf_op jit(solution)/shard_map/ppermute | solution.py:511
  83.1 3.1 %collective-permute-done.9 = bf16[56,192]{1,0:T(8,128)(2,1)S(1)} collective-permute-done((bf16[56,192]{1,0:T(8,128)(2,1)S(1)}, bf16[56,192]{1,0:T(8,128)(2,1)S(1)}, u32[]{:S(2)}, u32[]{:S(2)}) %collective-permute-start.9) | collective-permute-done | bytes 21536 | tf_op jit(solution)/shard_map/ppermute | solution.py:511
  86.6 1.6 %collective-permute-start.12 = (bf16[2,2,2,24,384]{4,3,0,1,2:T(8,128)(2,1)S(1)}, bf16[2,2,2,24,384]{4,3,0,1,2:T(8,128)(2,1)S(1)}, u32[]{:S(2)}, u32[]{:S(2)}) collective-permute-start(bf16[2,2,2,24,384]{4,3,0,1,2:T(8,128)(2,1)S(1)} %dynamic-slice_bitcast_fusion.1), channel_id=1, source_target_pairs={{0,2},{1,3},{2,0},{3,1},{4,6},{5,7},{6,4},{7,5},{8,10},{9,11},{10,... | collective-permute-start | bytes 442376 | tf_op jit(solution)/shard_map/ppermute | solution.py:511
  88.2 2.8 %collective-permute-done.10 = bf16[32,192]{1,0:T(8,128)(2,1)S(1)} collective-permute-done((bf16[32,192]{1,0:T(8,128)(2,1)S(1)}, bf16[32,192]{1,0:T(8,128)(2,1)S(1)}, u32[]{:S(2)}, u32[]{:S(2)}) %collective-permute-start.10) | collective-permute-done | bytes 12320 | tf_op jit(solution)/shard_map/ppermute | solution.py:511
  91.9 2.5 %collective-permute-start.13 = (bf16[2,2,24,384]{3,2,0,1:T(8,128)(2,1)S(1)}, bf16[2,2,24,384]{3,2,0,1:T(8,128)(2,1)S(1)}, u32[]{:S(2)}, u32[]{:S(2)}) collective-permute-start(bf16[2,2,24,384]{3,2,0,1:T(8,128)(2,1)S(1)} %dynamic-slice_bitcast_fusion.3), channel_id=1, source_target_pairs={{0,4},{1,5},{2,6},{3,7},{4,0},{5,1},{6,2},{7,3},{8,12},{9,13},{10,... | collective-permute-start | bytes 221192 | tf_op jit(solution)/shard_map/ppermute | solution.py:511
  94.5 1.6 %collective-permute-start.17 = (bf16[2,2,2,24,576]{4,3,0,1,2:T(8,128)(2,1)S(1)}, bf16[2,2,2,24,576]{4,3,0,1,2:T(8,128)(2,1)S(1)}, u32[]{:S(2)}, u32[]{:S(2)}) collective-permute-start(bf16[2,2,2,24,576]{4,3,0,1,2:T(8,128)(2,1)S(1)} %dynamic-slice_bitcast_fusion), channel_id=1, source_target_pairs={{0,2},{1,3},{2,0},{3,1},{4,6},{5,7},{6,4},{7,5},{8,10},{9,11},{10,... | collective-permute-start | bytes 663560 | tf_op jit(solution)/shard_map/ppermute | solution.py:511
  96.8 2.5 %collective-permute-start.14 = (bf16[2,24,384]{2,1,0:T(8,128)(2,1)S(1)}, bf16[2,24,384]{2,1,0:T(8,128)(2,1)S(1)}, u32[]{:S(2)}, u32[]{:S(2)}) collective-permute-start(bf16[2,24,384]{2,1,0:T(8,128)(2,1)S(1)} %dynamic-slice_bitcast_fusion.5), channel_id=1, source_target_pairs={{0,8},{1,9},{2,10},{3,11},{4,12},{5,13},{6,14},{7,15},{8,0},{9,1},... | collective-permute-start | bytes 110600 | tf_op jit(solution)/shard_map/ppermute | solution.py:511
  101.9 3.8 %collective-permute-done.18 = bf16[2,2,24,576]{3,2,0,1:T(8,128)(2,1)S(1)} collective-permute-done((bf16[2,2,24,576]{3,2,0,1:T(8,128)(2,1)S(1)}, bf16[2,2,24,576]{3,2,0,1:T(8,128)(2,1)S(1)}, u32[]{:S(2)}, u32[]{:S(2)}) %collective-permute-start.18) | collective-permute-done | bytes 110624 | tf_op jit(solution)/shard_map/ppermute | solution.py:511
  105.8 2.4 %collective-permute-start.19 = (bf16[2,24,576]{2,1,0:T(8,128)(2,1)S(1)}, bf16[2,24,576]{2,1,0:T(8,128)(2,1)S(1)}, u32[]{:S(2)}, u32[]{:S(2)}) collective-permute-start(bf16[2,24,576]{2,1,0:T(8,128)(2,1)S(1)} %dynamic-slice_bitcast_fusion.4), channel_id=1, source_target_pairs={{0,8},{1,9},{2,10},{3,11},{4,12},{5,13},{6,14},{7,15},{8,0},{9,1},... | collective-permute-start | bytes 165896 | tf_op jit(solution)/shard_map/ppermute | solution.py:511
  108.7 1.7 %collective-permute-done.19 = bf16[2,24,576]{2,1,0:T(8,128)(2,1)S(1)} collective-permute-done((bf16[2,24,576]{2,1,0:T(8,128)(2,1)S(1)}, bf16[2,24,576]{2,1,0:T(8,128)(2,1)S(1)}, u32[]{:S(2)}, u32[]{:S(2)}) %collective-permute-start.19) | collective-permute-done | bytes 55328 | tf_op jit(solution)/shard_map/ppermute | solution.py:511
  110.4 1.6 %collective-permute-start.20 = (bf16[24,576]{1,0:T(8,128)(2,1)S(1)}, bf16[24,576]{1,0:T(8,128)(2,1)S(1)}, u32[]{:S(2)}, u32[]{:S(2)}) collective-permute-start(bf16[24,576]{1,0:T(8,128)(2,1)S(1)} %dynamic-slice_bitcast_fusion.6), channel_id=1, source_target_pairs={{0,16},{1,17},{2,18},{3,19},{4,20},{5,21},{6,22},{7,23},{8,24},{9,... | collective-permute-start | bytes 82952 | tf_op jit(solution)/shard_map/ppermute | solution.py:511
  112.9 2.4 %collective-permute-done.20 = bf16[24,576]{1,0:T(8,128)(2,1)S(1)} collective-permute-done((bf16[24,576]{1,0:T(8,128)(2,1)S(1)}, bf16[24,576]{1,0:T(8,128)(2,1)S(1)}, u32[]{:S(2)}, u32[]{:S(2)}) %collective-permute-start.20) | collective-permute-done | bytes 27680 | tf_op jit(solution)/shard_map/ppermute | solution.py:511
  (246 shorter events, 43.9 us)
Async XLA Ops:
  28.8 13.3 %collective-permute-start = (bf16[108,384]{1,0:T(8,128)(2,1)}, bf16[108,384]{1,0:T(8,128)(2,1)}, u32[]{:S(2)}, u32[]{:S(2)}) collective-permute-start(bf16[108,384]{1,0:T(8,128)(2,1)} %get-tuple-element.57), channel_id=1, source_target_pairs={{0,28},{1,29},{2,30},{3,31},{4,0},{5,1},{6,2},{7,3},{8,4},{9,5},{1... | collective-permute-start | bytes 248840 | tf_op jit(solution)/shard_map/ppermute | solution.py:420
  34.8 7.3 %collective-permute-start.1 = (bf16[36,384]{1,0:T(8,128)(2,1)}, bf16[36,384]{1,0:T(8,128)(2,1)}, u32[]{:S(2)}, u32[]{:S(2)}) collective-permute-start(bf16[36,384]{1,0:T(8,128)(2,1)} %get-tuple-element.58), channel_id=1, source_target_pairs={{0,3},{1,0},{2,1},{3,2},{4,7},{5,4},{6,5},{7,6},{8,11},{9,8},{10,9... | collective-permute-start | bytes 82952 | tf_op jit(solution)/shard_map/ppermute | solution.py:420
  35.5 6.6 %collective-permute-start.2 = (bf16[36,384]{1,0:T(8,128)(2,1)}, bf16[36,384]{1,0:T(8,128)(2,1)}, u32[]{:S(2)}, u32[]{:S(2)}) collective-permute-start(bf16[36,384]{1,0:T(8,128)(2,1)} %get-tuple-element.59), channel_id=1, source_target_pairs={{0,31},{1,28},{2,29},{3,30},{4,3},{5,0},{6,1},{7,2},{8,7},{9,4},{1... | collective-permute-start | bytes 82952 | tf_op jit(solution)/shard_map/ppermute | solution.py:420
  53.4 2.1 %collective-permute-start.23 = (bf16[2,6,828]{2,1,0:T(8,128)(2,1)}, bf16[2,6,828]{2,1,0:T(8,128)(2,1)}, u32[]{:S(2)}, u32[]{:S(2)}) collective-permute-start(bf16[2,6,828]{2,1,0:T(8,128)(2,1)} %fusion.15), channel_id=1, source_target_pairs={{0,1},{1,0},{2,3},{3,2},{4,5},{5,4},{6,7},{7,6},{8,9},{9,8},{10,11... | collective-permute-start | bytes 59624 | tf_op jit(solution)/shard_map/ppermute | solution.py:511
  53.5 8.7 %collective-permute-start.3 = (bf16[108,192]{1,0:T(8,128)(2,1)S(1)}, bf16[108,192]{1,0:T(8,128)(2,1)S(1)}, u32[]{:S(2)}, u32[]{:S(2)}) collective-permute-start(bf16[108,192]{1,0:T(8,128)(2,1)S(1)} %get-tuple-element.64), channel_id=1, source_target_pairs={{0,4},{1,5},{2,6},{3,7},{4,8},{5,9},{6,10},{7,11},{8,12},{9,13},{1... | collective-permute-start | bytes 124424 | tf_op jit(solution)/shard_map/ppermute | solution.py:420
  55.0 5.1 %collective-permute-start.4 = (bf16[36,192]{1,0:T(8,128)(2,1)}, bf16[36,192]{1,0:T(8,128)(2,1)S(1)}, u32[]{:S(2)}, u32[]{:S(2)}) collective-permute-start(bf16[36,192]{1,0:T(8,128)(2,1)} %copy-done.70), channel_id=1, source_target_pairs={{0,1},{1,2},{2,3},{3,0},{4,5},{5,6},{6,7},{7,4},{8,9},{9,10},{10,1... | collective-permute-start | bytes 41480 | tf_op jit(solution)/shard_map/ppermute | solution.py:420
  55.2 7.0 %collective-permute-start.5 = (bf16[36,192]{1,0:T(8,128)(2,1)}, bf16[36,192]{1,0:T(8,128)(2,1)S(1)}, u32[]{:S(2)}, u32[]{:S(2)}) collective-permute-start(bf16[36,192]{1,0:T(8,128)(2,1)} %copy-done.69), channel_id=1, source_target_pairs={{0,5},{1,6},{2,7},{3,4},{4,9},{5,10},{6,11},{7,8},{8,13},{9,14},{1... | collective-permute-start | bytes 41480 | tf_op jit(solution)/shard_map/ppermute | solution.py:420
  56.3 3.8 %collective-permute-start.24 = (bf16[6,828]{1,0:T(8,128)(2,1)S(1)}, bf16[6,828]{1,0:T(8,128)(2,1)S(1)}, u32[]{:S(2)}, u32[]{:S(2)}) collective-permute-start(bf16[6,828]{1,0:T(8,128)(2,1)S(1)} %dynamic-slice_bitcast_fusion.8), channel_id=1, source_target_pairs={{0,2},{1,3},{2,0},{3,1},{4,6},{5,7},{6,4},{7,5},{8,10},{9,11},{10,... | collective-permute-start | bytes 29816 | tf_op jit(solution)/shard_map/ppermute | solution.py:511
  57.9 33.1 %collective-permute-start.16 = (bf16[2,2,2,2,24,576]{5,4,0,1,2,3:T(8,128)(2,1)S(1)}, bf16[2,2,2,2,24,576]{5,4,0,1,2,3:T(8,128)(2,1)S(1)}, u32[]{:S(2)}, u32[]{:S(2)}) collective-permute-start(bf16[2,2,2,2,24,576]{5,4,0,1,2,3:T(8,128)(2,1)S(1)} %bitcast.147), channel_id=1, source_target_pairs={{0,1},{1,0},{2,3},{3,2},{4,5},{5,4},{6,7},{7,6},{8,9},{9,8},{10,11... | collective-permute-start | bytes 1327112 | tf_op jit(solution)/shard_map/ppermute | solution.py:511
  70.6 1.6 %collective-permute-start.6 = (bf16[392,192]{1,0:T(8,128)(2,1)S(1)}, bf16[392,192]{1,0:T(8,128)(2,1)S(1)}, u32[]{:S(2)}, u32[]{:S(2)}) collective-permute-start(bf16[392,192]{1,0:T(8,128)(2,1)S(1)} %pad_maximum_fusion), channel_id=1, source_target_pairs={{0,1},{1,0},{2,3},{3,2},{4,5},{5,4},{6,7},{7,6},{8,9},{9,8},{10,11... | collective-permute-start | bytes 451592 | tf_op jit(solution)/shard_map/ppermute | solution.py:511
  71.3 15.2 %collective-permute-start.11 = (bf16[2,2,2,2,24,384]{5,4,0,1,2,3:T(8,128)(2,1)S(1)}, bf16[2,2,2,2,24,384]{5,4,0,1,2,3:T(8,128)(2,1)S(1)}, u32[]{:S(2)}, u32[]{:S(2)}) collective-permute-start(bf16[2,2,2,2,24,384]{5,4,0,1,2,3:T(8,128)(2,1)S(1)} %bitcast.150), channel_id=1, source_target_pairs={{0,1},{1,0},{2,3},{3,2},{4,5},{5,4},{6,7},{7,6},{8,9},{9,8},{10,11... | collective-permute-start | bytes 884744 | tf_op jit(solution)/shard_map/ppermute | solution.py:511
  72.4 5.4 %collective-permute-start.7 = (bf16[200,192]{1,0:T(8,128)(2,1)S(1)}, bf16[200,192]{1,0:T(8,128)(2,1)S(1)}, u32[]{:S(2)}, u32[]{:S(2)}) collective-permute-start(bf16[200,192]{1,0:T(8,128)(2,1)S(1)} %pad_maximum_fusion.1), channel_id=1, source_target_pairs={{0,2},{1,3},{2,0},{3,1},{4,6},{5,7},{6,4},{7,5},{8,10},{9,11},{10,... | collective-permute-start | bytes 230408 | tf_op jit(solution)/shard_map/ppermute | solution.py:511
  73.4 4.6 %collective-permute-start.22 = (bf16[6,828]{1,0:T(8,128)(2,1)S(1)}, bf16[6,828]{1,0:T(8,128)(2,1)S(1)}, u32[]{:S(2)}, u32[]{:S(2)}) collective-permute-start(bf16[6,828]{1,0:T(8,128)(2,1)S(1)} %dynamic-slice_bitcast_fusion.9), channel_id=1, source_target_pairs={{0,2},{1,3},{2,0},{3,1},{4,6},{5,7},{6,4},{7,5},{8,10},{9,11},{10,... | collective-permute-start | bytes 29816 | tf_op jit(solution)/shard_map/ppermute | solution.py:511
  78.0 4.2 %collective-permute-start.8 = (bf16[104,192]{1,0:T(8,128)(2,1)S(1)}, bf16[104,192]{1,0:T(8,128)(2,1)S(1)}, u32[]{:S(2)}, u32[]{:S(2)}) collective-permute-start(bf16[104,192]{1,0:T(8,128)(2,1)S(1)} %pad_maximum_fusion.2), channel_id=1, source_target_pairs={{0,4},{1,5},{2,6},{3,7},{4,0},{5,1},{6,2},{7,3},{8,12},{9,13},{10,... | collective-permute-start | bytes 119816 | tf_op jit(solution)/shard_map/ppermute | solution.py:511
  82.3 3.9 %collective-permute-start.9 = (bf16[56,192]{1,0:T(8,128)(2,1)S(1)}, bf16[56,192]{1,0:T(8,128)(2,1)S(1)}, u32[]{:S(2)}, u32[]{:S(2)}) collective-permute-start(bf16[56,192]{1,0:T(8,128)(2,1)S(1)} %pad_maximum_fusion.3), channel_id=1, source_target_pairs={{0,8},{1,9},{2,10},{3,11},{4,12},{5,13},{6,14},{7,15},{8,0},{9,1},... | collective-permute-start | bytes 64520 | tf_op jit(solution)/shard_map/ppermute | solution.py:511
  86.3 4.7 %collective-permute-start.10 = (bf16[32,192]{1,0:T(8,128)(2,1)S(1)}, bf16[32,192]{1,0:T(8,128)(2,1)S(1)}, u32[]{:S(2)}, u32[]{:S(2)}) collective-permute-start(bf16[32,192]{1,0:T(8,128)(2,1)S(1)} %pad_maximum_fusion.4), channel_id=1, source_target_pairs={{0,16},{1,17},{2,18},{3,19},{4,20},{5,21},{6,22},{7,23},{8,24},{9,... | collective-permute-start | bytes 36872 | tf_op jit(solution)/shard_map/ppermute | solution.py:511
  86.6 5.3 %collective-permute-start.12 = (bf16[2,2,2,24,384]{4,3,0,1,2:T(8,128)(2,1)S(1)}, bf16[2,2,2,24,384]{4,3,0,1,2:T(8,128)(2,1)S(1)}, u32[]{:S(2)}, u32[]{:S(2)}) collective-permute-start(bf16[2,2,2,24,384]{4,3,0,1,2:T(8,128)(2,1)S(1)} %dynamic-slice_bitcast_fusion.1), channel_id=1, source_target_pairs={{0,2},{1,3},{2,0},{3,1},{4,6},{5,7},{6,4},{7,5},{8,10},{9,11},{10,... | collective-permute-start | bytes 442376 | tf_op jit(solution)/shard_map/ppermute | solution.py:511
  91.9 4.8 %collective-permute-start.13 = (bf16[2,2,24,384]{3,2,0,1:T(8,128)(2,1)S(1)}, bf16[2,2,24,384]{3,2,0,1:T(8,128)(2,1)S(1)}, u32[]{:S(2)}, u32[]{:S(2)}) collective-permute-start(bf16[2,2,24,384]{3,2,0,1:T(8,128)(2,1)S(1)} %dynamic-slice_bitcast_fusion.3), channel_id=1, source_target_pairs={{0,4},{1,5},{2,6},{3,7},{4,0},{5,1},{6,2},{7,3},{8,12},{9,13},{10,... | collective-permute-start | bytes 221192 | tf_op jit(solution)/shard_map/ppermute | solution.py:511
  94.5 6.3 %collective-permute-start.17 = (bf16[2,2,2,24,576]{4,3,0,1,2:T(8,128)(2,1)S(1)}, bf16[2,2,2,24,576]{4,3,0,1,2:T(8,128)(2,1)S(1)}, u32[]{:S(2)}, u32[]{:S(2)}) collective-permute-start(bf16[2,2,2,24,576]{4,3,0,1,2:T(8,128)(2,1)S(1)} %dynamic-slice_bitcast_fusion), channel_id=1, source_target_pairs={{0,2},{1,3},{2,0},{3,1},{4,6},{5,7},{6,4},{7,5},{8,10},{9,11},{10,... | collective-permute-start | bytes 663560 | tf_op jit(solution)/shard_map/ppermute | solution.py:511
  96.8 5.1 %collective-permute-start.14 = (bf16[2,24,384]{2,1,0:T(8,128)(2,1)S(1)}, bf16[2,24,384]{2,1,0:T(8,128)(2,1)S(1)}, u32[]{:S(2)}, u32[]{:S(2)}) collective-permute-start(bf16[2,24,384]{2,1,0:T(8,128)(2,1)S(1)} %dynamic-slice_bitcast_fusion.5), channel_id=1, source_target_pairs={{0,8},{1,9},{2,10},{3,11},{4,12},{5,13},{6,14},{7,15},{8,0},{9,1},... | collective-permute-start | bytes 110600 | tf_op jit(solution)/shard_map/ppermute | solution.py:511
  100.8 4.9 %collective-permute-start.18 = (bf16[2,2,24,576]{3,2,0,1:T(8,128)(2,1)S(1)}, bf16[2,2,24,576]{3,2,0,1:T(8,128)(2,1)S(1)}, u32[]{:S(2)}, u32[]{:S(2)}) collective-permute-start(bf16[2,2,24,576]{3,2,0,1:T(8,128)(2,1)S(1)} %dynamic-slice_bitcast_fusion.2), channel_id=1, source_target_pairs={{0,4},{1,5},{2,6},{3,7},{4,0},{5,1},{6,2},{7,3},{8,12},{9,13},{10,... | collective-permute-start | bytes 331784 | tf_op jit(solution)/shard_map/ppermute | solution.py:511
  105.8 4.6 %collective-permute-start.19 = (bf16[2,24,576]{2,1,0:T(8,128)(2,1)S(1)}, bf16[2,24,576]{2,1,0:T(8,128)(2,1)S(1)}, u32[]{:S(2)}, u32[]{:S(2)}) collective-permute-start(bf16[2,24,576]{2,1,0:T(8,128)(2,1)S(1)} %dynamic-slice_bitcast_fusion.4), channel_id=1, source_target_pairs={{0,8},{1,9},{2,10},{3,11},{4,12},{5,13},{6,14},{7,15},{8,0},{9,1},... | collective-permute-start | bytes 165896 | tf_op jit(solution)/shard_map/ppermute | solution.py:511
  108.2 4.7 %collective-permute-start.15 = (bf16[24,384]{1,0:T(8,128)(2,1)S(1)}, bf16[24,384]{1,0:T(8,128)(2,1)S(1)}, u32[]{:S(2)}, u32[]{:S(2)}) collective-permute-start(bf16[24,384]{1,0:T(8,128)(2,1)S(1)} %dynamic-slice_bitcast_fusion.7), channel_id=1, source_target_pairs={{0,16},{1,17},{2,18},{3,19},{4,20},{5,21},{6,22},{7,23},{8,24},{9,... | collective-permute-start | bytes 55304 | tf_op jit(solution)/shard_map/ppermute | solution.py:511
  110.4 4.9 %collective-permute-start.20 = (bf16[24,576]{1,0:T(8,128)(2,1)S(1)}, bf16[24,576]{1,0:T(8,128)(2,1)S(1)}, u32[]{:S(2)}, u32[]{:S(2)}) collective-permute-start(bf16[24,576]{1,0:T(8,128)(2,1)S(1)} %dynamic-slice_bitcast_fusion.6), channel_id=1, source_target_pairs={{0,16},{1,17},{2,18},{3,19},{4,20},{5,21},{6,22},{7,23},{8,24},{9,... | collective-permute-start | bytes 82952 | tf_op jit(solution)/shard_map/ppermute | solution.py:511
  (72 other events, 357.7 us)

commit v3 on v2

v3 whole, which is shorter than its diff:
```python
import functools

import jax
import jax.numpy as jnp
import numpy as np
from jax import lax
from jax.experimental import pallas as pl
from jax.experimental.pallas import tpu as pltpu
from jax.sharding import PartitionSpec as P

WZ = 2
WH = 6
WW = 12
ZH = WZ * WH
SPAN = 2 * WW - 1
WT = ZH * WW
EPS = 1e-05
NEG = -1e30

f32 = jnp.float32
bf16 = jnp.bfloat16


def one_hot(sources, width):
    table = np.zeros((len(sources), width), np.float32)
    for row, source in enumerate(sources):
        if source >= 0:
            table[row, source] = 1.0
    return jnp.asarray(table, bf16)


class Plan:
    def __init__(self, lon, heads, channels):
        half_h, half_w = WH // 2, WW // 2
        self.lon, self.heads, self.channels = lon, heads, channels
        self.tokens = lon * ZH
        self.windows = lon // WW
        order = [(l, z, h) for l in range(lon) for z in range(WZ) for h in range(WH)]
        self.index = {t: i for i, t in enumerate(order)}
        natural = {(l, z, h): (z * WH + h) * lon + l for l, z, h in order}
        self.to_order = one_hot([natural[t] for t in order], self.tokens)
        place = {natural[t]: i for i, t in enumerate(order)}
        self.to_natural = one_hot([place[i] for i in range(self.tokens)], self.tokens)
        lat_msg = [t for t in order if t[2] < half_h and t[0] >= half_w]
        lon_msg = [t for t in order if t[2] >= half_h and t[0] < half_w]
        cor_msg = [t for t in order if t[2] < half_h and t[0] < half_w]
        self.sizes = (len(lat_msg), len(lon_msg), len(cor_msg))
        self.send_down = [one_hot([self.index[t] for t in m], self.tokens) for m in (lat_msg, lon_msg, cor_msg)]
        picks = ([], [], [], [])
        for l, z, h in order:
            t = (l + half_w, (z + WZ // 2) % WZ, h + half_h)
            over_l, over_h = t[0] >= lon, t[2] >= WH
            t = (t[0] % lon, t[1], t[2] % WH)
            which = {(False, False): 0, (False, True): 1, (True, False): 2, (True, True): 3}[(over_l, over_h)]
            source = self.index[t] if which == 0 else (lat_msg, lon_msg, cor_msg)[which - 1].index(t)
            for i, pick in enumerate(picks):
                pick.append(source if i == which else -1)
        self.roll = [one_hot(picks[0], self.tokens)] + [one_hot(p, n) for p, n in zip(picks[1:], self.sizes)]
        back = {}
        for l, z, h in order:
            t = (l + half_w, (z + WZ // 2) % WZ, h + half_h)
            which = {(False, False): 0, (False, True): 1, (True, False): 2, (True, True): 3}[(t[0] >= lon, t[2] >= WH)]
            back[(t[0] % lon, t[1], t[2] % WH)] = (which, self.index[(l, z, h)])
        msgs = ([], [], [])
        picks = ([], [], [], [])
        for t in order:
            which, source = back[t]
            if which:
                msgs[which - 1].append(source)
            for i, pick in enumerate(picks):
                pick.append((source if which == 0 else len(msgs[which - 1]) - 1) if i == which else -1)
        self.send_up = [one_hot(m, self.tokens) for m in msgs]
        self.unroll = [one_hot(picks[0], self.tokens)] + [one_hot(p, n) for p, n in zip(picks[1:], self.sizes)]
        row = -np.ones(16 * heads, np.int64)
        for h in range(heads):
            for i in range(ZH):
                row[16 * h + i] = 8 * i + h
        self.row_pick = one_hot(row, 8 * ZH)
        lane = -np.ones(384, np.int64)
        for d in range(SPAN):
            for zk in range(WZ):
                for hk in range(WH):
                    lane[(SPAN - 1 - d) * ZH + zk * WH + hk] = zk * 256 + hk * SPAN + d
        self.lane_pick = one_hot(lane, 512).T
        level = np.array([(r % ZH) // WH for r in range(WT)])
        late = np.array([int(r % WH >= WH // 2) for r in range(WT)])
        self.level_mask = jnp.asarray(np.where(level[:, None] == level[None, :], 0.0, NEG), f32)
        self.late_mask = jnp.asarray(np.where(late[:, None] == late[None, :], 0.0, NEG), f32)


def mm(a, b):
    return lax.dot_general(a, b, (((1,), (0,)), ((), ())), preferred_element_type=f32)


def mm_nt(a, b):
    return lax.dot_general(a, b, (((1,), (1,)), ((), ())), preferred_element_type=f32)


def mm_tn(a, b):
    return lax.dot_general(a, b, (((0,), (0,)), ((), ())), preferred_element_type=f32)


def split3(v):
    hi = v.astype(bf16)
    rest = v - hi.astype(f32)
    mid = rest.astype(bf16)
    low = (rest - mid.astype(f32)).astype(bf16)
    return hi, mid, low


def norm(u, gain):
    average = jnp.mean(u, -1, keepdims=True)
    centred = u - average
    scale = lax.rsqrt(jnp.mean(centred * centred, -1, keepdims=True) + EPS)
    hat = centred * scale
    return (hat * gain).astype(bf16), hat, scale


def norm_back(grad, hat, scale, gain):
    inner = grad * gain
    gain_grad = jnp.sum(grad * hat, 0, keepdims=True)
    value = scale * (inner - jnp.mean(inner, -1, keepdims=True) - hat * jnp.mean(inner * hat, -1, keepdims=True))
    return value, gain_grad


def expand_bias(table_ref, row_pick, lane_pick, rows_ref, x_ref, bias_ref, heads, mask):
    x_ref[...] = jnp.zeros_like(x_ref)
    for h in range(heads):
        rows_ref[h : h + 1, :] = table_ref[h]
    table = rows_ref[0:heads, :]
    piece = WH * SPAN
    for i in range(ZH):
        for zk in range(WZ):
            zq, hq = i // WH, i % WH
            start = ((zq * WZ + zk) * WH + hq) * piece
            x_ref[8 * i : 8 * i + heads, 256 * zk : 256 * zk + piece] = table[:, start : start + piece]
    wide = None
    for part in split3(x_ref[...]):
        moved = mm(mm(row_pick[...], part).astype(bf16), lane_pick[...])
        wide = moved if wide is None else wide + moved
    for w in range(WW):
        start = (WW - 1 - w) * ZH
        turned = pltpu.roll(wide, (384 - start) % 384, 1) if start else wide
        for h in range(heads):
            rows = turned[16 * h : 16 * h + ZH, 0:WT]
            if mask is not None:
                rows = rows + mask[ZH * w : ZH * w + ZH, :]
            bias_ref[h, ZH * w : ZH * w + ZH, :] = rows


class Board:
    def __init__(self, lats, lons, channels, width, entries):
        self.lats, self.lons, self.channels, self.width = lats, lons, channels, width
        self.rows = channels // lats
        self.half = lons // 2
        self.chunk = entries // lons
        self.segments = -(-self.chunk // width)
        self.gain_segments = -(-channels // width)
        self.table_at = lats * self.half * self.rows
        self.gain_at = self.table_at + self.half * 8 * self.segments
        self.total = self.gain_at + 8

    def put_slices(self, ref, side, parts):
        for j in range(self.lons):
            pieces = []
            for part in parts:
                wide = part.shape[1] // self.lons
                pieces.append(part[:, j * wide : (j + 1) * wide])
            mine = jnp.concatenate(pieces, 1)
            at = side[j % 2]
            for i in range(self.lats):
                row = (i * self.half + j // 2) * self.rows
                ref[at, row : row + self.rows, :] = mine[i * self.rows : (i + 1) * self.rows]

    def put_table(self, ref, side, back, heads):
        piece = WH * SPAN
        for i in range(ZH):
            for zk in range(WZ):
                zq, hq = i // WH, i % WH
                start = ((zq * WZ + zk) * WH + hq) * piece
                at = start
                while at < start + piece:
                    j, inside = at // self.chunk, at % self.chunk
                    segment = inside // self.width
                    end = min(start + piece, (j + 1) * self.chunk, j * self.chunk + (segment + 1) * self.width)
                    lane = 256 * zk + at - start
                    row = self.table_at + ((j // 2) * self.segments + segment) * 8
                    first = inside - segment * self.width
                    value = back[8 * i : 8 * i + heads, lane : lane + end - at]
                    ref[side[j % 2], row : row + heads, first : first + end - at] = value
                    at = end

    def put_gains(self, ref, gains):
        both = []
        for part in range(2):
            for gain in gains:
                high = gain.astype(bf16).astype(f32)
                both.append(high if part == 0 else gain - high)
        for n, value in enumerate(both):
            for segment in range(self.gain_segments):
                cut = value[:, segment * self.width : min(self.channels, (segment + 1) * self.width)]
                row = self.gain_at + n * self.gain_segments + segment
                for at in range(2):
                    ref[at, row : row + 1, 0 : cut.shape[1]] = cut


def fold_bias(bias_grad_ref, row_pick, lane_pick, fold_ref, heads):
    fold_ref[...] = jnp.zeros_like(fold_ref)
    total = None
    for w in range(WW):
        for h in range(heads):
            fold_ref[16 * h : 16 * h + ZH, 0:WT] = bias_grad_ref[h, ZH * w : ZH * w + ZH, :]
        start = (WW - 1 - w) * ZH
        turned = fold_ref[...]
        if start:
            turned = pltpu.roll(turned, start, 1)
        total = turned if total is None else total + turned
    return mm_nt(mm_tn(row_pick[...], total.astype(bf16)).astype(bf16), lane_pick[...])


def head_masks(heads, channels):
    lanes = lax.broadcasted_iota(jnp.int32, (1, channels), 1)
    size = channels // heads
    return [(lanes >= size * h) & (lanes < size * (h + 1)) for h in range(heads)]


def pick(mask, value):
    return jnp.where(mask, value, jnp.zeros_like(value))


def forward(u, gains, w, bias_ref, p_ref, plan):
    channels, heads = plan.channels, plan.heads
    w_qkv, w_proj, w_fc1 = w
    n1, hat1, scale1 = norm(u, gains[0:1, :])
    qkv_w = w_qkv[...]
    q, k, v = (mm(n1, qkv_w[:, i * channels : (i + 1) * channels]).astype(bf16) for i in range(3))
    masks = head_masks(heads, channels)
    factor = (channels // heads) ** (-0.5)
    joined = []
    for n in range(plan.windows):
        rows = slice(n * WT, (n + 1) * WT)
        qw, kw, vw = q[rows], k[rows], v[rows]
        total = None
        for h in range(heads):
            s = mm_nt(pick(masks[h], qw), kw) * factor + bias_ref[h]
            e = jnp.exp(s - jnp.max(s, -1, keepdims=True))
            p = e / jnp.sum(e, -1, keepdims=True)
            p_ref[n * heads + h] = p.astype(p_ref.dtype)
            o = mm(p.astype(bf16), pick(masks[h], vw))
            total = o if total is None else total + o
        joined.append(total.astype(bf16))
    o = jnp.concatenate(joined, 0)
    middle = u + mm(o, w_proj[...])
    n2, hat2, scale2 = norm(middle, gains[1:2, :])
    wide = mm(n2, w_fc1[...])
    cdf = 0.5 * (1.0 + lax.erf(wide * (0.5**0.5)))
    g = (wide * cdf).astype(bf16)
    return (n1, hat1, scale1, q, k, v, o, middle, n2, hat2, scale2, wide, cdf, g)


def slope(wide, cdf):
    return cdf + wide * (jnp.exp(-0.5 * wide * wide) * (1.0 / np.sqrt(2.0 * np.pi)))


def mlp_back(grad, gains, w, hat2, scale2, gelu_slope):
    w_fc1, w_fc2 = w
    dz = grad.astype(bf16)
    dg = mm(dz, w_fc2[...]).astype(bf16).astype(f32)
    dh = (dg * gelu_slope).astype(bf16)
    dn2 = mm_nt(dh, w_fc1[...]).astype(bf16).astype(f32)
    dmid, gain_grad = norm_back(dn2, hat2, scale2, gains[1:2, :])
    return grad + dmid, gain_grad, dz, dh


def attention_back(dmid, gains, w, hat1, scale1, q, k, v, p_ref, bias_grad_ref, plan):
    channels, heads = plan.channels, plan.heads
    w_qkv, w_proj = w
    dp_out = dmid.astype(bf16)
    do = mm_nt(dp_out, w_proj[...]).astype(bf16)
    masks = head_masks(heads, channels)
    factor = (channels // heads) ** (-0.5)
    dqs, dks, dvs = [], [], []
    for n in range(plan.windows):
        rows = slice(n * WT, (n + 1) * WT)
        qw, kw, vw, dow = q[rows], k[rows], v[rows], do[rows]
        dq = dk = dv = None
        for h in range(heads):
            dom = pick(masks[h], dow)
            p = p_ref[n * heads + h].astype(f32)
            dp = mm_nt(dom, vw).astype(bf16).astype(f32)
            ds = p * (dp - jnp.sum(dp * p, -1, keepdims=True))
            if n == 0:
                bias_grad_ref[h] = ds
            else:
                bias_grad_ref[h] += ds
            dsb = (ds * factor).astype(bf16)
            a = mm(dsb, pick(masks[h], kw))
            b = mm_tn(dsb, pick(masks[h], qw))
            c = mm_tn(p.astype(bf16), dom)
            dq, dk, dv = (a, b, c) if dq is None else (dq + a, dk + b, dv + c)
        dqs.append(dq.astype(bf16))
        dks.append(dk.astype(bf16))
        dvs.append(dv.astype(bf16))
    dq, dk, dv = (jnp.concatenate(parts, 0) for parts in (dqs, dks, dvs))
    qkv_w = w_qkv[...]
    dn1 = None
    for i, part in enumerate((dq, dk, dv)):
        term = mm_nt(part, qkv_w[:, i * channels : (i + 1) * channels])
        dn1 = term if dn1 is None else dn1 + term
    dn1 = dn1.astype(bf16).astype(f32)
    du, gain_grad = norm_back(dn1, hat1, scale1, gains[0:1, :])
    return dmid + du, gain_grad, dq, dk, dv, dp_out


def attention_weights(n1, o, dq, dk, dv, dp_out):
    return [jnp.concatenate([mm_tn(n1, part) for part in (dq, dk, dv)], 1), mm_tn(o, dp_out)]


def mlp_weights(n2, g, dh, dz, lat):
    channels = n2.shape[1]
    groups = g.shape[1] // channels
    g_fc2 = mm_tn(g, dz).reshape(lat, groups, channels // lat, channels)
    return [mm_tn(n2, dh)] + [g_fc2[:, a].reshape(channels, channels) for a in range(groups)]


class Late:
    def __init__(self, copy, buffer):
        self.copy, self.buffer, self.here = copy, buffer, False

    def ready(self):
        if not self.here:
            self.copy.wait()
            self.here = True
        return self.buffer

    def __getitem__(self, index):
        return self.ready()[index]


class Sink:
    def __init__(self, copy, buffer):
        self.copy, self.buffer, self.sent = copy, buffer, False
        self.shape, self.dtype = buffer.shape, buffer.dtype

    def __getitem__(self, index):
        return self.buffer[index]

    def __setitem__(self, index, value):
        self.buffer[index] = value

    def send(self):
        if not self.sent:
            self.copy.start()
            self.sent = True


def call(fn, ins, outs, near, scratch, name, flops, limit, scalar=None):
    arrays = [array for array, _ in ins]
    picks = [index for _, index in ins]
    n_in, n_out, n_near = len(ins), len(outs), len(near)
    n_scalar = 0 if scalar is None else 1
    in_buffers = [pltpu.VMEM(a.shape if i is None else a.shape[1:], a.dtype) for a, i in ins]
    out_buffers = [pltpu.VMEM(o.shape, o.dtype) for o in outs]

    def kernel(*refs):
        refs = list(refs)

        def take(n):
            front = refs[:n]
            del refs[:n]
            return front

        scalars, sources, targets, nears = take(n_scalar), take(n_in), take(n_out), take(n_near)
        in_refs, out_refs, (in_sems, out_sems) = take(n_in), take(n_out), take(2)
        lates, sinks = [], []
        for i, (source, index, buffer) in enumerate(zip(sources, picks, in_refs)):
            copy = pltpu.make_async_copy(source if index is None else source.at[index], buffer, in_sems.at[i])
            copy.start()
            lates.append(Late(copy, buffer))
        for i, (target, buffer) in enumerate(zip(targets, out_refs)):
            sinks.append(Sink(pltpu.make_async_copy(buffer, target, out_sems.at[i]), buffer))
        fn(*scalars, lates, sinks, nears, refs)
        for late in lates:
            late.ready()
        for sink in sinks:
            sink.send()
        for sink in sinks:
            sink.copy.wait()

    hbm = pl.BlockSpec(memory_space=pltpu.HBM)
    vmem = pl.BlockSpec(memory_space=pltpu.VMEM)
    moved = sum(b.size * b.dtype.itemsize for b in [*arrays, *outs])
    with jax.named_scope("k_" + name):
        return pl.pallas_call(
            kernel,
            out_shape=[*outs, *near],
            in_specs=[pl.BlockSpec(memory_space=pltpu.SMEM)] * n_scalar + [hbm] * n_in,
            out_specs=[hbm] * n_out + [vmem] * n_near,
            scratch_shapes=in_buffers + out_buffers
            + [pltpu.SemaphoreType.DMA((n_in,)), pltpu.SemaphoreType.DMA((max(n_out, 1),))] + list(scratch),
            name=name,
            compiler_params=pltpu.CompilerParams(vmem_limit_bytes=limit * 1024 * 1024),
            cost_estimate=pl.CostEstimate(flops=flops, bytes_accessed=moved, transcendentals=0),
        )(*([] if scalar is None else [scalar]), *arrays)


def put_norm(ref, hat, scale):
    channels = hat.shape[1]
    ref[:, :channels] = hat
    ref[:, channels : channels + 1] = scale


def get_norm(ref, channels):
    value = ref[...]
    return value[:, :channels], value[:, channels : channels + 1]


def send_messages(value, chosen, messages):
    for message, choice in zip(messages, chosen):
        message[...] = mm(choice[...], value).astype(bf16)


def join(parts, choices):
    total = None
    for part, choice in zip(parts, choices):
        term = mm(choice[...], part[...])
        total = term if total is None else total + term
    return total


def first_kernel(plan, ins, outs, near, scratch):
    table, row_pick, lane_pick, x, to_order, w_qkv, gains, w_proj, w_fc1, w_fc2, cot, *chosen = ins
    s1, p_out, norm1, q_out, k_out, v_out, o_out, norm2, slope_out, g_out = outs
    rows_ref, x_ref, bias_ref = scratch
    expand_bias(table, row_pick, lane_pick, rows_ref, x_ref, bias_ref, plan.heads, None)
    u = mm(to_order[...], x[...])
    n1, hat1, scale1, q, k, v, o, middle, n2, hat2, scale2, wide, cdf, g = forward(
        u, gains, (w_qkv, w_proj, w_fc1), bias_ref, p_out, plan)
    put_norm(norm1, hat1, scale1)
    put_norm(norm2, hat2, scale2)
    for ref, value in ((q_out, q), (k_out, k), (v_out, v), (o_out, o), (slope_out, slope(wide, cdf).astype(bf16)), (g_out, g)):
        ref[...] = value
    for ref in outs[1:]:
        ref.send()
    out = middle + mm_nt(g, w_fc2[...])
    both = jnp.concatenate([out, mm(to_order[...], cot[...])], 1).astype(bf16)
    send_messages(both, chosen, near)
    s1[...] = both


def between_kernel(plan, last, ins, outs, near, scratch):
    table, row_pick, lane_pick, level_mask, late_mask = ins
    mask = level_mask[...] + late_mask[...] * last[0].astype(f32)
    expand_bias(table, row_pick, lane_pick, *scratch, outs[0], plan.heads, mask)


def sides(mine):
    return 1 - mine[0], mine[0]


def second_kernel(plan, board, mine, ins, outs, near, scratch):
    channels = plan.channels
    s1, roll0, r_lat, r_lon, r_cor, roll1, roll2, roll3, w_qkv, gains, bias, w_proj, w_fc1, w_fc2, *chosen = ins[:-2]
    row_pick, lane_pick = ins[-2:]
    rolled, keep, send = outs
    p_ref, bias_grad, fold_ref, grads = scratch
    grads[:, board.table_at :, :] = jnp.zeros_like(grads[:, board.table_at :, :])
    both = join((s1, r_lat, r_lon, r_cor), (roll0, roll1, roll2, roll3))
    u, cot = both[:, :channels], both[:, channels:]
    n1, hat1, scale1, q, k, v, o, middle, n2, hat2, scale2, wide, cdf, g = forward(
        u, gains, (w_qkv, w_proj, w_fc1), bias, p_ref, plan)
    dmid, gain_two, dz, dh = mlp_back(cot, gains, (w_fc1, w_fc2), hat2, scale2, slope(wide, cdf))
    du, gain_one, dq, dk, dv, dp_out = attention_back(
        dmid, gains, (w_qkv, w_proj), hat1, scale1, q, k, v, p_ref, bias_grad, plan)
    du = du.astype(bf16)
    rolled[...] = du
    rolled.send()
    send_messages(du, chosen, near)
    side = sides(mine)
    parts = attention_weights(n1, o, dq, dk, dv, dp_out) + mlp_weights(n2, g, dh, dz, board.lats)
    board.put_slices(grads, side, parts)
    board.put_gains(grads, (gain_one, gain_two))
    board.put_table(grads, side, fold_bias(bias_grad, row_pick, lane_pick, fold_ref, plan.heads), plan.heads)
    send[...] = grads[0].astype(bf16)
    send.send()
    keep[...] = grads[1].astype(bf16)


def third_kernel(plan, board, mine, ins, outs, near, scratch):
    rolled, r_lat, r_lon, r_cor, unroll0, unroll1, unroll2, unroll3, w_fc2, gelu_slope, w_fc1, norm2, gains, g = ins[:14]
    w_proj, v, p, k, q, w_qkv, norm1, o, to_natural, row_pick, lane_pick = ins[14:]
    send, keep, state_grad = outs
    bias_grad, fold_ref, grads = scratch
    grads[:, board.table_at :, :] = jnp.zeros_like(grads[:, board.table_at :, :])
    grad = join((rolled, r_lat, r_lon, r_cor), (unroll0, unroll1, unroll2, unroll3))
    hat2, scale2 = get_norm(norm2, plan.channels)
    dmid, gain_two, dz, dh = mlp_back(grad, gains, (w_fc1, w_fc2), hat2, scale2, gelu_slope[...].astype(f32))
    hat1, scale1 = get_norm(norm1, plan.channels)
    du, gain_one, dq, dk, dv, dp_out = attention_back(
        dmid, gains, (w_qkv, w_proj), hat1, scale1, q[...], k[...], v[...], p, bias_grad, plan)
    state_grad[...] = sum(mm(to_natural[...], part) for part in split3(du))
    state_grad.send()
    side = sides(mine)
    n1 = (hat1 * gains[0:1, :]).astype(bf16)
    n2 = (hat2 * gains[1:2, :]).astype(bf16)
    parts = attention_weights(n1, o[...], dq, dk, dv, dp_out) + mlp_weights(n2, g[...], dh, dz, board.lats)
    board.put_slices(grads, side, parts)
    board.put_gains(grads, (gain_one, gain_two))
    board.put_table(grads, side, fold_bias(bias_grad, row_pick, lane_pick, fold_ref, plan.heads), plan.heads)
    send[...] = grads[0].astype(bf16)
    send.send()
    keep[...] = grads[1].astype(bf16)


def last_kernel(board, widths, heads, ins, outs, near, scratch):
    w_qkv, w_proj, w_fc1, w_fc2 = widths
    own, one, two, three, table_one, table_two = ins
    qkv, proj, fc1, fc2, gain_out, table_out = near
    rows, width = board.rows, board.width
    pieces = [part[...].astype(f32) for part in (own, one, two, three)]
    whole = (pieces[0][:rows] + pieces[1][:rows]) + (pieces[2][:rows] + pieces[3][:rows])
    gains = []
    count = 2 * board.gain_segments
    for piece in pieces:
        gains.append(piece[rows : rows + count] + piece[rows + count : rows + 2 * count])
    gain = (gains[0] + gains[1]) + (gains[2] + gains[3])
    for b, table in enumerate((table_one, table_two)):
        start = b * width
        for n in range(2):
            for segment in range(board.gain_segments):
                low = segment * width
                high = min(board.channels, low + width)
                row = n * board.gain_segments + segment
                gain_out[b, n : n + 1, low:high] = gain[row : row + 1, start : start + high - low]
        qkv[b] = whole[:, start : start + w_qkv]
        start += w_qkv
        proj[b] = whole[:, start : start + w_proj]
        start += w_proj
        fc1[b] = whole[:, start : start + w_fc1]
        start += w_fc1
        groups = (width - w_qkv - w_proj - w_fc1) // w_fc2
        tall = jnp.concatenate([whole[:, start + w_fc2 * a : start + w_fc2 * (a + 1)] for a in range(groups)], 0)
        fc2[b] = tall.T
        value = table[...].astype(f32)
        for segment in range(board.segments):
            low = segment * width
            high = min(board.chunk, low + width)
            for h in range(heads):
                table_out[b, h, :, low:high] = value[8 * segment + h : 8 * segment + h + 1, : high - low]


def rounded(v):
    return lax.reduce_precision(v, 8, 7)


def body(state, out_cot, qkv_weight, proj_weight, fc1_weight, fc2_weight, norm_gain, bias_table):
    levels, rows, lon, channels = state.shape
    heads = bias_table.shape[3]
    assert levels == WZ and rows == WH and lon % WW == 0
    plan = Plan(lon, heads, channels)
    tokens, windows = plan.tokens, plan.windows
    lats, lons = lax.axis_size("lat"), lax.axis_size("lon")
    count = lats * lons
    axes = ("lat", "lon")
    lat, lon_at = lax.axis_index("lat"), lax.axis_index("lon")
    me = lat * lons + lon_at

    def shift(value, by_lat, by_lon, scope):
        pairs = []
        for a in range(lats):
            for b in range(lons):
                pairs.append((a * lons + b, ((a + by_lat) % lats) * lons + (b + by_lon) % lons))
        with jax.named_scope(scope):
            return lax.ppermute(value, axes, pairs)

    def shape(*dims, kind=bf16):
        return jax.ShapeDtypeStruct(dims, kind)

    def whole(*arrays):
        return [(array, None) for array in arrays]

    x = state.reshape(tokens, channels)
    cot = out_cot.reshape(tokens, channels)
    entries = bias_table.shape[-1]
    table = bias_table.reshape(2, heads, 1, entries)
    w_qkv, w_proj, w_fc1 = qkv_weight, proj_weight, fc1_weight
    w_fc2 = fc2_weight.transpose(0, 2, 1)
    weights = (w_qkv, w_proj, w_fc1, w_fc2)
    hidden = fc1_weight.shape[-1]
    groups = hidden // channels
    widths = tuple(w.shape[-1] // lons for w in (w_qkv, w_proj, w_fc1)) + (channels // lons,)
    part_a = widths[0] + widths[1]
    part_b = widths[2] + groups * widths[3]
    width = part_a + part_b
    board = Board(lats, lons, channels, width, entries)
    bias_shape = shape(heads, WT, WT, kind=f32)
    expand_scratch = [pltpu.VMEM((8, entries), f32), pltpu.VMEM((8 * ZH, 512), f32)]
    bias_scratch = pltpu.VMEM(bias_shape.shape, f32)
    fold_scratch = pltpu.VMEM((16 * heads, 384), f32)
    board_scratch = pltpu.VMEM((2, board.total, width), f32)
    board_shape = shape(board.total, width)
    wide_f32 = shape(tokens, channels, kind=f32)
    norm_shape = shape(tokens, 128 * (channels // 128 + 1), kind=f32)
    narrow = shape(tokens, channels)
    hidden_bf16 = shape(tokens, hidden)
    picks = whole(plan.row_pick, plan.lane_pick)
    mine = (me & 1).reshape(1)

    def messages(wide):
        return [shape(n, wide) for n in plan.sizes]

    flops = 2 * tokens * sum(w.size // 2 for w in weights)
    s1, p, norm1, q, k, v, o, norm2, gelu_slope, g, m_lat, m_lon, m_cor = call(
        functools.partial(first_kernel, plan),
        [(table, 0), *picks, *whole(x, plan.to_order), (w_qkv, 0), (norm_gain, 0), (w_proj, 0), (w_fc1, 0), (w_fc2, 0),
         *whole(cot, *plan.send_down)],
        [shape(tokens, 2 * channels), shape(windows * heads, WT, WT), norm_shape, narrow, narrow, narrow, narrow, norm_shape,
         hidden_bf16, hidden_bf16],
        messages(2 * channels),
        expand_scratch + [bias_scratch],
        "first", flops, LIMIT,
    )
    r_lat = shift(m_lat, -1, 0, "x1_lat")
    r_lon = shift(m_lon, 0, -1, "x1_lon")
    r_cor = shift(m_cor, -1, -1, "x1_cor")
    last = (lat == lats - 1).astype(jnp.int32).reshape(1)
    (bias_two,) = call(
        functools.partial(between_kernel, plan),
        [(table, 1), *picks, *whole(plan.level_mask, plan.late_mask)],
        [bias_shape], [], expand_scratch, "between", flops, LIMIT, last,
    )
    rolled, keep_two, send_two, m_lat, m_lon, m_cor = call(
        functools.partial(second_kernel, plan, board),
        [*whole(s1, plan.roll[0], r_lat, r_lon, r_cor, *plan.roll[1:]), (w_qkv, 1), (norm_gain, 1), *whole(bias_two),
         (w_proj, 1), (w_fc1, 1), (w_fc2, 1), *whole(*plan.send_up), *picks],
        [narrow, board_shape, board_shape],
        messages(channels),
        [pltpu.VMEM((windows * heads, WT, WT), f32), bias_scratch, fold_scratch, board_scratch],
        "second", 2 * flops, LIMIT, mine,
    )
    r_lat = shift(m_lat, 1, 0, "x2_lat")
    r_lon = shift(m_lon, 0, 1, "x2_lon")
    r_cor = shift(m_cor, 1, 1, "x2_cor")
    send_one, keep_one, state_grad = call(
        functools.partial(third_kernel, plan, board),
        [*whole(rolled, r_lat, r_lon, r_cor, *plan.unroll), (w_fc2, 0), *whole(gelu_slope), (w_fc1, 0), *whole(norm2),
         (norm_gain, 0), *whole(g), (w_proj, 0), *whole(v, p, k, q), (w_qkv, 0), *whole(norm1, o, plan.to_natural), *picks],
        [board_shape, board_shape, wide_f32], [],
        [bias_scratch, fold_scratch, board_scratch], "third", 2 * flops, LIMIT, mine,
    )

    bits = count.bit_length() - 1
    lon_bits = lons.bit_length() - 1
    gain_rows = 2 * board.gain_segments

    def exchange(value, mask, scope):
        with jax.named_scope(scope):
            return lax.ppermute(value, axes, [(i, i ^ mask) for i in range(count)])

    def part(held, at):
        return lax.dynamic_index_in_dim(held, at, held.ndim - 3, keepdims=False)

    def flat(value):
        return value.reshape(-1, value.shape[-1])

    def pack_gain(gain):
        high = rounded(gain)
        low = rounded(gain - high)
        both = jnp.concatenate((high, low, jnp.zeros((8 - 2 * gain_rows, gain.shape[-1]), f32)), 0)
        return high + low, both.astype(bf16)

    def unpack_gain(got):
        got = got.astype(f32)
        return got[:gain_rows] + got[gain_rows : 2 * gain_rows]

    def begin(send, keep, scope):
        got = exchange(send, 1, scope)
        table, gain = board.table_at, board.gain_at
        total = (keep[:gain].astype(f32) + got[:gain].astype(f32)).astype(bf16)
        slices = total[:table].reshape((2,) * (bits - 1) + (board.rows, width))
        tables = total[table:].reshape((2,) * (lon_bits - 1) + (8 * board.segments, width))
        return slices, tables, unpack_gain(keep[gain:]) + unpack_gain(got[gain:])

    def advance(held, bit, scope):
        slices, tables, gain = held
        at = (me >> bit) & 1
        gain, extra = pack_gain(gain)
        send = flat(part(slices, 1 - at))
        pieces = [send, extra]
        with_table = bit < lon_bits
        if with_table:
            pieces.append(flat(part(tables, 1 - at)))
        got = exchange(jnp.concatenate(pieces, 0), 1 << bit, scope)
        size = send.shape[0]
        keep = part(slices, at)
        slices = (keep.astype(f32) + got[:size].reshape(keep.shape).astype(f32)).astype(bf16)
        gain = gain + unpack_gain(got[size : size + 8])
        if with_table:
            keep = part(tables, at)
            tables = keep.astype(f32) + got[size + 8 :].reshape(keep.shape).astype(f32)
            if bit < lon_bits - 1:
                tables = tables.astype(bf16)
        return slices, tables, gain

    two = begin(send_two, keep_two, "two_0")
    one = begin(send_one, keep_one, "one_0")
    for bit in range(1, bits - 2):
        two = advance(two, bit, "two_%d" % bit)
        one = advance(one, bit, "one_%d" % bit)
    slices = jnp.concatenate((one[0], two[0]), -1).reshape(4, board.rows, 2 * width)
    _, extra = pack_gain(jnp.concatenate((one[2], two[2]), -1))
    high = me >> (bits - 2)

    def message(step):
        return jnp.concatenate((part(slices, high ^ step), extra), 0)

    got = [exchange(message(step), step << (bits - 2), "high_%d" % step) for step in (1, 2, 3)]
    qkv, proj, fc1, fc2, gain, tables = call(
        functools.partial(last_kernel, board, widths, heads),
        whole(message(0), *got, one[1], two[1]), [],
        [shape(2, board.rows, n, kind=f32) for n in widths[:3]]
        + [shape(2, widths[3], groups * board.rows, kind=f32), shape(2, 2, channels, kind=f32),
           shape(2, heads, 1, board.chunk, kind=f32)],
        [], "last", 1000, 8,
    )
    return (
        state_grad.reshape(state.shape),
        qkv,
        proj,
        fc1,
        fc2.transpose(0, 2, 1),
        gain,
        tables.reshape(2, 1, 1, heads, -1),
    )


LIMIT = 60


def solution(mesh):
    in_specs = (
        P(None, "lat", "lon", None),
        P(None, "lat", "lon", None),
        P(),
        P(),
        P(),
        P(),
        P(),
        P(None, "lat", None, None, None),
    )
    out_specs = (
        P(None, "lat", "lon", None),
        P(None, "lat", "lon"),
        P(None, "lat", "lon"),
        P(None, "lat", "lon"),
        P(None, "lat", "lon"),
        P(),
        P(None, "lat", None, None, "lon"),
    )
    return jax.shard_map(body, mesh=mesh, in_specs=in_specs, out_specs=out_specs, check_vma=False)
```

time: 118 us -> 90.7 us (0.77)
  local copies, waits for them, and re-layouts: 30 us -> 2 us
  Pallas kernels: 25.5 us -> 39 us
  starting transfers between devices: 28 us -> 18.6 us
  waiting for transfers between devices: 29.9 us -> 27.2 us
    unnamed x143 -> x16, local copies, waits for them, and re-layouts: 28.2 us -> 1.26 us
    pallas_call x7 -> x5, Pallas kernels: 25.5 us -> 39 us  [call(): pl.pallas_call(kernel, out_shape=[*outs, *near], in_specs=[pl.BlockSpec(m...]
    ppermute x19 -> x9, starting transfers between devices: 18.4 us -> 9.13 us  [exchange(): return lax.ppermute(value, axes, [(i, i ^ mask) for i in range(count)])]
    ppermute x19 -> x9, waiting for transfers between devices: 27.8 us -> 21.5 us  [exchange(): return lax.ppermute(value, axes, [(i, i ^ mask) for i in range(count)])]
    ppermute x6, waiting for transfers between devices: 2.09 us -> 5.7 us  [shift(): return lax.ppermute(value, axes, pairs)]
  transfers between devices with their start and end apart: 25 -> 15, of which waited for: 15 -> 7; matrix products, arithmetic and copies ran while one was open for 2% -> 3% of each run, Pallas kernels for 8% -> 17%
where the time goes in v3:
time: 90.7 us; the launch traced here: 90.4 us
  Pallas kernels  39 us (43%)
  waiting for transfers between devices  27.2 us (30%)
  starting transfers between devices  18.6 us (21%)
  other arithmetic  2.42 us (3%)
  local copies, waits for them, and re-layouts  2 us (2%)
  between operations  1.19 us (1%)
    pallas_call x5, Pallas kernels, call(): pl.pallas_call(kernel, out_shape=[*outs, *near], in_specs=[pl.BlockSpec(m...  39 us
    ppermute x9, waiting for transfers between devices, exchange(): return lax.ppermute(value, axes, [(i, i ^ mask) for i in range(count)])  21.5 us
    ppermute x6, starting transfers between devices, shift(): return lax.ppermute(value, axes, pairs)  9.5 us
    ppermute x9, starting transfers between devices, exchange(): return lax.ppermute(value, axes, [(i, i ^ mask) for i in range(count)])  9.13 us
    ppermute x6, waiting for transfers between devices, shift(): return lax.ppermute(value, axes, pairs)  5.7 us
  transfers between devices with their start and end apart: 15, of which 7 were waited for; matrix products, arithmetic and copies ran while one was open for 3% of the time, Pallas kernels for 17%

profile of v3, /device:TPU:0, one launch (start us, length us, event | category | flops | bytes accessed | tf_op | source)
XLA Modules:
  0.0 90.4 jit_solution(1645664529806707908)
XLA Ops:
  0.6 8.1 %first.1 = (bf16[288,384]{1,0:T(8,128)(2,1)}, bf16[12,144,144]{2,1,0:T(8,128)(2,1)}, f32[288,256]{1,0:T(8,128)}, bf16[288,192]{1,0:T(8,128)(2,1)}, bf16[288,192]...) custom-call(f32[2,6,1,3312]{3,2,1,0:T(1,128)} %bitcast.71, ...), custom_call_target="tpu_custom_call" | custom-call | flops 254803968 | bytes 5469696 | tf_op jit(solution)/shard_map/k_first/first/pallas_call | solution.py:394
  8.7 6.1 %collective-permute-start = (bf16[108,384]{1,0:T(8,128)(2,1)}, bf16[108,384]{1,0:T(8,128)(2,1)S(1)}, u32[]{:S(2)}, u32[]{:S(2)}) collective-permute-start(bf16[108,384]{1,0:T(8,128)(2,1)} %get-tuple-element.36), channel_id=1, source_target_pairs={{0,28},{1,29},{2,30},{3,31},{4,0},{5,1},{6,2},{7,3},{8,4},{9,5},{1... | collective-permute-start | bytes 248840 | tf_op jit(solution)/shard_map/x1_lat/ppermute | solution.py:574
  14.8 0.7 collective-permute-start.1
  15.5 0.9 %collective-permute-start.2 = (bf16[36,384]{1,0:T(8,128)(2,1)}, bf16[36,384]{1,0:T(8,128)(2,1)S(1)}, u32[]{:S(2)}, u32[]{:S(2)}) collective-permute-start(bf16[36,384]{1,0:T(8,128)(2,1)} %get-tuple-element.38), channel_id=1, source_target_pairs={{0,31},{1,28},{2,29},{3,30},{4,3},{5,0},{6,1},{7,2},{8,7},{9,4},{1... | collective-permute-start | bytes 82952 | tf_op jit(solution)/shard_map/x1_cor/ppermute | solution.py:574
  16.5 3.5 %between.1.refs_11_ = f32[6,144,144]{2,1,0:T(8,128)} custom-call(s32[1]{0:T(128)} %bitcast.5.refs_0_, f32[2,6,1,3312]{3,2,1,0:T(1,128)} %bitcast.72, bf16[96,96]{1,0:T(8,128)(2,1)} %constant.122.clone.refs_1_.refs_2_.refs_18_.refs_24_, bf16[512,384]{1,0:T(8,128)(2,1)} %constant.129.refs_2_.refs_3_.refs_19_.refs_25_, f32[144,144]{1,0:T(8,128)} %constant.124.clone.refs_4_, ...), custom_call_target="tpu_custom_call" | custom-call | flops 254803968 | bytes 1234176 | tf_op jit(solution)/shard_map/k_between/between/pallas_call | solution.py:394
  20.7 13.5 %second.1 = (bf16[288,192]{1,0:T(8,128)(2,1)}, bf16[424,576]{1,0:T(8,128)(2,1)}, bf16[424,576]{1,0:T(8,128)(2,1)}, bf16[108,192]{1,0:T(8,128)(2,1)}, bf16[36,192]{1,0:T(8,128)(2,1)}, /*index=5*/bf16[36,192]{1,0:T(8,128)(2,1)}) custom-call(s32[1]{0:T(128)} %bitcast.refs_0_, bf16[288,384]{1,0:T(8,128)(2,1)} %get-tuple-element.35.refs_1_, ...), custom_call_target="tpu_custom_call" | custom-call | flops 509607936 | bytes 4502016 | tf_op jit(solution)/shard_map/k_second/second/pallas_call | solution.py:394
  34.3 1.6 %collective-permute-start.3 = (bf16[108,192]{1,0:T(8,128)(2,1)}, bf16[108,192]{1,0:T(8,128)(2,1)S(1)}, u32[]{:S(2)}, u32[]{:S(2)}) collective-permute-start(bf16[108,192]{1,0:T(8,128)(2,1)} %get-tuple-element.40), channel_id=1, source_target_pairs={{0,4},{1,5},{2,6},{3,7},{4,8},{5,9},{6,10},{7,11},{8,12},{9,13},{1... | collective-permute-start | bytes 124424 | tf_op jit(solution)/shard_map/x2_lat/ppermute | solution.py:574
  36.4 0.7 slice_convert_fusion.6
  37.1 2.1 %collective-permute-done.4.refs_3_ = bf16[36,192]{1,0:T(8,128)(2,1)S(1)} collective-permute-done((bf16[36,192]{1,0:T(8,128)(2,1)}, bf16[36,192]{1,0:T(8,128)(2,1)S(1)}, u32[]{:S(2)}, u32[]{:S(2)}) %collective-permute-start.4) | collective-permute-done | bytes 13856 | tf_op jit(solution)/shard_map/x2_lon/ppermute | solution.py:574
  39.2 3.6 %collective-permute-done.5.refs_4_ = bf16[36,192]{1,0:T(8,128)(2,1)S(1)} collective-permute-done((bf16[36,192]{1,0:T(8,128)(2,1)}, bf16[36,192]{1,0:T(8,128)(2,1)S(1)}, u32[]{:S(2)}, u32[]{:S(2)}) %collective-permute-start.5) | collective-permute-done | bytes 13856 | tf_op jit(solution)/shard_map/x2_cor/ppermute | solution.py:574
  42.8 0.6 copy-done.7
  43.5 12.2 %third.1 = (bf16[424,576]{1,0:T(8,128)(2,1)}, bf16[424,576]{1,0:T(8,128)(2,1)}, f32[288,192]{1,0:T(8,128)}) custom-call(s32[1]{0:T(128)} %bitcast.refs_0_, bf16[288,192]{1,0:T(8,128)(2,1)} %get-tuple-element.39.refs_1_, bf16[108,192]{1,0:T(8,128)(2,1)} %copy-done.3, bf16[36,192]{1,0:T(8,128)(2,1)} %copy-done.6, bf16[36,192]{1,0:T(8,128)(2,1)} %copy-done.7, ...), custom_call_target="tpu_custom_call" | custom-call | flops 509607936 | bytes 6412032 | tf_op jit(solution)/shard_map/k_third/third/pallas_call | solution.py:394
  55.7 0.7 slice_convert_fusion.7
  57.0 1.3 %collective-permute-start.10 = (bf16[216,576]{1,0:T(8,128)(2,1)S(1)}, bf16[216,576]{1,0:T(8,128)(2,1)S(1)}, u32[]{:S(2)}, u32[]{:S(2)}) collective-permute-start(bf16[216,576]{1,0:T(8,128)(2,1)S(1)} %concatenate.51), channel_id=1, source_target_pairs={{0,2},{1,3},{2,0},{3,1},{4,6},{5,7},{6,4},{7,5},{8,10},{9,11},{10,... | collective-permute-start | bytes 746504 | tf_op jit(solution)/shard_map/two_1/ppermute | solution.py:658
  58.7 0.9 collective-permute-start.7
  59.6 6.9 %collective-permute-done.10 = bf16[216,576]{1,0:T(8,128)(2,1)S(1)} collective-permute-done((bf16[216,576]{1,0:T(8,128)(2,1)S(1)}, bf16[216,576]{1,0:T(8,128)(2,1)S(1)}, u32[]{:S(2)}, u32[]{:S(2)}) %collective-permute-start.10) | collective-permute-done | bytes 248864 | tf_op jit(solution)/shard_map/two_1/ppermute | solution.py:658
  66.7 5.3 %collective-permute-done.7 = bf16[216,576]{1,0:T(8,128)(2,1)S(1)} collective-permute-done((bf16[216,576]{1,0:T(8,128)(2,1)S(1)}, bf16[216,576]{1,0:T(8,128)(2,1)S(1)}, u32[]{:S(2)}, u32[]{:S(2)}) %collective-permute-start.7) | collective-permute-done | bytes 248864 | tf_op jit(solution)/shard_map/one_1/ppermute | solution.py:658
  72.3 2.1 %collective-permute-start.8 = (bf16[104,576]{1,0:T(8,128)(2,1)S(1)}, bf16[104,576]{1,0:T(8,128)(2,1)S(1)}, u32[]{:S(2)}, u32[]{:S(2)}) collective-permute-start(bf16[104,576]{1,0:T(8,128)(2,1)S(1)} %get-tuple-element.94), channel_id=1, source_target_pairs={{0,4},{1,5},{2,6},{3,7},{4,0},{5,1},{6,2},{7,3},{8,12},{9,13},{10,... | collective-permute-start | bytes 359432 | tf_op jit(solution)/shard_map/one_2/ppermute | solution.py:658
  74.4 4.3 %collective-permute-done.11 = bf16[104,576]{1,0:T(8,128)(2,1)S(1)} collective-permute-done((bf16[104,576]{1,0:T(8,128)(2,1)S(1)}, bf16[104,576]{1,0:T(8,128)(2,1)S(1)}, u32[]{:S(2)}, u32[]{:S(2)}) %collective-permute-start.11) | collective-permute-done | bytes 119840 | tf_op jit(solution)/shard_map/two_2/ppermute | solution.py:658
  78.7 1.5 %collective-permute-done.8 = bf16[104,576]{1,0:T(8,128)(2,1)S(1)} collective-permute-done((bf16[104,576]{1,0:T(8,128)(2,1)S(1)}, bf16[104,576]{1,0:T(8,128)(2,1)S(1)}, u32[]{:S(2)}, u32[]{:S(2)}) %collective-permute-start.8) | collective-permute-done | bytes 119840 | tf_op jit(solution)/shard_map/one_2/ppermute | solution.py:658
  80.7 1.1 %collective-permute-start.13 = (bf16[32,1152]{1,0:T(8,128)(2,1)S(1)}, bf16[32,1152]{1,0:T(8,128)(2,1)S(1)}, u32[]{:S(2)}, u32[]{:S(2)}) collective-permute-start(bf16[32,1152]{1,0:T(8,128)(2,1)S(1)} %get-tuple-element.92), channel_id=1, source_target_pairs={{0,16},{1,17},{2,18},{3,19},{4,20},{5,21},{6,22},{7,23},{8,24},{9,... | collective-permute-start | bytes 221192 | tf_op jit(solution)/shard_map/high_2/ppermute | solution.py:658
  81.9 3.2 %collective-permute-start.14 = (bf16[32,1152]{1,0:T(8,128)(2,1)S(1)}, bf16[32,1152]{1,0:T(8,128)(2,1)S(1)}, u32[]{:S(2)}, u32[]{:S(2)}) collective-permute-start(bf16[32,1152]{1,0:T(8,128)(2,1)S(1)} %get-tuple-element.90), channel_id=1, source_target_pairs={{0,24},{1,25},{2,26},{3,27},{4,28},{5,29},{6,30},{7,31},{8,16},{9,... | collective-permute-start | bytes 221192 | tf_op jit(solution)/shard_map/high_3/ppermute | solution.py:658
  85.1 3.5 %collective-permute-done.13.refs_2_ = bf16[32,1152]{1,0:T(8,128)(2,1)S(1)} collective-permute-done((bf16[32,1152]{1,0:T(8,128)(2,1)S(1)}, bf16[32,1152]{1,0:T(8,128)(2,1)S(1)}, u32[]{:S(2)}, u32[]{:S(2)}) %collective-permute-start.13) | collective-permute-done | bytes 73760 | tf_op jit(solution)/shard_map/high_2/ppermute | solution.py:658
  88.6 1.6 %last.1 = (f32[2,24,144]{2,1,0:T(8,128)}, f32[2,24,48]{2,1,0:T(8,128)}, f32[2,24,192]{2,1,0:T(8,128)}, f32[2,48,96]{2,1,0:T(8,128)}, f32[2,2,192]{2,1,0:T(2,128)}, /*index=5*/f32[2,6,1,828]{3,2,1,0:T(1,128)}) custom-call(bf16[32,1152]{1,0:T(8,128)(2,1)S(1)} %get-tuple-element.93.refs_0_, bf16[32,1152]{1,0:T(8,128)(2,1)S(1)} %collective-permute-done.12.refs_1_, ...), custom_call_target="tpu_custom_call" | custom-call | flops 1000 | bytes 368640 | tf_op jit(solution)/shard_map/k_last/last/pallas_call | solution.py:394
  (75 shorter events, 3.3 us)
Async XLA Ops:
  8.7 11.4 %collective-permute-start = (bf16[108,384]{1,0:T(8,128)(2,1)}, bf16[108,384]{1,0:T(8,128)(2,1)S(1)}, u32[]{:S(2)}, u32[]{:S(2)}) collective-permute-start(bf16[108,384]{1,0:T(8,128)(2,1)} %get-tuple-element.36), channel_id=1, source_target_pairs={{0,28},{1,29},{2,30},{3,31},{4,0},{5,1},{6,2},{7,3},{8,4},{9,5},{1... | collective-permute-start | bytes 248840 | tf_op jit(solution)/shard_map/x1_lat/ppermute | solution.py:574
  14.8 5.3 %collective-permute-start.1 = (bf16[36,384]{1,0:T(8,128)(2,1)}, bf16[36,384]{1,0:T(8,128)(2,1)S(1)}, u32[]{:S(2)}, u32[]{:S(2)}) collective-permute-start(bf16[36,384]{1,0:T(8,128)(2,1)} %get-tuple-element.37), channel_id=1, source_target_pairs={{0,3},{1,0},{2,1},{3,2},{4,7},{5,4},{6,5},{7,6},{8,11},{9,8},{10,9... | collective-permute-start | bytes 82952 | tf_op jit(solution)/shard_map/x1_lon/ppermute | solution.py:574
  15.5 4.6 %collective-permute-start.2 = (bf16[36,384]{1,0:T(8,128)(2,1)}, bf16[36,384]{1,0:T(8,128)(2,1)S(1)}, u32[]{:S(2)}, u32[]{:S(2)}) collective-permute-start(bf16[36,384]{1,0:T(8,128)(2,1)} %get-tuple-element.38), channel_id=1, source_target_pairs={{0,31},{1,28},{2,29},{3,30},{4,3},{5,0},{6,1},{7,2},{8,7},{9,4},{1... | collective-permute-start | bytes 82952 | tf_op jit(solution)/shard_map/x1_cor/ppermute | solution.py:574
  20.0 0.6 copy-start.4
  20.1 0.6 copy-start.5
  20.1 0.6 copy-start.2
  34.3 8.6 %collective-permute-start.3 = (bf16[108,192]{1,0:T(8,128)(2,1)}, bf16[108,192]{1,0:T(8,128)(2,1)S(1)}, u32[]{:S(2)}, u32[]{:S(2)}) collective-permute-start(bf16[108,192]{1,0:T(8,128)(2,1)} %get-tuple-element.40), channel_id=1, source_target_pairs={{0,4},{1,5},{2,6},{3,7},{4,8},{5,9},{6,10},{7,11},{8,12},{9,13},{1... | collective-permute-start | bytes 124424 | tf_op jit(solution)/shard_map/x2_lat/ppermute | solution.py:574
  35.8 3.4 %collective-permute-start.4 = (bf16[36,192]{1,0:T(8,128)(2,1)}, bf16[36,192]{1,0:T(8,128)(2,1)S(1)}, u32[]{:S(2)}, u32[]{:S(2)}) collective-permute-start(bf16[36,192]{1,0:T(8,128)(2,1)} %get-tuple-element.41), channel_id=1, source_target_pairs={{0,1},{1,2},{2,3},{3,0},{4,5},{5,6},{6,7},{7,4},{8,9},{9,10},{10,1... | collective-permute-start | bytes 41480 | tf_op jit(solution)/shard_map/x2_lon/ppermute | solution.py:574
  35.8 7.0 %collective-permute-start.5 = (bf16[36,192]{1,0:T(8,128)(2,1)}, bf16[36,192]{1,0:T(8,128)(2,1)S(1)}, u32[]{:S(2)}, u32[]{:S(2)}) collective-permute-start(bf16[36,192]{1,0:T(8,128)(2,1)} %get-tuple-element.42), channel_id=1, source_target_pairs={{0,5},{1,6},{2,7},{3,4},{4,9},{5,10},{6,11},{7,8},{8,13},{9,14},{1... | collective-permute-start | bytes 41480 | tf_op jit(solution)/shard_map/x2_cor/ppermute | solution.py:574
  36.1 20.3 %collective-permute-start.9 = (bf16[424,576]{1,0:T(8,128)(2,1)}, bf16[424,576]{1,0:T(8,128)(2,1)S(1)}, u32[]{:S(2)}, u32[]{:S(2)}) collective-permute-start(bf16[424,576]{1,0:T(8,128)(2,1)} %get-tuple-element.56), channel_id=1, source_target_pairs={{0,1},{1,0},{2,3},{3,2},{4,5},{5,4},{6,7},{7,6},{8,9},{9,8},{10,11... | collective-permute-start | bytes 1465352 | tf_op jit(solution)/shard_map/two_0/ppermute | solution.py:658
  39.2 3.6 %copy-start.6 = (bf16[36,192]{1,0:T(8,128)(2,1)}, bf16[36,192]{1,0:T(8,128)(2,1)S(1)}, u32[]{:S(2)}) copy-start(bf16[36,192]{1,0:T(8,128)(2,1)S(1)} %collective-permute-done.4.refs_3_) | copy-start | bytes 41476
  42.8 0.6 copy-start.7
  42.8 0.6 copy-start.3
  43.5 13.0 %copy-start = (bf16[424,576]{1,0:T(8,128)(2,1)S(1)}, bf16[424,576]{1,0:T(8,128)(2,1)}, u32[]{:S(2)}) copy-start(bf16[424,576]{1,0:T(8,128)(2,1)} %get-tuple-element.55) | copy-start | bytes 1465348
  55.6 2.6 %collective-permute-start.6 = (bf16[424,576]{1,0:T(8,128)(2,1)}, bf16[424,576]{1,0:T(8,128)(2,1)S(1)}, u32[]{:S(2)}, u32[]{:S(2)}) collective-permute-start(bf16[424,576]{1,0:T(8,128)(2,1)} %get-tuple-element.54), channel_id=1, source_target_pairs={{0,1},{1,0},{2,3},{3,2},{4,5},{5,4},{6,7},{7,6},{8,9},{9,8},{10,11... | collective-permute-start | bytes 1465352 | tf_op jit(solution)/shard_map/one_0/ppermute | solution.py:658
  56.6 1.6 %copy-start.1 = (bf16[424,576]{1,0:T(8,128)(2,1)S(1)}, bf16[424,576]{1,0:T(8,128)(2,1)}, u32[]{:S(2)}) copy-start(bf16[424,576]{1,0:T(8,128)(2,1)} %get-tuple-element.53) | copy-start | bytes 1465348
  57.0 9.5 %collective-permute-start.10 = (bf16[216,576]{1,0:T(8,128)(2,1)S(1)}, bf16[216,576]{1,0:T(8,128)(2,1)S(1)}, u32[]{:S(2)}, u32[]{:S(2)}) collective-permute-start(bf16[216,576]{1,0:T(8,128)(2,1)S(1)} %concatenate.51), channel_id=1, source_target_pairs={{0,2},{1,3},{2,0},{3,1},{4,6},{5,7},{6,4},{7,5},{8,10},{9,11},{10,... | collective-permute-start | bytes 746504 | tf_op jit(solution)/shard_map/two_1/ppermute | solution.py:658
  58.7 13.2 %collective-permute-start.7 = (bf16[216,576]{1,0:T(8,128)(2,1)S(1)}, bf16[216,576]{1,0:T(8,128)(2,1)S(1)}, u32[]{:S(2)}, u32[]{:S(2)}) collective-permute-start(bf16[216,576]{1,0:T(8,128)(2,1)S(1)} %concatenate.49), channel_id=1, source_target_pairs={{0,2},{1,3},{2,0},{3,1},{4,6},{5,7},{6,4},{7,5},{8,10},{9,11},{10,... | collective-permute-start | bytes 746504 | tf_op jit(solution)/shard_map/one_1/ppermute | solution.py:658
  72.2 6.5 %collective-permute-start.11 = (bf16[104,576]{1,0:T(8,128)(2,1)S(1)}, bf16[104,576]{1,0:T(8,128)(2,1)S(1)}, u32[]{:S(2)}, u32[]{:S(2)}) collective-permute-start(bf16[104,576]{1,0:T(8,128)(2,1)S(1)} %get-tuple-element.95), channel_id=1, source_target_pairs={{0,4},{1,5},{2,6},{3,7},{4,0},{5,1},{6,2},{7,3},{8,12},{9,13},{10,... | collective-permute-start | bytes 359432 | tf_op jit(solution)/shard_map/two_2/ppermute | solution.py:658
  72.3 7.9 %collective-permute-start.8 = (bf16[104,576]{1,0:T(8,128)(2,1)S(1)}, bf16[104,576]{1,0:T(8,128)(2,1)S(1)}, u32[]{:S(2)}, u32[]{:S(2)}) collective-permute-start(bf16[104,576]{1,0:T(8,128)(2,1)S(1)} %get-tuple-element.94), channel_id=1, source_target_pairs={{0,4},{1,5},{2,6},{3,7},{4,0},{5,1},{6,2},{7,3},{8,12},{9,13},{10,... | collective-permute-start | bytes 359432 | tf_op jit(solution)/shard_map/one_2/ppermute | solution.py:658
  80.7 4.5 %collective-permute-start.12 = (bf16[32,1152]{1,0:T(8,128)(2,1)S(1)}, bf16[32,1152]{1,0:T(8,128)(2,1)S(1)}, u32[]{:S(2)}, u32[]{:S(2)}) collective-permute-start(bf16[32,1152]{1,0:T(8,128)(2,1)S(1)} %get-tuple-element.91), channel_id=1, source_target_pairs={{0,8},{1,9},{2,10},{3,11},{4,12},{5,13},{6,14},{7,15},{8,0},{9,1},... | collective-permute-start | bytes 221192 | tf_op jit(solution)/shard_map/high_1/ppermute | solution.py:658
  80.7 7.9 %collective-permute-start.13 = (bf16[32,1152]{1,0:T(8,128)(2,1)S(1)}, bf16[32,1152]{1,0:T(8,128)(2,1)S(1)}, u32[]{:S(2)}, u32[]{:S(2)}) collective-permute-start(bf16[32,1152]{1,0:T(8,128)(2,1)S(1)} %get-tuple-element.92), channel_id=1, source_target_pairs={{0,16},{1,17},{2,18},{3,19},{4,20},{5,21},{6,22},{7,23},{8,24},{9,... | collective-permute-start | bytes 221192 | tf_op jit(solution)/shard_map/high_2/ppermute | solution.py:658
  81.9 6.7 %collective-permute-start.14 = (bf16[32,1152]{1,0:T(8,128)(2,1)S(1)}, bf16[32,1152]{1,0:T(8,128)(2,1)S(1)}, u32[]{:S(2)}, u32[]{:S(2)}) collective-permute-start(bf16[32,1152]{1,0:T(8,128)(2,1)S(1)} %get-tuple-element.90), channel_id=1, source_target_pairs={{0,24},{1,25},{2,26},{3,27},{4,28},{5,29},{6,30},{7,31},{8,16},{9,... | collective-permute-start | bytes 221192 | tf_op jit(solution)/shard_map/high_3/ppermute | solution.py:658
